TPU v7x, 128 devices: a whole 4x4x4 slice. The times are simulated.
128 devices in a mesh: dp: 1, ep: 128 (over z, y, x, core).
Axes of the slice: x: 4, y: 4, z: 4, core: 2. Of those that a mesh axis runs over, the one named last changes fastest.
Arguments:
- hidden: bfloat16 [32768, 2048], P(('dp', 'ep'))
- route_idx: int32 [32768, 8], P(('dp', 'ep'))
- gate_weights: float32 [32768, 8], P(('dp', 'ep'))
- w_gate: bfloat16 [128, 2048, 768], P('ep')
- w_up: bfloat16 [128, 2048, 768], P('ep')
- w_down: bfloat16 [128, 768, 2048], P('ep')
Outputs:
- output: bfloat16 [32768, 2048], P(('dp', 'ep'))
All inputs are finite; a program needn't handle non-finite values.
Results may differ from a plain program's by a relative error of at most 0.00154.
Values are sent between devices in bfloat16 or wider.
A program may use at most 1 GiB of HBM per device.

v0:
```python
import jax
import jax.numpy as jnp
from jax import lax
from jax.sharding import PartitionSpec as P, NamedSharding


def pair_plan(route_rows, num_experts, row_cap):
    tok_count, top_k = route_rows.shape
    flat_ids = route_rows.reshape(-1)
    sort_order = jnp.argsort(flat_ids, stable=True)
    counts = jnp.bincount(flat_ids, length=num_experts)
    starts = jnp.cumsum(counts) - counts
    slot_range = jnp.arange(row_cap)
    pair_pos = jnp.minimum(starts[:, None] + slot_range[None, :], tok_count * top_k - 1)
    src_rows = sort_order[pair_pos] // top_k
    pair_rank = jnp.argsort(sort_order) - starts[flat_ids]
    return src_rows, flat_ids, pair_rank


def expert_ffn(rows_in, w_gate, w_up, w_down):
    gate_proj = jnp.einsum('lscd,ldf->lscf', rows_in, w_gate, preferred_element_type=jnp.float32)
    up_proj = jnp.einsum('lscd,ldf->lscf', rows_in, w_up, preferred_element_type=jnp.float32)
    hidden_act = (jax.nn.silu(gate_proj) * up_proj).astype(jnp.bfloat16)
    return jnp.einsum('lscf,lfd->lscd', hidden_act, w_down, preferred_element_type=jnp.float32).astype(jnp.bfloat16)


def solution(mesh):
    ep_size = mesh.shape['ep']

    def device_body(hidden, route_idx, gate_weights, w_gate, w_up, w_down):
        tok_count, top_k = route_idx.shape
        d_model = hidden.shape[1]
        local_experts = w_gate.shape[0]
        num_experts = local_experts * ep_size
        row_cap = min(tok_count, 4 * top_k * tok_count // num_experts)
        src_rows, flat_ids, pair_rank = pair_plan(route_idx, num_experts, row_cap)
        send_idx = src_rows.reshape(ep_size, local_experts, row_cap).transpose(1, 0, 2)
        send_rows = hidden[send_idx]
        recv_rows = lax.all_to_all(send_rows, 'ep', 1, 1, tiled=True)
        expert_out = expert_ffn(recv_rows, w_gate, w_up, w_down)
        back_rows = lax.all_to_all(expert_out, 'ep', 1, 1, tiled=True)
        slot_pos = (flat_ids % local_experts) * (ep_size * row_cap) + (flat_ids // local_experts) * row_cap + pair_rank
        picked = back_rows.reshape(-1, d_model)[slot_pos].reshape(tok_count, top_k, d_model)
        mixed_out = jnp.sum(gate_weights[:, :, None] * picked, axis=1)
        return mixed_out.astype(jnp.bfloat16)

    row_spec = P(('dp', 'ep'), None)
    expert_spec = P('ep', None, None)
    return jax.shard_map(device_body, mesh=mesh, in_specs=(row_spec, row_spec, row_spec, expert_spec, expert_spec, expert_spec), out_specs=row_spec, check_vma=False)
```

profile of v0, /device:TPU:1, one launch (start us, length us, event | category | flops | bytes accessed | tf_op | source)
XLA Modules:
  0.0 1376.3 jit_solution(18335022039465609631)
XLA Ops:
  0.0 0.0 copy-start
  0.0 1.0 copy.16
  1.0 0.1 reshape.208
  1.1 0.1 reshape.207
  1.2 0.0 copy-start.5
  1.2 0.6 compare_select_fusion.2
  1.8 14.7 %scatter_custom_fusion = s32[128]{0:T(128)S(1)} fusion(s32[2048]{0:T(1024)S(1)} %bitcast.51, s32[2048]{0:T(1024)S(1)} %broadcast.177, s32[]{:T(128)} %constant.52.clone.1), kind=kCustom, calls=%fused_computation.35 | custom fusion | flops 2048 | bytes 516 | tf_op jit(solution)/shard_map/scatter-add | solution.py:11
  16.5 0.1 copy.18
  16.6 0.2 reduce-window.9
  16.8 0.1 reduce
  16.9 0.0 copy-start.3
  16.9 0.5 copy-done.3
  17.4 0.1 compare_select_fusion.1
  17.5 0.1 reshape.219
  17.6 5.0 sort.34
  22.6 0.0 copy-start.1
  22.6 45.5 %gather_fusion = s32[8192]{0:T(1024)S(1)} fusion(s32[2048]{0:T(1024)S(1)} %get-tuple-element.7, s32[8192]{0:T(1024)S(1)} %broadcast_clamp_fusion.1), kind=kCustom, calls=%fused_computation | custom fusion | bytes 98304 | tf_op jit(solution)/shard_map/gather | solution.py:15
  68.2 0.0 copy-done.5
  68.2 0.0 copy-done.1
  68.2 0.1 gather.15
  68.3 0.1 reshape.227
  68.4 62.7 %gather_fusion.1 = bf16[8192,2048]{1,0:T(8,128)(2,1)} fusion(bf16[256,2048]{1,0:T(8,128)(2,1)} %param.6, s32[8192]{0:T(1024)S(1)} %broadcast_clamp_fusion), kind=kCustom, calls=%fused_computation.1 | custom fusion | bytes 67141632 | tf_op jit(solution)/shard_map/gather | solution.py:38
  131.1 0.0 copy-start.9
  131.1 460.8 %all_to_all.10 = bf16[1,128,64,2048]{3,2,0,1:T(8,128)(2,1)} all-to-all(bf16[1,128,64,2048]{3,2,0,1:T(8,128)(2,1)} %bitcast.49), channel_id=1, replica_groups=mesh['dp'=1,'ep'=128] {'ep'}, dimensions={1} | all-to-all | bytes 67108864 | tf_op jit(solution)/shard_map/all_to_all | solution.py:39
  591.9 0.0 copy-done.9
  591.9 58.4 %fusion = f32[128,64,768]{2,0,1:T(8,128)} fusion(bf16[1,128,64,2048]{3,2,0,1:T(8,128)(2,1)} %all_to_all.10, bf16[1,2048,768]{2,1,0:T(8,128)(2,1)S(1)} %copy-done.9), kind=kOutput, calls=%fused_computation.5 | convolution fusion | flops 25769803776 | bytes 61865984 | tf_op jit(solution)/shard_map/lscd,ldf->lscf/dot_general | solution.py:22
  650.3 63.7 %multiply_convert_fusion.4 = bf16[128,64,768]{2,0,1:T(8,128)(2,1)} fusion(f32[128,64,768]{2,0,1:T(8,128)} %fusion, bf16[1,128,64,2048]{3,2,0,1:T(8,128)(2,1)} %all_to_all.10, bf16[1,2048,768]{2,1,0:T(8,128)(2,1)} %param.9), kind=kOutput, calls=%fused_computation.12.clone.clone.1 | convolution fusion | flops 25807552512 | bytes 74448896 | tf_op jit(solution)/shard_map/lscd,ldf->lscf/dot_general | solution.py:21
  714.0 0.0 copy-done
  714.0 34.8 %convert_bitcast_fusion = bf16[1,128,64,2048]{3,1,2,0:T(8,128)(2,1)} fusion(bf16[1,768,2048]{2,1,0:T(8,128)(2,1)S(1)} %copy-done, bf16[128,64,768]{2,0,1:T(8,128)(2,1)} %multiply_convert_fusion.4), kind=kOutput, calls=%fused_computation.9 | convolution fusion | flops 25786580992 | bytes 49283072 | tf_op jit(solution)/shard_map/lscf,lfd->lscd/dot_general | solution.py:24
  748.8 29.9 %copy.21 = bf16[1,128,64,2048]{3,2,0,1:T(8,128)(2,1)} copy(bf16[1,128,64,2048]{3,1,2,0:T(8,128)(2,1)} %convert_bitcast_fusion) | data formatting | bytes 67108864 | tf_op jit(solution)/shard_map/convert_element_type | solution.py:24
  778.8 0.0 copy-start.7
  778.8 0.0 copy-start.4
  778.8 0.0 copy-start.2
  778.8 0.0 copy-start.8
  778.8 0.0 copy-start.6
  778.8 11.8 all-to-all-start.1
  790.6 0.0 copy-done.7
  790.7 0.0 copy-done.4
  790.7 12.6 gather_fusion.2
  803.3 0.0 copy-done.2
  803.3 5.0 sort.35
  808.3 0.0 copy-done.8
  808.4 0.1 copy.15
  808.5 0.0 copy-done.6
  808.5 507.1 %all-to-all-done.1 = bf16[1,128,64,2048]{3,2,0,1:T(8,128)(2,1)} async-done(((bf16[1,128,64,2048]{3,2,0,1:T(8,128)(2,1)}), bf16[1,128,64,2048]{3,2,0,1:T(8,128)(2,1)}, u32[]{:S(2)}, u32[]{:S(2)}) %all-to-all-start.1) | async-done | bytes 33554464 | tf_op jit(solution)/shard_map/all_to_all | solution.py:41
  1315.6 48.1 %gather_fusion.3 = bf16[2048,2048]{1,0:T(8,128)(2,1)} fusion(bf16[8192,2048]{1,0:T(8,128)(2,1)} %bitcast.12, s32[2048]{0:T(1024)S(1)} %fusion.18), kind=kCustom, calls=%fused_computation.3 | custom fusion | bytes 16785408 | tf_op jit(solution)/shard_map/gather | solution.py:43
  1363.6 12.2 fusion.6
  (9 shorter events, 0.1 us)
Async XLA Ops:
  0.0 714.0 %copy-start = (bf16[1,768,2048]{2,1,0:T(8,128)(2,1)S(1)}, bf16[1,768,2048]{2,1,0:T(8,128)(2,1)}, u32[]{:S(2)}) copy-start(bf16[1,768,2048]{2,1,0:T(8,128)(2,1)} %param.11) | copy-start | bytes 9437188
  1.2 67.0 %copy-start.5 = (s32[2048]{0:T(1024)}, s32[2048]{0:T(1024)S(1)}, u32[]{:S(2)}) copy-start(s32[2048]{0:T(1024)S(1)} %reshape.207) | copy-start | bytes 24580
  16.9 0.5 copy-start.3
  22.6 45.5 %copy-start.1 = (s32[2048]{0:T(1024)}, s32[2048]{0:T(1024)S(1)}, u32[]{:S(2)}) copy-start(s32[2048]{0:T(1024)S(1)} %get-tuple-element.7) | copy-start | bytes 24580
  131.1 460.8 %copy-start.9 = (bf16[1,2048,768]{2,1,0:T(8,128)(2,1)S(1)}, bf16[1,2048,768]{2,1,0:T(8,128)(2,1)}, u32[]{:S(2)}) copy-start(bf16[1,2048,768]{2,1,0:T(8,128)(2,1)} %param.10) | copy-start | bytes 9437188
  778.8 11.8 copy-start.7
  778.8 11.9 copy-start.4
  778.8 24.5 %copy-start.2 = (s32[2048]{0:T(1024)S(1)}, s32[2048]{0:T(1024)}, u32[]{:S(2)}) copy-start(s32[2048]{0:T(1024)} %copy-done.1) | copy-start | bytes 24580
  778.8 29.5 %copy-start.8 = (f32[256,8]{0,1:T(8,128)S(1)}, f32[256,8]{0,1:T(8,128)}, u32[]{:S(2)}) copy-start(f32[256,8]{0,1:T(8,128)} %param.8) | copy-start | bytes 24580
  778.8 29.7 %copy-start.6 = (s32[2048]{0:T(1024)S(1)}, s32[2048]{0:T(1024)}, u32[]{:S(2)}) copy-start(s32[2048]{0:T(1024)} %copy-done.5) | copy-start | bytes 24580
  778.8 536.7 %all-to-all-start.1 = ((bf16[1,128,64,2048]{3,2,0,1:T(8,128)(2,1)}), bf16[1,128,64,2048]{3,2,0,1:T(8,128)(2,1)}, u32[]{:S(2)}, u32[]{:S(2)}) async-start(bf16[1,128,64,2048]{3,2,0,1:T(8,128)(2,1)} %copy.21), calls=%async_computation.1 | async-start | bytes 67108864 | tf_op jit(solution)/shard_map/all_to_all | solution.py:41
where the time goes:
time: 1390 us; the launch traced here: 1380 us
  waiting for transfers between devices  507 us (36%)
  blocking collectives  461 us (33%)
  local copies, waits for them, and re-layouts  201 us (14%)
  matrix products  157 us (11%)
  other arithmetic  38 us (3%)
    all_to_all x1, waiting for transfers between devices, device_body(): back_rows = lax.all_to_all(expert_out, 'ep', 1, 1, tiled=True)  507 us
    all_to_all x1, blocking collectives, device_body(): recv_rows = lax.all_to_all(send_rows, 'ep', 1, 1, tiled=True)  461 us
    dot_general x1, matrix products, expert_ffn(): jnp.einsum('lscd,ldf->lscf', rows_in, w_gate, preferred_element_type=jnp....  63.7 us
    gather x1, local copies, waits for them, and re-layouts, device_body(): send_rows = hidden[send_idx]  62.7 us
    dot_general x1, matrix products, expert_ffn(): jnp.einsum('lscd,ldf->lscf', rows_in, w_up, preferred_element_type=jnp.fl...  58.4 us
    gather x1, local copies, waits for them, and re-layouts, device_body(): back_rows.reshape(-1, d_model)[slot_pos].reshape(tok_count, top_k, d_model)  48.1 us
    gather x2, local copies, waits for them, and re-layouts, pair_plan(): src_rows = sort_order[pair_pos] // top_k  45.6 us
    dot_general x1, matrix products, expert_ffn(): jnp.einsum('lscf,lfd->lscd', hidden_act, w_down, preferred_element_type=j...  34.8 us
  transfers between devices with their start and end apart: 1, of which 1 were waited for; matrix products, arithmetic and copies ran while one was open for 1% of the time, Pallas kernels for 0%

commit v1 on v0

v1 whole, which is shorter than its diff:
```python
import functools

import jax
import jax.numpy as jnp
from jax import lax
from jax.experimental import pallas as pl
from jax.experimental.pallas import tpu as pltpu
from jax.sharding import Mesh, PartitionSpec as P

BF16 = jnp.bfloat16
F32 = jnp.float32
GRID = ('z', 'y', 'x', 'c')
SIZES = (4, 4, 4, 2)
PLANE = ('z', 'y')
LINE = ('x', 'c')
ROW_CAP = 64
GROUP = 4


def split3(g):
    a = lax.reduce_precision(g, 8, 7)
    b = lax.reduce_precision(g - a, 8, 7)
    return a.astype(BF16), b.astype(BF16), (g - a - b).astype(BF16)


def down_kernel(h_ref, w_ref, g_ref, out_ref, o_ref):
    experts = h_ref.shape[0]
    slots = experts * ROW_CAP

    def one_expert(e, _):
        o = jnp.dot(h_ref[e], w_ref[e], preferred_element_type=F32).astype(BF16)
        at = pl.multiple_of(e * ROW_CAP, ROW_CAP)
        for q in range(GROUP):
            o_ref[q, pl.ds(at, ROW_CAP), :] = o[q * ROW_CAP:(q + 1) * ROW_CAP]
        return _

    lax.fori_loop(0, experts, one_expert, 0)

    def one_block(q, _):
        o = o_ref[q]
        g = g_ref[q]
        acc = jnp.dot(g[:, :slots], o, preferred_element_type=F32)
        acc += jnp.dot(g[:, slots:2 * slots], o, preferred_element_type=F32)
        acc += jnp.dot(g[:, 2 * slots:], o, preferred_element_type=F32)
        out_ref[q] = acc
        return _

    lax.fori_loop(0, GROUP, one_block, 0)


def down_and_mix(h, w, g):
    experts, rows, f = h.shape
    n = w.shape[2]
    blocks, tokens, _ = g.shape
    steps = blocks // GROUP
    flops = 2 * rows * experts * f * n + 2 * blocks * tokens * g.shape[2] * n
    return pl.pallas_call(
        down_kernel,
        grid=(steps,),
        in_specs=[
            pl.BlockSpec((experts, GROUP * ROW_CAP, f), lambda i: (0, i, 0)),
            pl.BlockSpec((experts, f, n), lambda i: (0, 0, 0)),
            pl.BlockSpec((GROUP, tokens, g.shape[2]), lambda i: (i, 0, 0)),
        ],
        out_specs=pl.BlockSpec((GROUP, tokens, n), lambda i: (i, 0, 0)),
        out_shape=jax.ShapeDtypeStruct((blocks, tokens, n), F32),
        scratch_shapes=[pltpu.VMEM((GROUP, experts * ROW_CAP, n), BF16)],
        compiler_params=pltpu.CompilerParams(vmem_limit_bytes=60 * 1024 * 1024),
        cost_estimate=pl.CostEstimate(flops=flops, bytes_accessed=2 * (h.size + w.size + g.size) + 4 * blocks * tokens * n, transcendentals=0),
        name='down_and_mix',
    )(h, w, g)


def solution(mesh):
    grid = Mesh(mesh.devices.reshape((mesh.shape['dp'],) + SIZES), ('dp',) + GRID)

    def body(hidden, route_idx, gate_weights, w_gate, w_up, w_down):
        T, K = route_idx.shape
        D = hidden.shape[1]
        half = D // 2
        gather = functools.partial(lax.all_gather, tiled=False)
        tok = lax.all_gather(hidden, PLANE, axis=0)
        wg = lax.all_gather(w_gate, LINE, axis=0, tiled=True)
        wu = lax.all_gather(w_up, LINE, axis=0, tiled=True)
        wd = [lax.all_gather(w_down[:, :, s:s + half], LINE, axis=0, tiled=True) for s in (0, half)]
        ids = lax.all_gather(route_idx, PLANE, axis=0)
        gates = lax.all_gather(gate_weights, PLANE, axis=0)
        E = wg.shape[0]
        B = tok.shape[0]
        base = (lax.axis_index('z') * SIZES[1] + lax.axis_index('y')) * E
        hit = ids[:, :, :, None] == base + jnp.arange(E)
        chosen = jnp.any(hit, axis=2)
        gate = jnp.sum(jnp.where(hit, gates[..., None], 0.0), axis=2)
        rank = jnp.cumsum(chosen.astype(jnp.int32), axis=1) - 1
        slot = jnp.where(chosen, rank, -1)
        pick = slot[..., None] == jnp.arange(ROW_CAP)
        onehot = pick.astype(BF16).reshape(B, T, E * ROW_CAP)
        mix = jnp.concatenate([jnp.where(pick, s[..., None], 0).reshape(B, T, E * ROW_CAP) for s in split3(gate)], axis=2)
        rows = jnp.einsum('btm,btd->bmd', onehot, tok, preferred_element_type=F32).astype(BF16)
        rows = rows.reshape(B, E, ROW_CAP, D).transpose(1, 0, 2, 3).reshape(E, B * ROW_CAP, D)
        a = jnp.einsum('erd,edf->erf', rows, wg, preferred_element_type=F32)
        b = jnp.einsum('erd,edf->erf', rows, wu, preferred_element_type=F32)
        h = (jax.nn.silu(a) * b).astype(BF16)
        outs = []
        for w in wd:
            part = down_and_mix(h, w, mix)
            out = lax.psum_scatter(part.reshape(B * T, half), PLANE, scatter_dimension=0, tiled=True)
            outs.append(out.astype(BF16))
        return jnp.concatenate(outs, axis=1)

    r = P(('dp',) + GRID, None)
    e = P(GRID, None, None)
    return jax.shard_map(body, mesh=grid, in_specs=(r, r, r, e, e, e), out_specs=r, check_vma=False)
```

time: 1390 us -> 747 us (0.54)
  blocking collectives: 461 us -> 40.7 us
  local copies, waits for them, and re-layouts: 201 us -> 67.6 us
  waiting for transfers between devices: 507 us -> 408 us
  Pallas kernels: 0 us -> 85.5 us
  matrix products: 157 us -> 100 us
    all_to_all x1 -> x0, waiting for transfers between devices: 507 us -> none  [device_body(): back_rows = lax.all_to_all(expert_out, 'ep', 1, 1, tiled=True)]
    all_to_all x1 -> x0, blocking collectives: 461 us -> none  [device_body(): recv_rows = lax.all_to_all(send_rows, 'ep', 1, 1, tiled=True)]
    all_gather x0 -> x5, waiting for transfers between devices: none -> 223 us  [the longest x1 83.6 us: body(): wu = lax.all_gather(w_up, LINE, axis=0, tiled=True)]
    reduce_scatter x0 -> x2, waiting for transfers between devices: none -> 183 us  [body(): lax.psum_scatter(part.reshape(B * T, half), PLANE, scatter_dimension=0, t...]
    gather x5 -> x0, local copies, waits for them, and re-layouts: 169 us -> none  [the longest x1 62.7 us: device_body(): send_rows = hidden[send_idx]]
    pallas_call x0 -> x2, Pallas kernels: none -> 85.5 us  [down_and_mix(): pl.pallas_call(down_kernel, grid=(steps,), in_specs=[pl.BlockSpec((expert...]
    dot_general x3, matrix products: 157 us -> 100 us  [the longest x1 40.8 us: body(): b = jnp.einsum('erd,edf->erf', rows, wu, preferred_element_type=F32)]
    all_gather x0 -> x2, blocking collectives: none -> 40.7 us  [the longest x1 22.3 us: body(): gates = lax.all_gather(gate_weights, PLANE, axis=0)]
  transfers between devices with their start and end apart: 1 -> 7, of which waited for: 1 -> 7; matrix products, arithmetic and copies ran while one was open for 1% -> 26% of each run, Pallas kernels for 0% -> 11%
where the time goes in v1:
time: 747 us; the launch traced here: 746 us
  waiting for transfers between devices  408 us (55%)
  matrix products  100 us (13%)
  Pallas kernels  85.5 us (11%)
  local copies, waits for them, and re-layouts  67.6 us (9%)
  blocking collectives  40.7 us (5%)
  other arithmetic  29.4 us (4%)
  between operations  13.6 us (2%)
    reduce_scatter x2, waiting for transfers between devices, body(): lax.psum_scatter(part.reshape(B * T, half), PLANE, scatter_dimension=0, t...  183 us
    pallas_call x2, Pallas kernels, down_and_mix(): pl.pallas_call(down_kernel, grid=(steps,), in_specs=[pl.BlockSpec((expert...  85.5 us
    all_gather x1, waiting for transfers between devices, body(): wu = lax.all_gather(w_up, LINE, axis=0, tiled=True)  83.6 us
    all_gather x1, waiting for transfers between devices, body(): wg = lax.all_gather(w_gate, LINE, axis=0, tiled=True)  80 us
    all_gather x2, waiting for transfers between devices, body(): lax.all_gather(w_down[:, :, s:s + half], LINE, axis=0, tiled=True)  55.4 us
    dot_general x1, matrix products, body(): b = jnp.einsum('erd,edf->erf', rows, wu, preferred_element_type=F32)  40.8 us
    dot_general x1, matrix products, body(): a = jnp.einsum('erd,edf->erf', rows, wg, preferred_element_type=F32)  39.8 us
    broadcast_in_dim x6, local copies, waits for them, and re-layouts, body(): jnp.where(pick, s[..., None], 0).reshape(B, T, E * ROW_CAP)  25.8 us
  transfers between devices with their start and end apart: 7, of which 7 were waited for; matrix products, arithmetic and copies ran while one was open for 26% of the time, Pallas kernels for 11%

profile of v1, /device:TPU:1, one launch (start us, length us, event | category | flops | bytes accessed | tf_op | source)
XLA Modules:
  0.0 745.7 jit_solution(9103194943347679283)
XLA Ops:
  6.5 0.0 copy-start.2
  6.5 0.0 copy-start.3
  6.5 0.0 all-gather.17.cloned.1.call-start
  6.5 0.7 all-gather.17.cloned.1.call-update
  7.3 0.0 all-gather.9.cloned.1.call-start
  7.3 0.7 all-gather.9.cloned.1.call-update
  8.0 0.0 all-gather.11.cloned.1.call-start
  8.1 0.7 all-gather.11.cloned.1.call-update
  8.7 0.0 all-gather.15.cloned.1.call-start
  8.8 3.9 fusion.4
  12.6 0.0 all-gather.15.cloned.1.call-update
  12.7 0.0 all-gather.13.cloned.1.call-start
  12.7 0.5 all-gather.13.cloned.1.call-update
  13.3 0.0 reduce-scatter.5.cloned.1.call-start
  13.3 0.0 copy-done.2
  13.3 22.3 %all-gather.2 = f32[4096,8]{0,1:T(8,128)S(1)} all-gather(f32[256,8]{0,1:T(8,128)S(1)} %copy-done.2), channel_id=4, replica_groups=mesh['dp'=1,'z'=4,'y'=4,'x'=4,'c'=2] {'z','y'}, dimensions={0}, use_global_device_ids=true | all-gather | bytes 139264 | tf_op jit(solution)/shard_map/all_gather | solution.py:87
  35.7 0.0 copy-done.3
  35.7 18.4 %all-gather = s32[4096,8]{0,1:T(8,128)S(1)} all-gather(s32[256,8]{0,1:T(8,128)S(1)} %copy-done.3), channel_id=2, replica_groups=mesh['dp'=1,'z'=4,'y'=4,'x'=4,'c'=2] {'z','y'}, dimensions={0}, use_global_device_ids=true | all-gather | bytes 139264 | tf_op jit(solution)/shard_map/all_gather | solution.py:86
  54.1 0.2 fusion
  54.3 2.2 broadcast_in_dim.54
  56.5 6.4 copy.36
  63.0 0.2 compare_reduce_fusion
  63.2 9.0 %reduce-window.6 = s32[16,8,2,128]{3,1,2,0:T(8,128)S(1)} reduce-window(s32[16,8,2,128]{3,1,2,0:T(8,128)S(1)} %convert_bitcast_fusion, s32[]{:T(128)} %constant.26.clone.1), window={size=1x1x1x128 pad=0_0x0_0x0_0x127_0}, to_apply=%region_1.2 | reduce-window | flops 4161536 | bytes 262148 | tf_op jit(solution)/shard_map/reduce-window
  72.2 0.1 slice.16
  72.3 0.2 copy.31
  72.5 0.1 fusion.2
  72.6 0.1 copy.32
  72.7 0.1 bitcast_select_fusion
  72.8 3.9 eq.39
  76.7 9.3 %copy.33 = s32[16,256,512]{2,1,0:T(8,128)} copy(s32[16,256,512]{1,2,0:T(8,128)} %bitcast.33) | data formatting | bytes 16777216 | tf_op jit(solution)/shard_map/eq | solution.py:96
  85.9 0.1 eq.42
  86.0 2.2 broadcast_in_dim.57
  88.2 6.3 copy.37
  94.6 2.2 broadcast_in_dim.59
  96.8 6.4 copy.38
  103.2 0.0 copy-start
  103.2 0.0 copy-start.1
  103.2 5.7 broadcast_select_fusion.2
  108.9 0.1 copy-done
  109.0 1.3 copy-done.1
  110.3 1.1 broadcast_select_fusion.1
  111.4 9.3 %pad_maximum_fusion.g_ref = bf16[16,256,1536]{2,1,0:T(8,128)(2,1)} fusion(bf16[16,256,512]{2,1,0:T(8,128)(2,1)S(1)} %get-tuple-element.10, bf16[16,256,512]{2,1,0:T(8,128)(2,1)S(1)} %get-tuple-element.9, bf16[16,256,512]{2,1,0:T(8,128)(2,1)S(1)} %get-tuple-element.5), kind=kLoop, calls=%fused_computation.2 | loop fusion | flops 37748736 | bytes 25165824 | tf_op jit(solution)/shard_map/concatenate | solution.py:98
  120.7 3.7 all-gather.17.cloned.1.call-done
  124.4 19.8 %convolution_convert_fusion = bf16[16,512,2048]{2,1,0:T(8,128)(2,1)} fusion(pred[16,256,512]{2,1,0:T(32,128)(4,1)S(1)} %get-tuple-element.6, bf16[16,256,2048]{2,1,0:T(8,128)(2,1)} %bitcast.34), kind=kOutput, calls=%fused_computation.1 | convolution fusion | flops 8606711808 | bytes 52428800 | tf_op jit(solution)/shard_map/btm,btd->bmd/dot_general | solution.py:99
  144.2 22.9 %copy.35 = bf16[8,16,64,2048]{3,2,1,0:T(8,128)(2,1)} copy(bf16[8,16,64,2048]{3,2,0,1:T(8,128)(2,1)} %bitcast.30) | data formatting | bytes 67108864 | tf_op jit(solution)/shard_map/transpose | solution.py:100
  167.1 80.0 %all-gather.9.cloned.1.call-done = bf16[8,2048,768]{2,1,0:T(8,128)(2,1)} async-done(((bf16[1,2048,768]{2,1,0:T(8,128)(2,1)}), bf16[8,2048,768]{2,1,0:T(8,128)(2,1)}) %all-gather.9.cloned.1.call-update) | async-done | bytes 25165840 | tf_op jit(solution)/shard_map/all_gather | solution.py:83
  247.1 39.8 %fusion.5 = f32[8,1024,768]{2,1,0:T(8,128)} fusion(bf16[8,1024,2048]{2,1,0:T(8,128)(2,1)} %bitcast.31, bf16[8,2048,768]{2,1,0:T(8,128)(2,1)} %all-gather.9.cloned.1.call-done), kind=kOutput, calls=%fused_computation.22 | convolution fusion | flops 25769803776 | bytes 83886080 | tf_op jit(solution)/shard_map/erd,edf->erf/dot_general | solution.py:101
  286.9 83.6 %all-gather.11.cloned.1.call-done = bf16[8,2048,768]{2,1,0:T(8,128)(2,1)} async-done(((bf16[1,2048,768]{2,1,0:T(8,128)(2,1)}), bf16[8,2048,768]{2,1,0:T(8,128)(2,1)}) %all-gather.11.cloned.1.call-update) | async-done | bytes 25165840 | tf_op jit(solution)/shard_map/all_gather | solution.py:84
  370.5 40.8 %multiply_convert_fusion.h_ref = bf16[8,1024,768]{2,1,0:T(8,128)(2,1)} fusion(f32[8,1024,768]{2,1,0:T(8,128)} %fusion.5, bf16[8,1024,2048]{2,1,0:T(8,128)(2,1)} %bitcast.32, bf16[8,2048,768]{2,1,0:T(8,128)(2,1)} %all-gather.11.cloned.1.call-done), kind=kOutput, calls=%fused_computation | convolution fusion | flops 25807552512 | bytes 96468992 | tf_op jit(solution)/shard_map/erd,edf->erf/dot_general | solution.py:102
  411.4 29.0 %all-gather.15.cloned.1.call-done.w_ref = bf16[8,768,1024]{2,1,0:T(8,128)(2,1)} async-done(((bf16[1,768,1024]{2,1,0:T(8,128)(2,1)}), bf16[8,768,1024]{2,1,0:T(8,128)(2,1)}) %all-gather.15.cloned.1.call-update) | async-done | bytes 12582928 | tf_op jit(solution)/shard_map/all_gather | solution.py:85
  440.3 42.7 %down_and_mix.3 = f32[16,256,1024]{2,1,0:T(8,128)} custom-call(bf16[8,1024,768]{2,1,0:T(8,128)(2,1)} %multiply_convert_fusion.h_ref, bf16[8,768,1024]{2,1,0:T(8,128)(2,1)} %all-gather.15.cloned.1.call-done.w_ref, bf16[16,256,1536]{2,1,0:T(8,128)(2,1)} %pad_maximum_fusion.g_ref), custom_call_target="tpu_custom_call" | custom-call | flops 25769803776 | bytes 54525952 | tf_op jit(solution)/shard_map/down_and_mix/pallas_call | solution.py:57
  483.0 0.0 reduce-scatter.5.cloned.1.call-update
  483.1 0.0 reduce-scatter.3.cloned.1.call-start
  483.1 26.5 %all-gather.13.cloned.1.call-done.w_ref = bf16[8,768,1024]{2,1,0:T(8,128)(2,1)} async-done(((bf16[1,768,1024]{2,1,0:T(8,128)(2,1)}), bf16[8,768,1024]{2,1,0:T(8,128)(2,1)}) %all-gather.13.cloned.1.call-update) | async-done | bytes 12582928 | tf_op jit(solution)/shard_map/all_gather | solution.py:85
  509.6 42.7 %down_and_mix.2 = f32[16,256,1024]{2,1,0:T(8,128)} custom-call(bf16[8,1024,768]{2,1,0:T(8,128)(2,1)} %multiply_convert_fusion.h_ref, bf16[8,768,1024]{2,1,0:T(8,128)(2,1)} %all-gather.13.cloned.1.call-done.w_ref, bf16[16,256,1536]{2,1,0:T(8,128)(2,1)} %pad_maximum_fusion.g_ref), custom_call_target="tpu_custom_call" | custom-call | flops 25769803776 | bytes 54525952 | tf_op jit(solution)/shard_map/down_and_mix/pallas_call | solution.py:57
  552.4 0.0 reduce-scatter.3.cloned.1.call-update
  552.4 70.6 %reduce-scatter.5.cloned.1.call-done = f32[256,1024]{1,0:T(8,128)} async-done(((f32[4096,1024]{1,0:T(8,128)}), f32[256,1024]{1,0:T(8,128)}) %reduce-scatter.5.cloned.1.call-update) | async-done | bytes 1048592 | tf_op jit(solution)/shard_map/reduce_scatter | solution.py:107
  623.0 1.3 convert_element_type.50
  624.3 112.3 %reduce-scatter.3.cloned.1.call-done = f32[256,1024]{1,0:T(8,128)} async-done(((f32[4096,1024]{1,0:T(8,128)}), f32[256,1024]{1,0:T(8,128)}) %reduce-scatter.3.cloned.1.call-update) | async-done | bytes 1048592 | tf_op jit(solution)/shard_map/reduce_scatter | solution.py:107
  736.5 1.3 convert_element_type.49
  737.8 1.1 pad_maximum_fusion.1
  (5 shorter events, 0.1 us)
Async XLA Ops:
  6.5 6.8 copy-start.2
  6.5 29.1 %copy-start.3 = (s32[256,8]{0,1:T(8,128)S(1)}, s32[256,8]{0,1:T(8,128)}, u32[]{:S(2)}) copy-start(s32[256,8]{0,1:T(8,128)} %param.7) | copy-start | bytes 24580
  6.5 117.9 %all-gather.17.cloned.1.call-start = ((), (), s32[]{:S(2)}) async-start(), calls=%async_computation.8 | async-start | bytes 17825792 | tf_op jit(solution)/shard_map/all_gather | solution.py:82
  7.3 239.9 %all-gather.9.cloned.1.call-start = ((), (), s32[]{:S(2)}) async-start(), calls=%async_computation.2 | async-start | bytes 28311552 | tf_op jit(solution)/shard_map/all_gather | solution.py:83
  8.0 362.5 %all-gather.11.cloned.1.call-start = ((), (), s32[]{:S(2)}) async-start(), calls=%async_computation.3 | async-start | bytes 28311552 | tf_op jit(solution)/shard_map/all_gather | solution.py:84
  8.7 431.6 %all-gather.15.cloned.1.call-start = ((), (), s32[]{:S(2)}) async-start(), calls=%async_computation.6 | async-start | bytes 14155776 | tf_op jit(solution)/shard_map/all_gather | solution.py:85
  12.7 496.9 %all-gather.13.cloned.1.call-start = ((), (), s32[]{:S(2)}) async-start(), calls=%async_computation.4 | async-start | bytes 14155776 | tf_op jit(solution)/shard_map/all_gather | solution.py:85
  13.3 609.7 %reduce-scatter.5.cloned.1.call-start = ((), (), s32[]{:S(2)}) async-start(), calls=%async_computation.7 | async-start | bytes 17825792 | tf_op jit(solution)/shard_map/reduce_scatter | solution.py:107
  103.2 5.8 copy-start
  103.2 7.1 copy-start.1
  483.1 253.5 %reduce-scatter.3.cloned.1.call-start = ((), (), s32[]{:S(2)}) async-start(), calls=%async_computation.5 | async-start | bytes 17825792 | tf_op jit(solution)/shard_map/reduce_scatter | solution.py:107
Sparse Core Ops, SparseCore 0:
  9.5 114.8 all-gather.16
  126.1 120.9 all-gather.8
  248.8 121.6 all-gather.10
  372.1 68.1 all-gather.14
  441.8 67.7 all-gather.12
  512.9 110.0 reduce-scatter.4
  626.4 110.1 reduce-scatter.2

commit v2 on v0

v2 whole, which is shorter than its diff:
```python
import jax
import jax.numpy as jnp
from jax import lax
from jax.experimental import pallas as pl
from jax.experimental.pallas import tpu as pltpu
from jax.sharding import Mesh, PartitionSpec as P

BF16 = jnp.bfloat16
F32 = jnp.float32
MESH = pl.DeviceIdType.MESH
GRID = ('z', 'y', 'x', 'c')
SIZES = (4, 4, 4, 2)
ROW_CAP = 64
EXPERTS = 8
BLOCKS = 16
TILE = 8
MIB = 1024 * 1024


def expert_ids(place, x, c, line):
    dx = jnp.where((place == 2) | (place == 4), 3, 0) + jnp.where((place == 3) | (place == 5), 1, 0)
    dx += jnp.where(place >= 6, 2, 0)
    core = jnp.where(place == 0, c, 0) + jnp.where(place == 1, 1 - c, 0)
    core += jnp.where((place == 4) | (place == 5) | (place == 7), 1, 0)
    return line * EXPERTS + lax.rem(x + dx, 4) * 2 + core


def moe_kernel(hid, meta, wg, wu, wd, out, o_hbm, x_hbm, rows_in, relay, hg, hu, hd,
               tok, metas, slots, tabs, acc, rf2, rn2, stage, xt, hbuf, bg, bu, bd,
               tsend, trecv, msend, mrecv, isend, irecv, fsend, frecv, dsend, drecv, psend, precv,
               nrsend, nrrecv, frsend, frrecv, fwsend, fwrecv, f2send, f2recv, n2send, n2recv,
               lsem, ssem, wsem, xsem, csem):
    z, y, x, c = (lax.axis_index(a) for a in GRID)
    right, left = lax.rem(x + 1, 4), lax.rem(x + 3, 4)
    tokens, d = hid.shape
    half, cols = tokens // 2, d // 2
    rows = TILE * ROW_CAP
    own = (wg, wu, wd)
    held = (hg, hu, hd)
    partner = {'c': 1 - c}

    def remote(src, dst, send, recv, where):
        return pltpu.make_async_remote_copy(src_ref=src, dst_ref=dst, send_sem=send, recv_sem=recv, device_id=where, device_id_type=MESH)

    def along(dim, step):
        return {'z': lax.rem(z + (1 - dim) * step, 4), 'y': lax.rem(y + dim * step, 4)}

    def quarter(ref, m, lane, q, count=1):
        n = own[m].shape[0] // 4
        return ref.at[pl.ds(pl.multiple_of((2 * lane + q) * n, n), count * n), :]

    def line_copy(way, k, m, q, src):
        dst = held[m].at[2 + 2 * k + way]
        return remote(quarter(src, m, c, q), quarter(dst, m, c, q), isend.at[way, k, m, q], irecv.at[way, k, m, q], {'x': right if way == 0 else left})

    def far_copy(k, m, q):
        src, dst = held[m].at[2 + 2 * k + q], held[m].at[6 + k]
        return remote(quarter(src, m, c, q), quarter(dst, m, c, q), fsend.at[k, m, q], frecv.at[k, m, q], {'x': right if q == 0 else left})

    def hand_own(m, n):
        lane = 1 - c if n == 0 else c
        return remote(quarter(own[m], m, lane, 0, 2), quarter(held[m].at[c], m, lane, 0, 2), dsend.at[m, n], drecv.at[m, n], partner)

    def hand_on(slot, m):
        ref = quarter(held[m].at[slot], m, c, 0, 2)
        return remote(ref, ref, psend.at[slot - 2, m], precv.at[slot - 2, m], partner)

    def start_line(k, srcs):
        for n in (0, 1):
            for m in range(3):
                line_copy(0, k, m, n, srcs[m]).start()
                line_copy(1, k, m, 1 - n, srcs[m]).start()

    def place(k, a, b):
        return a * 4 + b if k == 0 else b * 4 + a

    def part(k, a, b, h=None):
        r = pl.ds(0, tokens) if h is None else pl.ds(h * half, half)
        return tok.at[place(k, a, b), r, pl.ds(k * cols, cols)]

    def first_copy(k, way):
        sems = tsend.at[k, 4, way], trecv.at[k, 4, way], along(k, 1 + 2 * (way % 2))
        if way < 2:
            return remote(part(k, 0, 0), part(k, 3 - 2 * way, 0), *sems)
        return remote(part(k, 7 - 2 * way, 0, way - 2), part(k, 2, 0, way - 2), *sems)

    def second_copy(k, a, way):
        sems = tsend.at[k, a, way], trecv.at[k, a, way], along(1 - k, 1 + 2 * (way % 2))
        if way < 2:
            return remote(part(k, a, 0), part(k, a, 3 - 2 * way), *sems)
        return remote(part(k, a, 7 - 2 * way, way - 2), part(k, a, 2, way - 2), *sems)

    def meta_copy(dz, dy):
        s = ((4 - dz) % 4) * 4 + (4 - dy) % 4
        return remote(metas.at[0], metas.at[s], msend.at[s], mrecv.at[s], {'z': lax.rem(z + dz, 4), 'y': lax.rem(y + dy, 4)})

    peers = [(dz, dy) for dz in range(4) for dy in range(4) if dz or dy]

    def spread(color, i, ring, m, n):
        if color == 0:
            return o_hbm.at[i, pl.ds(m, n), ring, :, pl.ds(0, cols)]
        return o_hbm.at[i, ring, pl.ds(m, n), :, pl.ds(cols, cols)]

    def near_rows(i, color, h):
        return remote(spread(color, i, 1 + 2 * h, 0, 4), rows_in.at[i, color, 2 - 2 * h], nrsend.at[i, color, h], nrrecv.at[i, color, h], along(1 - color, 1 + 2 * h))

    def far_rows(i, color, h):
        return remote(spread(color, i, 2, 2 * h, 2), relay.at[i, color, h], frsend.at[i, color, h], frrecv.at[i, color, h], along(1 - color, 1 + 2 * h))

    def pass_rows(i, color, h):
        return remote(relay.at[i, color, h], rows_in.at[i, color, 1, pl.ds(2 * h, 2)], fwsend.at[i, color, h], fwrecv.at[i, color, h], along(1 - color, 1 + 2 * h))

    def far_sum(color, h):
        return remote(acc.at[color, 2, pl.ds(h * half, half), :], rf2.at[color, h], f2send.at[color, h], f2recv.at[color, h], along(color, 1 + 2 * h))

    def near_sum(color, h):
        return remote(acc.at[color, 1 + 2 * h], rn2.at[color, h], n2send.at[color, h], n2recv.at[color, h], along(color, 1 + 2 * h))

    both = [(color, h) for color in (0, 1) for h in (0, 1)]

    own_tok = pltpu.make_async_copy(hid, tok.at[0], lsem.at[0])
    own_tok.start()
    own_meta = pltpu.make_async_copy(meta, metas.at[0], lsem.at[1])
    own_meta.start()

    barrier = pltpu.get_barrier_semaphore()
    for where in [partner, {'x': right}, {'x': left}] + [{'z': lax.rem(z + dz, 4), 'y': lax.rem(y + dy, 4)} for dz, dy in peers]:
        pl.semaphore_signal(barrier, inc=1, device_id=where, device_id_type=MESH)
    pl.semaphore_wait(barrier, 3 + len(peers))

    for n in (0, 1):
        for m in range(3):
            hand_own(m, n).start()

    @pl.when(c == 0)
    def _():
        start_line(0, own)

    own_tok.wait()
    for k in (0, 1):
        for way in (0, 1):
            first_copy(k, way).start()
            second_copy(k, 0, way).start()
    own_meta.wait()
    for dz, dy in peers:
        meta_copy(dz, dy).start()
    for m in range(3):
        hand_own(m, 0).wait_recv()

    @pl.when(c == 0)
    def _():
        start_line(1, [ref.at[1] for ref in held])

    @pl.when(c == 1)
    def _():
        start_line(0, [ref.at[0] for ref in held])
        start_line(1, own)

    for k in (0, 1):
        first_copy(k, 0).wait_recv()
        first_copy(k, 2).start()
        second_copy(k, 3, 0).start()
        second_copy(k, 3, 1).start()
        first_copy(k, 1).wait_recv()
        first_copy(k, 3).start()
        second_copy(k, 1, 0).start()
        second_copy(k, 1, 1).start()
    for k in (0, 1):
        for way in (0, 1):
            second_copy(k, 0, way).wait_recv()
            second_copy(k, 0, 2 + way).start()
    for k in (0, 1):
        first_copy(k, 2).wait_recv()
        first_copy(k, 3).wait_recv()
        second_copy(k, 2, 0).start()
        second_copy(k, 2, 1).start()

    for dz, dy in peers:
        meta_copy(dz, dy).wait_recv()
    order = lax.broadcasted_iota(jnp.int32, (EXPERTS, tokens), 0)
    earlier = lax.broadcasted_iota(jnp.int32, (tokens, tokens), 0) < lax.broadcasted_iota(jnp.int32, (tokens, tokens), 1)
    earlier = jnp.where(earlier, 1.0, 0.0).astype(BF16)

    def table(s, line, terms):
        mine = expert_ids(order, x, c, line).astype(F32)
        rec = metas[s]
        top = rec.shape[0] // 4
        sums = [jnp.zeros((EXPERTS, tokens), F32) for _ in range(1 + terms)]
        for k in range(top):
            hit = rec[k:k + 1, :] == mine
            sums[0] += jnp.where(hit, 1.0, 0.0)
            for p in range(1, 1 + terms):
                sums[p] += jnp.where(hit, rec[p * top + k:p * top + k + 1, :], 0.0)
        rank = jnp.dot(sums[0].astype(BF16), earlier, preferred_element_type=F32)
        return [jnp.where(sums[0] > 0.5, rank, -1.0)] + sums[1:]

    def own_table(s, carry):
        slots[s], = table(s, z * 4 + y, 0)
        return carry

    lax.fori_loop(0, BLOCKS, own_table, 0)

    def ring_table(n, carry):
        color, m, s = n // 16, lax.rem(n // 4, 4), lax.rem(n, 4)
        line = lax.rem(z + color * s, 4) * 4 + lax.rem(y + (1 - color) * s, 4)
        for p, t in enumerate(table((4 - 3 * color) * m, line, 3)):
            tabs[color, m, s, p] = t
        return carry

    def turn(a):
        for k in (0, 1):
            for way in (0, 1):
                second_copy(k, a, way).wait_recv()
                second_copy(k, a, 2 + way).start()

    turn(3)
    turn(1)
    turn(2)
    lax.fori_loop(0, 32, ring_table, 0)
    for a in range(4):
        for k in (0, 1):
            for way in (2, 3):
                second_copy(k, a, way).wait_recv()

    def x_store(s, b):
        return pltpu.make_async_copy(stage.at[b], x_hbm.at[:, s], ssem.at[b])

    lanes = lax.broadcasted_iota(jnp.int32, (ROW_CAP, tokens), 0).astype(F32)

    def gather(s, carry):
        b = lax.rem(s, 2)
        pick = jnp.concatenate([jnp.where(slots[s, pl.ds(e, 1), :] == lanes, 1.0, 0.0).astype(BF16) for e in range(EXPERTS)], axis=0)
        got = jnp.dot(pick, tok[s], preferred_element_type=F32).astype(BF16)

        @pl.when(s >= 2)
        def _():
            x_store(s, b).wait()

        stage[b] = got.reshape(EXPERTS, ROW_CAP, d)
        x_store(s, b).start()
        return carry

    lax.fori_loop(0, BLOCKS, gather, 0)
    acc[...] = jnp.zeros(acc.shape, F32)
    x_store(0, 0).wait()
    x_store(0, 1).wait()
    for k in (0, 1):
        for way in range(4):
            first_copy(k, way).wait_send()
            for a in range(4):
                second_copy(k, a, way).wait_send()

    def load(i, m, go):
        dst = (bg, bu, bd)[m]

        @pl.when(i == 0)
        def _():
            go(pltpu.make_async_copy(own[m], dst, wsem.at[m]))

        @pl.when(i == 1)
        def _():
            go(pltpu.make_async_copy(held[m].at[1 - c], dst, wsem.at[m]))

        @pl.when(i >= 2)
        def _():
            go(pltpu.make_async_copy(held[m].at[i], dst, wsem.at[m]))

    def arrive(i, ms):
        @pl.when(i == 1)
        def _():
            for m in ms:
                hand_own(m, 1).wait_recv()

        for k in (0, 1):
            @pl.when(i == 2 + 2 * k)
            def _():
                for m in ms:
                    for way in (0, 1):
                        for q in (way, 1 - way):
                            line_copy(way, k, m, q, held[m].at[k]).wait_recv()
                        far_copy(k, m, way).start()
                        hand_on(2 + 2 * k + way, m).start()
                for m in ms:
                    hand_on(2 + 2 * k, m).wait_recv()

            @pl.when(i == 3 + 2 * k)
            def _():
                for m in ms:
                    hand_on(3 + 2 * k, m).wait_recv()

            @pl.when(i == 6 + k)
            def _():
                for m in ms:
                    far_copy(k, m, 0).wait_recv()
                    far_copy(k, m, 1).wait_recv()
                    hand_on(6 + k, m).start()
                for m in ms:
                    hand_on(6 + k, m).wait_recv()

    def x_load(i, t):
        return pltpu.make_async_copy(x_hbm.at[i, pl.ds(t * TILE, TILE)], xt.at[t], xsem.at[t])

    def o_store(i, t):
        return pltpu.make_async_copy(stage.at[t].reshape(2, 4, ROW_CAP, d), o_hbm.at[i, pl.ds(2 * t, 2)], ssem.at[t])

    def begin(cp):
        cp.start()

    def finish(cp):
        cp.wait()

    def relay_rows(i):
        for color, h in both:
            far_rows(i, color, h).wait_recv()
            pass_rows(i, color, h).start()

    def row_loads(i, color):
        at = pl.ds(8 * lax.rem(i, 2) + 4 * color, 4)
        srcs = [spread(color, i, 0, 0, 4)] + [rows_in.at[i, color, s] for s in range(3)]
        return [pltpu.make_async_copy(src, tok.at[at, pl.ds(s * ROW_CAP, ROW_CAP), pl.ds(0, cols)], csem.at[color, s]) for s, src in enumerate(srcs)]

    def combine(i):
        for color in (0, 1):
            for h in (0, 1):
                near_rows(i, color, h).wait_recv()
                pass_rows(i, color, h).wait_recv()
            for cp in row_loads(i, color):
                cp.start()
        for color in (0, 1):
            for cp in row_loads(i, color):
                cp.wait()

        def one(n, carry):
            j, color = n // 2, lax.rem(n, 2)
            m = lax.rem(2 + 3 * j + 3 * (j * (j - 1) // 2), 4)
            got = tok[8 * lax.rem(i, 2) + 4 * color + m, :, pl.ds(0, cols)]
            total = acc[color, m]
            for p in range(1, 4):
                g = jnp.concatenate([
                    jnp.where(tabs[color, m, s, 0, pl.ds(i, 1), :] == lanes, tabs[color, m, s, p, pl.ds(i, 1), :], 0.0).astype(BF16)
                    for s in range(4)], axis=0)
                total += lax.dot_general(g, got, (((0,), (0,)), ((), ())), preferred_element_type=F32)
            acc[color, m] = total
            for k in (0, 1):
                @pl.when((i == EXPERTS - 1) & (n == k))
                def _():
                    far_sum(k, 0).start()
                    far_sum(k, 1).start()
            return carry

        lax.fori_loop(0, 8, one, 0)

    def expert(i, carry):
        @pl.when(i < EXPERTS)
        def _():
            for t in (0, 1):
                x_load(i, t).start()

        @pl.when((i >= 1) & (i <= EXPERTS))
        def _():
            relay_rows(i - 1)

        @pl.when(i < EXPERTS)
        def _():
            arrive(i, (0, 1))
            load(i, 0, begin)
            load(i, 1, begin)
            load(i, 0, finish)
            load(i, 1, finish)

            def up(t, carry):
                x_load(i, t).wait()
                xs = xt[t].reshape(rows, d)
                a = jnp.dot(xs, bg[...], preferred_element_type=F32)
                u = jnp.dot(xs, bu[...], preferred_element_type=F32)
                hbuf[t] = (jax.nn.silu(a) * u).astype(BF16)
                return carry

            lax.fori_loop(0, 2, up, 0)

        @pl.when(i >= 2)
        def _():
            combine(i - 2)

        @pl.when(i < EXPERTS)
        def _():
            arrive(i, (2,))
            load(i, 2, begin)
            load(i, 2, finish)

            def down(t, carry):
                o = jnp.dot(hbuf[t], bd[...], preferred_element_type=F32).astype(BF16)
                stage[t] = o.reshape(TILE, ROW_CAP, d)
                o_store(i, t).start()
                return carry

            lax.fori_loop(0, 2, down, 0)
            for t in (0, 1):
                o_store(i, t).wait()
            for color, h in both:
                far_rows(i, color, h).start()
            for color, h in both:
                near_rows(i, color, h).start()

        return carry

    lax.fori_loop(0, EXPERTS + 2, expert, 0)

    for color, h in both:
        far_sum(color, h).wait_recv()
        r = pl.ds(h * half, half)
        acc[color, 1 + 2 * h, r, :] = acc[color, 1 + 2 * h, r, :] + rf2[color, h]
        near_sum(color, h).start()
    for color in (0, 1):
        for h in (0, 1):
            near_sum(color, h).wait_recv()
        out[:, color * cols:(color + 1) * cols] = (acc[color, 0] + rn2[color, 0] + rn2[color, 1]).astype(out.dtype)

    for color, h in both:
        far_sum(color, h).wait_send()
        near_sum(color, h).wait_send()

    def drain(i, carry):
        for color, h in both:
            near_rows(i, color, h).wait_send()
            far_rows(i, color, h).wait_send()
            pass_rows(i, color, h).wait_send()
        return carry

    lax.fori_loop(0, EXPERTS, drain, 0)
    for dz, dy in peers:
        meta_copy(dz, dy).wait_send()
    for m in range(3):
        for n in (0, 1):
            hand_own(m, n).wait_send()
            for k in (0, 1):
                far_copy(k, m, n).wait_send()
                for way in (0, 1):
                    line_copy(way, k, m, n, held[m].at[k]).wait_send()
        for slot in range(2, 8):
            hand_on(slot, m).wait_send()


def run_moe(hidden, meta, w_gate, w_up, w_down):
    tokens, d = hidden.shape
    f = w_gate.shape[1]
    half, cols = tokens // 2, d // 2
    hbm = pl.BlockSpec(memory_space=pl.ANY)
    dma = pltpu.SemaphoreType.DMA
    flops = 2 * EXPERTS * BLOCKS * ROW_CAP * d * (3 * f + 4 * tokens)

    def both_ways(*shape):
        return [dma(shape), dma(shape)]

    return pl.pallas_call(
        moe_kernel,
        in_specs=[hbm] * 5,
        out_specs=[pl.BlockSpec(memory_space=pltpu.VMEM)] + [hbm] * 7,
        out_shape=[
            jax.ShapeDtypeStruct((tokens, d), BF16),
            jax.ShapeDtypeStruct((EXPERTS, 4, 4, ROW_CAP, d), BF16),
            jax.ShapeDtypeStruct((EXPERTS, BLOCKS, ROW_CAP, d), BF16),
            jax.ShapeDtypeStruct((EXPERTS, 2, 3, 4, ROW_CAP, cols), BF16),
            jax.ShapeDtypeStruct((EXPERTS, 2, 2, 2, ROW_CAP, cols), BF16),
            jax.ShapeDtypeStruct((8, d, f), BF16),
            jax.ShapeDtypeStruct((8, d, f), BF16),
            jax.ShapeDtypeStruct((8, f, d), BF16),
        ],
        scratch_shapes=[
            pltpu.VMEM((BLOCKS, tokens, d), BF16),
            pltpu.VMEM((BLOCKS,) + meta.shape, F32),
            pltpu.VMEM((BLOCKS, EXPERTS, tokens), F32),
            pltpu.VMEM((2, 4, 4, 4, EXPERTS, tokens), F32),
            pltpu.VMEM((2, 4, tokens, cols), F32),
            pltpu.VMEM((2, 2, half, cols), F32),
            pltpu.VMEM((2, 2, tokens, cols), F32),
            pltpu.VMEM((2, TILE, ROW_CAP, d), BF16),
            pltpu.VMEM((2, TILE, ROW_CAP, d), BF16),
            pltpu.VMEM((2, TILE * ROW_CAP, f), BF16),
            pltpu.VMEM((d, f), BF16),
            pltpu.VMEM((d, f), BF16),
            pltpu.VMEM((f, d), BF16),
            *both_ways(2, 5, 4), *both_ways(BLOCKS), *both_ways(2, 2, 3, 2), *both_ways(2, 3, 2), *both_ways(3, 2), *both_ways(6, 3),
            *both_ways(EXPERTS, 2, 2), *both_ways(EXPERTS, 2, 2), *both_ways(EXPERTS, 2, 2), *both_ways(2, 2), *both_ways(2, 2),
            dma((2,)), dma((2,)), dma((3,)), dma((2,)), dma((2, 4)),
        ],
        compiler_params=pltpu.CompilerParams(collective_id=0, has_side_effects=True, vmem_limit_bytes=63 * MIB),
        cost_estimate=pl.CostEstimate(flops=flops, bytes_accessed=400 * MIB, transcendentals=0),
        name='run_moe',
    )(hidden, meta, w_gate, w_up, w_down)[0]


def split3(g):
    a = lax.reduce_precision(g, 8, 7)
    b = lax.reduce_precision(g - a, 8, 7)
    return a, b, g - a - b


def solution(mesh):
    grid = Mesh(mesh.devices.reshape((mesh.shape['dp'],) + SIZES), ('dp',) + GRID)

    def body(hidden, route_idx, gate_weights, w_gate, w_up, w_down):
        meta = jnp.concatenate((route_idx.T.astype(F32),) + split3(gate_weights.T), axis=0)
        return run_moe(hidden, meta, w_gate[0], w_up[0], w_down[0])

    r = P(('dp',) + GRID, None)
    e = P(GRID, None, None)
    return jax.shard_map(body, mesh=grid, in_specs=(r, r, r, e, e, e), out_specs=r, check_vma=False)
```

time: 1390 us -> 459 us (0.33)
  waiting for transfers between devices: 507 us -> 0 us
  blocking collectives: 461 us -> 0 us
  Pallas kernels: 0 us -> 451 us
  local copies, waits for them, and re-layouts: 201 us -> 2.3 us
  matrix products: 157 us -> 0 us
  other arithmetic: 38 us -> 2.02 us
    all_to_all x1 -> x0, waiting for transfers between devices: 507 us -> none  [device_body(): back_rows = lax.all_to_all(expert_out, 'ep', 1, 1, tiled=True)]
    all_to_all x1 -> x0, blocking collectives: 461 us -> none  [device_body(): recv_rows = lax.all_to_all(send_rows, 'ep', 1, 1, tiled=True)]
    pallas_call x0 -> x1, Pallas kernels: none -> 451 us  [run_moe(): pl.pallas_call(moe_kernel, in_specs=[hbm] * 5, out_specs=[pl.BlockSpec(me...]
    gather x5 -> x0, local copies, waits for them, and re-layouts: 169 us -> none  [the longest x1 62.7 us: device_body(): send_rows = hidden[send_idx]]
    dot_general x3 -> x0, matrix products: 157 us -> none  [the longest x1 63.7 us: expert_ffn(): jnp.einsum('lscd,ldf->lscf', rows_in, w_gate, preferred_element_type=jnp....]
    convert_element_type x1 -> x0, local copies, waits for them, and re-layouts: 29.9 us -> none  [expert_ffn(): jnp.einsum('lscf,lfd->lscd', hidden_act, w_down, preferred_element_type=j...]
    scatter-add x1 -> x0, other arithmetic: 14.7 us -> none  [pair_plan(): counts = jnp.bincount(flat_ids, length=num_experts)]
  transfers between devices with their start and end apart: 1 -> 0, of which waited for: 1 -> 0; matrix products, arithmetic and copies ran while one was open for 1% -> 0% of each run, Pallas kernels for 0% -> 0%
where the time goes in v2:
time: 459 us; the launch traced here: 455 us
  Pallas kernels  451 us (98%)
    pallas_call x1, Pallas kernels, run_moe(): pl.pallas_call(moe_kernel, in_specs=[hbm] * 5, out_specs=[pl.BlockSpec(me...  451 us

profile of v2, /device:TPU:1, one launch (start us, length us, event | category | flops | bytes accessed | tf_op | source)
XLA Modules:
  0.0 455.4 jit_solution(3011709328144296553)
XLA Ops:
  0.0 0.7 convert_bitcast_fusion
  0.7 0.7 bitcast_reduce-precision_fusion
  1.4 0.6 pad_maximum_fusion.meta
  2.0 451.1 %run_moe.1 = (bf16[256,2048]{1,0:T(8,128)(2,1)}, bf16[8,4,4,64,2048]{4,3,2,1,0:T(8,128)(2,1)}, bf16[8,16,64,2048]{3,2,1,0:T(8,128)(2,1)}, bf16[8,2,3,4,64,1024]{...) custom-call(bf16[256,2048]{1,0:T(8,128)(2,1)} %hid.1, ...), custom_call_target="tpu_custom_call" | custom-call | flops 111669149696 | bytes 419430400 | tf_op jit(solution)/shard_map/run_moe/pallas_call | solution.py:455
  453.1 2.3 copy.8

commit v3 on v2

--- a/solution.py
+++ b/solution.py
@@ -15,6 +15,7 @@
 BLOCKS = 16
 TILE = 8
 MIB = 1024 * 1024
+scope = jax.named_scope
 
 
 def expert_ids(place, x, c, line):
@@ -265,37 +266,30 @@
         def _():
             go(pltpu.make_async_copy(held[m].at[i], dst, wsem.at[m]))
 
-    def arrive(i, ms):
+    def line_arrived(k, ms):
+        for m in ms:
+            for way in (0, 1):
+                for q in (way, 1 - way):
+                    line_copy(way, k, m, q, held[m].at[k]).wait_recv()
+                far_copy(k, m, way).start()
+                hand_on(2 + 2 * k + way, m).start()
+
+    def far_arrived(k, ms):
+        for m in ms:
+            far_copy(k, m, 0).wait_recv()
+            far_copy(k, m, 1).wait_recv()
+            hand_on(6 + k, m).start()
+
+    def handed(i, ms):
         @pl.when(i == 1)
         def _():
             for m in ms:
                 hand_own(m, 1).wait_recv()
 
-        for k in (0, 1):
-            @pl.when(i == 2 + 2 * k)
-            def _():
-                for m in ms:
-                    for way in (0, 1):
-                        for q in (way, 1 - way):
-                            line_copy(way, k, m, q, held[m].at[k]).wait_recv()
-                        far_copy(k, m, way).start()
-                        hand_on(2 + 2 * k + way, m).start()
-                for m in ms:
-                    hand_on(2 + 2 * k, m).wait_recv()
-
-            @pl.when(i == 3 + 2 * k)
-            def _():
-                for m in ms:
-                    hand_on(3 + 2 * k, m).wait_recv()
-
-            @pl.when(i == 6 + k)
-            def _():
-                for m in ms:
-                    far_copy(k, m, 0).wait_recv()
-                    far_copy(k, m, 1).wait_recv()
-                    hand_on(6 + k, m).start()
-                for m in ms:
-                    hand_on(6 + k, m).wait_recv()
+        @pl.when(i >= 2)
+        def _():
+            for m in ms:
+                hand_on(i, m).wait_recv()
 
     def x_load(i, t):
         return pltpu.make_async_copy(x_hbm.at[i, pl.ds(t * TILE, TILE)], xt.at[t], xsem.at[t])
@@ -321,14 +315,16 @@
 
     def combine(i):
         for color in (0, 1):
-            for h in (0, 1):
-                near_rows(i, color, h).wait_recv()
-                pass_rows(i, color, h).wait_recv()
+            with scope('rows_wait'):
+                for h in (0, 1):
+                    near_rows(i, color, h).wait_recv()
+                    pass_rows(i, color, h).wait_recv()
             for cp in row_loads(i, color):
                 cp.start()
-        for color in (0, 1):
-            for cp in row_loads(i, color):
-                cp.wait()
+        with scope('rowload_wait'):
+            for color in (0, 1):
+                for cp in row_loads(i, color):
+                    cp.wait()
 
         def one(n, carry):
             j, color = n // 2, lax.rem(n, 2)
@@ -350,23 +346,40 @@
 
         lax.fori_loop(0, 8, one, 0)
 
+    def load_up(i):
+        handed(i, (0, 1))
+        load(i, 0, begin)
+        load(i, 1, begin)
+
+    def load_down(i):
+        handed(i, (2,))
+        load(i, 2, begin)
+
     def expert(i, carry):
+        late = (i == 4) | (i == 6) | (i == 7)
+
         @pl.when(i < EXPERTS)
         def _():
             for t in (0, 1):
                 x_load(i, t).start()
 
-        @pl.when((i >= 1) & (i <= EXPERTS))
-        def _():
-            relay_rows(i - 1)
-
-        @pl.when(i < EXPERTS)
-        def _():
-            arrive(i, (0, 1))
-            load(i, 0, begin)
-            load(i, 1, begin)
-            load(i, 0, finish)
-            load(i, 1, finish)
+            @pl.when(jnp.logical_not(late))
+            def _():
+                load_down(i)
+
+            @pl.when(i == 7)
+            def _():
+                with scope('far1_gu'):
+                    far_arrived(1, (0, 1))
+
+            @pl.when(late)
+            def _():
+                with scope('late_gu'):
+                    load_up(i)
+
+            with scope('load_gu'):
+                load(i, 0, finish)
+                load(i, 1, finish)
 
             def up(t, carry):
                 x_load(i, t).wait()
@@ -376,17 +389,59 @@
                 hbuf[t] = (jax.nn.silu(a) * u).astype(BF16)
                 return carry
 
-            lax.fori_loop(0, 2, up, 0)
+            with scope('up'):
+                lax.fori_loop(0, 2, up, 0)
+
+            @pl.when((i < 3) | (i == 4))
+            def _():
+                with scope('next_gu'):
+                    load_up(i + 1)
+
+        @pl.when(i == 4)
+        def _():
+            with scope('line1_d'):
+                line_arrived(1, (2,))
+
+        for k in (0, 1):
+            @pl.when(i == 6 + k)
+            def _():
+                with scope('far_d'):
+                    far_arrived(k, (2,))
+
+        @pl.when((i >= 1) & (i < EXPERTS))
+        def _():
+            with scope('relay'):
+                relay_rows(i - 1)
 
         @pl.when(i >= 2)
         def _():
-            combine(i - 2)
+            with scope('combine'):
+                combine(i - 2)
+
+        @pl.when(i == EXPERTS)
+        def _():
+            with scope('relay'):
+                relay_rows(i - 1)
+
+        @pl.when(i == 3)
+        def _():
+            with scope('line1_gu'):
+                line_arrived(1, (0, 1))
+
+        @pl.when(i == 5)
+        def _():
+            with scope('far0_gu'):
+                far_arrived(0, (0, 1))
 
         @pl.when(i < EXPERTS)
         def _():
-            arrive(i, (2,))
-            load(i, 2, begin)
-            load(i, 2, finish)
+            @pl.when(late)
+            def _():
+                with scope('late_d'):
+                    load_down(i)
+
+            with scope('load_d'):
+                load(i, 2, finish)
 
             def down(t, carry):
                 o = jnp.dot(hbuf[t], bd[...], preferred_element_type=F32).astype(BF16)
@@ -394,9 +449,10 @@
                 o_store(i, t).start()
                 return carry
 
-            lax.fori_loop(0, 2, down, 0)
-            for t in (0, 1):
-                o_store(i, t).wait()
+            with scope('down'):
+                lax.fori_loop(0, 2, down, 0)
+                for t in (0, 1):
+                    o_store(i, t).wait()
             for color, h in both:
                 far_rows(i, color, h).start()
             for color, h in both:
@@ -404,16 +460,21 @@
 
         return carry
 
+    with scope('line0'):
+        line_arrived(0, (0, 1, 2))
+    load_up(0)
     lax.fori_loop(0, EXPERTS + 2, expert, 0)
 
     for color, h in both:
-        far_sum(color, h).wait_recv()
+        with scope('farsum_wait'):
+            far_sum(color, h).wait_recv()
         r = pl.ds(h * half, half)
         acc[color, 1 + 2 * h, r, :] = acc[color, 1 + 2 * h, r, :] + rf2[color, h]
         near_sum(color, h).start()
     for color in (0, 1):
         for h in (0, 1):
-            near_sum(color, h).wait_recv()
+            with scope('nearsum_wait'):
+                near_sum(color, h).wait_recv()
         out[:, color * cols:(color + 1) * cols] = (acc[color, 0] + rn2[color, 0] + rn2[color, 1]).astype(out.dtype)
 
     for color, h in both:

time: 459 us -> 400 us (0.87)
  Pallas kernels: 451 us -> 393 us
    pallas_call x1, Pallas kernels: 451 us -> 393 us  [run_moe(): pl.pallas_call(moe_kernel, in_specs=[hbm] * 5, out_specs=[pl.BlockSpec(me...]
where the time goes in v3:
time: 400 us; the launch traced here: 397 us
  Pallas kernels  393 us (98%)
    pallas_call x1, Pallas kernels, run_moe(): pl.pallas_call(moe_kernel, in_specs=[hbm] * 5, out_specs=[pl.BlockSpec(me...  393 us

profile of v3, /device:TPU:1, one launch (start us, length us, event | category | flops | bytes accessed | tf_op | source)
XLA Modules:
  0.0 397.0 jit_solution(1759718745699541432)
XLA Ops:
  0.0 0.7 convert_bitcast_fusion
  0.7 0.7 bitcast_reduce-precision_fusion
  1.4 0.6 pad_maximum_fusion.meta
  2.0 392.7 %run_moe.1 = (bf16[256,2048]{1,0:T(8,128)(2,1)}, bf16[8,4,4,64,2048]{4,3,2,1,0:T(8,128)(2,1)}, bf16[8,16,64,2048]{3,2,1,0:T(8,128)(2,1)}, bf16[8,2,3,4,64,1024]{...) custom-call(bf16[256,2048]{1,0:T(8,128)(2,1)} %hid.1, ...), custom_call_target="tpu_custom_call" | custom-call | flops 111669149696 | bytes 419430400 | tf_op jit(solution)/shard_map/run_moe/pallas_call | solution.py:516
  394.7 2.3 copy.8

commit v4 on v3

v4 whole, which is shorter than its diff:
```python
import jax
import jax.numpy as jnp
from jax import lax
from jax.experimental import pallas as pl
from jax.experimental.pallas import tpu as pltpu
from jax.sharding import Mesh, PartitionSpec as P

BF16 = jnp.bfloat16
F32 = jnp.float32
MESH = pl.DeviceIdType.MESH
GRID = ('z', 'y', 'x', 'c')
SIZES = (4, 4, 4, 2)
ROW_CAP = 64
EXPERTS = 8
BLOCKS = 16
TILE = 8
MIB = 1024 * 1024
scope = jax.named_scope


def expert_ids(place, x, c, line):
    dx = jnp.where((place == 2) | (place == 4), 3, 0) + jnp.where((place == 3) | (place == 5), 1, 0)
    dx += jnp.where(place >= 6, 2, 0)
    core = jnp.where(place == 0, c, 0) + jnp.where(place == 1, 1 - c, 0)
    core += jnp.where((place == 4) | (place == 5) | (place == 7), 1, 0)
    return line * EXPERTS + lax.rem(x + dx, 4) * 2 + core


def moe_kernel(hid, ids, gates, wg, wu, wd, out, o_hbm, x_hbm, rows_in, relay, hg, hu, hd,
               tok, all_ids, all_gates, slots, tabs, acc, rf2, rn2, stage, xt, abuf, hbuf, bg, bu, bd,
               tsend, trecv, msend, mrecv, isend, irecv, fsend, frecv, dsend, drecv, psend, precv,
               nrsend, nrrecv, frsend, frrecv, fwsend, fwrecv, f2send, f2recv, n2send, n2recv,
               gsend, grecv, qsend, qrecv, lsem, ssem, osem, wsem, xsem, csem):
    z, y, x, c = (lax.axis_index(a) for a in GRID)
    right, left = lax.rem(x + 1, 4), lax.rem(x + 3, 4)
    tokens, d = hid.shape
    half, cols = tokens // 2, d // 2
    rows = TILE * ROW_CAP
    own = (wg, wu, wd)
    held = (hg, hu, hd)
    partner = {'c': 1 - c}

    def remote(src, dst, send, recv, where):
        return pltpu.make_async_remote_copy(src_ref=src, dst_ref=dst, send_sem=send, recv_sem=recv, device_id=where, device_id_type=MESH)

    def along(dim, step):
        return {'z': lax.rem(z + (1 - dim) * step, 4), 'y': lax.rem(y + dim * step, 4)}

    def quarter(ref, m, lane, q, count=1):
        n = own[m].shape[0] // 4
        return ref.at[pl.ds(pl.multiple_of((2 * lane + q) * n, n), count * n), :]

    def line_copy(way, k, m, q, src):
        dst = held[m].at[2 + 2 * k + way]
        return remote(quarter(src, m, c, q), quarter(dst, m, c, q), isend.at[way, k, m, q], irecv.at[way, k, m, q], {'x': right if way == 0 else left})

    def far_copy(k, m, q):
        src, dst = held[m].at[2 + 2 * k + q], held[m].at[6 + k]
        return remote(quarter(src, m, c, q), quarter(dst, m, c, q), fsend.at[k, m, q], frecv.at[k, m, q], {'x': right if q == 0 else left})

    def hand_own(m, n):
        lane = 1 - c if n == 0 else c
        return remote(quarter(own[m], m, lane, 0, 2), quarter(held[m].at[c], m, lane, 0, 2), dsend.at[m, n], drecv.at[m, n], partner)

    def hand_on(slot, m):
        ref = quarter(held[m].at[slot], m, c, 0, 2)
        return remote(ref, ref, psend.at[slot - 2, m], precv.at[slot - 2, m], partner)

    def start_line(k, srcs, skip=0):
        for n, m in [(n, m) for n in (0, 1) for m in range(3)][skip:]:
            line_copy(0, k, m, n, srcs[m]).start()
            line_copy(1, k, m, 1 - n, srcs[m]).start()

    def piece(color, part):
        return pl.ds(color * cols + part * (cols // 2), cols // 2)

    def piece_of(ref, lane, q, count, color, part):
        n = ref.shape[0] // 4
        return ref.at[pl.ds(pl.multiple_of((2 * lane + q) * n, n), count * n), piece(color, part)]

    def far_piece(q, part, color):
        src, dst = hd.at[4 + q], hd.at[7]
        return remote(piece_of(src, c, q, 1, color, part), piece_of(dst, c, q, 1, color, part), gsend.at[q, part, color], grecv.at[q, part, color], {'x': right if q == 0 else left})

    def hand_piece(part, color):
        ref = piece_of(hd.at[7], c, 0, 2, color, part)
        return remote(ref, ref, qsend.at[part, color], qrecv.at[part, color], partner)

    def place(k, a, b):
        return a * 4 + b if k == 0 else b * 4 + a

    def part(k, a, b, h=None):
        r = pl.ds(0, tokens) if h is None else pl.ds(h * half, half)
        return tok.at[place(k, a, b), r, pl.ds(k * cols, cols)]

    def first_copy(k, way):
        sems = tsend.at[k, 4, way], trecv.at[k, 4, way], along(k, 1 + 2 * (way % 2))
        if way < 2:
            return remote(part(k, 0, 0), part(k, 3 - 2 * way, 0), *sems)
        return remote(part(k, 7 - 2 * way, 0, way - 2), part(k, 2, 0, way - 2), *sems)

    def second_copy(k, a, way):
        sems = tsend.at[k, a, way], trecv.at[k, a, way], along(1 - k, 1 + 2 * (way % 2))
        if way < 2:
            return remote(part(k, a, 0), part(k, a, 3 - 2 * way), *sems)
        return remote(part(k, a, 7 - 2 * way, way - 2), part(k, a, 2, way - 2), *sems)

    def route_copies(dz, dy):
        s = ((4 - dz) % 4) * 4 + (4 - dy) % 4
        where = {'z': lax.rem(z + dz, 4), 'y': lax.rem(y + dy, 4)}
        return [remote(ref.at[0], ref.at[s], msend.at[n, s], mrecv.at[n, s], where) for n, ref in enumerate((all_ids, all_gates))]

    peers = [(dz, dy) for dz in range(4) for dy in range(4) if dz or dy]

    def spread(color, i, ring, m, n, part=None):
        w = pl.ds(color * cols, cols) if part is None else piece(color, part)
        if color == 0:
            return o_hbm.at[i, pl.ds(m, n), ring, :, w]
        return o_hbm.at[i, ring, pl.ds(m, n), :, w]

    def within(part):
        return pl.ds(0, cols) if part is None else pl.ds(part * (cols // 2), cols // 2)

    def row_sems(send, recv, i, part, color, h):
        n = i if part is None else i + part
        return send.at[n, color, h], recv.at[n, color, h], along(1 - color, 1 + 2 * h)

    def near_rows(i, color, h, part=None):
        return remote(spread(color, i, 1 + 2 * h, 0, 4, part), rows_in.at[i, color, 2 - 2 * h, :, :, within(part)], *row_sems(nrsend, nrrecv, i, part, color, h))

    def far_rows(i, color, h, part=None):
        return remote(spread(color, i, 2, 2 * h, 2, part), relay.at[i, color, h, :, :, within(part)], *row_sems(frsend, frrecv, i, part, color, h))

    def pass_rows(i, color, h, part=None):
        return remote(relay.at[i, color, h, :, :, within(part)], rows_in.at[i, color, 1, pl.ds(2 * h, 2), :, within(part)], *row_sems(fwsend, fwrecv, i, part, color, h))

    def far_sum(color, h, part):
        r, w = pl.ds(h * half, half), within(part)
        return remote(acc.at[color, 2, r, w], rf2.at[color, h, :, w], f2send.at[color, h, part], f2recv.at[color, h, part], along(color, 1 + 2 * h))

    def near_sum(color, h, waits, part):
        r, w = pl.ds((h if waits else 1 - h) * half, half), within(part)
        return remote(acc.at[color, 1 + 2 * h, r, w], rn2.at[color, h, r, w], n2send.at[color, h, waits, part], n2recv.at[color, h, waits, part], along(color, 1 + 2 * h))

    both = [(color, h) for color in (0, 1) for h in (0, 1)]

    own_tok = pltpu.make_async_copy(hid, tok.at[0], lsem.at[0])
    own_tok.start()
    own_routes = [pltpu.make_async_copy(ids, all_ids.at[0], lsem.at[1]), pltpu.make_async_copy(gates, all_gates.at[0], lsem.at[2])]
    for cp in own_routes:
        cp.start()

    barrier = pltpu.get_barrier_semaphore()
    for where in [partner, {'x': right}, {'x': left}] + [{'z': lax.rem(z + dz, 4), 'y': lax.rem(y + dy, 4)} for dz, dy in peers]:
        pl.semaphore_signal(barrier, inc=1, device_id=where, device_id_type=MESH)
    pl.semaphore_wait(barrier, 3 + len(peers))

    for n in (0, 1):
        for m in range(3):
            hand_own(m, n).start()

    @pl.when(c == 0)
    def _():
        start_line(0, own)

    @pl.when(c == 1)
    def _():
        line_copy(0, 1, 0, 0, own[0]).start()
        line_copy(1, 1, 0, 1, own[0]).start()

    own_tok.wait()
    for k in (0, 1):
        for way in (0, 1):
            first_copy(k, way).start()
            second_copy(k, 0, way).start()
    for cp in own_routes:
        cp.wait()
    for dz, dy in peers:
        for cp in route_copies(dz, dy):
            cp.start()
    for m in range(3):
        hand_own(m, 0).wait_recv()

    @pl.when(c == 0)
    def _():
        start_line(1, [ref.at[1] for ref in held])

    @pl.when(c == 1)
    def _():
        start_line(0, [ref.at[0] for ref in held])
        start_line(1, own, 1)

    for k in (0, 1):
        first_copy(k, 0).wait_recv()
        first_copy(k, 2).start()
        second_copy(k, 3, 0).start()
        second_copy(k, 3, 1).start()
        first_copy(k, 1).wait_recv()
        first_copy(k, 3).start()
        second_copy(k, 1, 0).start()
        second_copy(k, 1, 1).start()
    for k in (0, 1):
        for way in (0, 1):
            second_copy(k, 0, way).wait_recv()
            second_copy(k, 0, 2 + way).start()
    for k in (0, 1):
        first_copy(k, 2).wait_recv()
        first_copy(k, 3).wait_recv()
        second_copy(k, 2, 0).start()
        second_copy(k, 2, 1).start()

    for dz, dy in peers:
        for cp in route_copies(dz, dy):
            cp.wait_recv()
    order = lax.broadcasted_iota(jnp.int32, (EXPERTS, tokens), 0)
    earlier = lax.broadcasted_iota(jnp.int32, (tokens, tokens), 0) < lax.broadcasted_iota(jnp.int32, (tokens, tokens), 1)
    earlier = jnp.where(earlier, 1.0, 0.0).astype(BF16)

    def table(s, line):
        mine = expert_ids(order, x, c, line)
        rec, weight = all_ids[s], all_gates[s]
        chosen = jnp.zeros((EXPERTS, tokens), F32)
        gate = jnp.zeros((EXPERTS, tokens), F32)
        for k in range(rec.shape[0]):
            hit = rec[k:k + 1, :] == mine
            chosen += jnp.where(hit, 1.0, 0.0)
            gate += jnp.where(hit, weight[k:k + 1, :], 0.0)
        rank = jnp.dot(chosen.astype(BF16), earlier, preferred_element_type=F32)
        return jnp.where(chosen > 0.5, rank, -1.0), gate

    def own_table(s, carry):
        slots[s] = table(s, z * 4 + y)[0]
        return carry

    lax.fori_loop(0, BLOCKS, own_table, 0)

    def ring_table(n, carry):
        color, m, s = n // 16, lax.rem(n // 4, 4), lax.rem(n, 4)
        line = lax.rem(z + color * s, 4) * 4 + lax.rem(y + (1 - color) * s, 4)
        slot, gate = table((4 - 3 * color) * m, line)
        tabs[color, m, s, 0] = slot
        for p in range(1, 4):
            term = gate.astype(BF16).astype(F32)
            tabs[color, m, s, p] = term
            gate = gate - term
        return carry

    def turn(a):
        for k in (0, 1):
            for way in (0, 1):
                second_copy(k, a, way).wait_recv()
                second_copy(k, a, 2 + way).start()

    turn(3)
    turn(1)
    turn(2)
    lax.fori_loop(0, 32, ring_table, 0)
    for a in range(4):
        for k in (0, 1):
            for way in (2, 3):
                second_copy(k, a, way).wait_recv()

    def x_store(s, b):
        return pltpu.make_async_copy(stage.at[b].reshape(EXPERTS, ROW_CAP, d), x_hbm.at[:, s], ssem.at[b])

    lanes = lax.broadcasted_iota(jnp.int32, (ROW_CAP, tokens), 0).astype(F32)

    def gather(s, carry):
        b = lax.rem(s, 2)
        pick = jnp.concatenate([jnp.where(slots[s, pl.ds(e, 1), :] == lanes, 1.0, 0.0).astype(BF16) for e in range(EXPERTS)], axis=0)
        got = jnp.dot(pick, tok[s], preferred_element_type=F32).astype(BF16)

        @pl.when(s >= 2)
        def _():
            x_store(s, b).wait()

        stage[b] = got.reshape(2, 4, ROW_CAP, d)
        x_store(s, b).start()
        return carry

    lax.fori_loop(0, BLOCKS, gather, 0)
    acc[...] = jnp.zeros(acc.shape, F32)
    x_store(0, 0).wait()
    x_store(0, 1).wait()
    for k in (0, 1):
        for way in range(4):
            first_copy(k, way).wait_send()
            for a in range(4):
                second_copy(k, a, way).wait_send()

    def load(i, m, go):
        dst = (bg, bu, bd)[m]

        @pl.when(i == 0)
        def _():
            go(pltpu.make_async_copy(own[m], dst, wsem.at[m]))

        @pl.when(i == 1)
        def _():
            go(pltpu.make_async_copy(held[m].at[1 - c], dst, wsem.at[m]))

        @pl.when(i >= 2)
        def _():
            go(pltpu.make_async_copy(held[m].at[i], dst, wsem.at[m]))

    def line_arrived(k, ms):
        for m in ms:
            for way in (0, 1):
                for q in (way, 1 - way):
                    line_copy(way, k, m, q, held[m].at[k]).wait_recv()
                if (k, m) == (1, 2):
                    for part in (0, 1):
                        for color in (0, 1):
                            far_piece(way, part, color).start()
                else:
                    far_copy(k, m, way).start()
                hand_on(2 + 2 * k + way, m).start()

    def far_arrived(k, ms):
        for m in ms:
            far_copy(k, m, 0).wait_recv()
            far_copy(k, m, 1).wait_recv()
            hand_on(6 + k, m).start()

    def handed(i, ms):
        @pl.when(i == 1)
        def _():
            for m in ms:
                hand_own(m, 1).wait_recv()

        @pl.when(i >= 2)
        def _():
            for m in ms:
                hand_on(i, m).wait_recv()

    def x_load(i, t):
        return pltpu.make_async_copy(x_hbm.at[i, pl.ds(t * TILE, TILE)], xt.at[t], xsem.at[t])

    def o_store(i, t, w):
        n = 0 if w.size == d else w.start // cols
        return pltpu.make_async_copy(stage.at[t, :, :, :, w], o_hbm.at[i, pl.ds(2 * t, 2), :, :, w], osem.at[t, n])

    def begin(cp):
        cp.start()

    def finish(cp):
        cp.wait()

    def relay_rows(i, part=None):
        for color, h in both:
            far_rows(i, color, h, part).wait_recv()
            pass_rows(i, color, h, part).start()

    def row_loads(i, color, part):
        at = pl.ds(8 * lax.rem(i, 2) + 4 * color, 4)
        srcs = [spread(color, i, 0, 0, 4, part)] + [rows_in.at[i, color, s, :, :, within(part)] for s in range(3)]
        return [pltpu.make_async_copy(src, tok.at[at, pl.ds(s * ROW_CAP, ROW_CAP), within(part)], csem.at[color, s]) for s, src in enumerate(srcs)]

    def combine(i, part=None, then=None):
        for color in (0, 1):
            with scope('rows_wait'):
                for h in (0, 1):
                    near_rows(i, color, h, part).wait_recv()
                    pass_rows(i, color, h, part).wait_recv()
            for cp in row_loads(i, color, part):
                cp.start()
        with scope('rowload_wait'):
            for color in (0, 1):
                for cp in row_loads(i, color, part):
                    cp.wait()

        def one(n, carry):
            j, color = n // 2, lax.rem(n, 2)
            m = lax.rem(2 + 3 * j + 3 * (j * (j - 1) // 2), 4)
            got = tok[8 * lax.rem(i, 2) + 4 * color + m, :, within(part)]
            total = acc[color, m, :, within(part)]
            for p in range(1, 4):
                g = jnp.concatenate([
                    jnp.where(tabs[color, m, s, 0, pl.ds(i, 1), :] == lanes, tabs[color, m, s, p, pl.ds(i, 1), :], 0.0).astype(BF16)
                    for s in range(4)], axis=0)
                total += lax.dot_general(g, got, (((0,), (0,)), ((), ())), preferred_element_type=F32)
            acc[color, m, :, within(part)] = total
            if then is not None:
                then(j, color)
            return carry

        lax.fori_loop(0, 8, one, 0)

    def load_up(i):
        handed(i, (0, 1))
        load(i, 0, begin)
        load(i, 1, begin)

    def load_down(i):
        handed(i, (2,))
        load(i, 2, begin)

    def down(i, ws):
        def one(t, carry):
            for w in ws:
                o = jnp.dot(hbuf[t], bd[:, w], preferred_element_type=F32).astype(BF16)
                stage[t, :, :, :, w] = o.reshape(2, 4, ROW_CAP, o.shape[-1])
                o_store(i, t, w).start()
            return carry

        with scope('down'):
            lax.fori_loop(0, 2, one, 0)
            for t in (0, 1):
                for w in ws:
                    o_store(i, t, w).wait()

    def send(i, part=None):
        for color, h in both:
            far_rows(i, color, h, part).start()
        for color, h in both:
            near_rows(i, color, h, part).start()

    def expert(i, carry):
        late = (i == 4) | (i == 6)
        for t in (0, 1):
            x_load(i, t).start()

        @pl.when(jnp.logical_not(late))
        def _():
            load_down(i)

        @pl.when(late)
        def _():
            with scope('late_gu'):
                load_up(i)

        with scope('load_gu'):
            load(i, 0, finish)
            load(i, 1, finish)

        def up(t, carry):
            x_load(i, t).wait()
            xs = xt[t].reshape(rows, d)
            a = jnp.dot(xs, bg[...], preferred_element_type=F32)
            u = jnp.dot(xs, bu[...], preferred_element_type=F32)
            hbuf[t] = (jax.nn.silu(a) * u).astype(BF16)
            return carry

        with scope('up'):
            lax.fori_loop(0, 2, up, 0)

        @pl.when((i < 3) | (i == 4))
        def _():
            with scope('next_gu'):
                load_up(i + 1)

        @pl.when(i == 4)
        def _():
            with scope('line1_d'):
                line_arrived(1, (2,))

        @pl.when(i == 6)
        def _():
            with scope('far0_d'):
                far_arrived(0, (2,))

        @pl.when(i >= 1)
        def _():
            with scope('relay'):
                relay_rows(i - 1)

        @pl.when(i >= 2)
        def _():
            with scope('combine'):
                combine(i - 2)

        @pl.when(i == 3)
        def _():
            with scope('line1_gu'):
                line_arrived(1, (0, 1))

        @pl.when(i == 5)
        def _():
            with scope('far0_gu'):
                far_arrived(0, (0, 1))

        @pl.when(late)
        def _():
            with scope('late_d'):
                load_down(i)

        with scope('load_d'):
            load(i, 2, finish)
        down(i, [pl.ds(0, d)])
        send(i)
        return carry

    with scope('line0'):
        line_arrived(0, (0, 1, 2))
    load_up(0)
    lax.fori_loop(0, EXPERTS - 1, expert, 0)

    last = EXPERTS - 1
    for t in (0, 1):
        x_load(last, t).start()
    with scope('combine'):
        combine(last - 2)
    with scope('last_g'):
        far_arrived(1, (0,))
        hand_on(last, 0).wait_recv()
        g_load = pltpu.make_async_copy(hg.at[last], bg, wsem.at[0])
        g_load.start()
        g_load.wait()

    def gate_half(t, carry):
        x_load(last, t).wait()
        a = jnp.dot(xt[t].reshape(rows, d), bg[...], preferred_element_type=F32)
        abuf[t] = jax.nn.silu(a)
        return carry

    with scope('gate_half'):
        lax.fori_loop(0, 2, gate_half, 0)
    with scope('relay'):
        relay_rows(last - 1)
    with scope('last_u'):
        far_arrived(1, (1,))
        hand_on(last, 1).wait_recv()
        u_load = pltpu.make_async_copy(hu.at[last], bu, wsem.at[1])
        u_load.start()
        u_load.wait()

    def up_half(t, carry):
        u = jnp.dot(xt[t].reshape(rows, d), bu[...], preferred_element_type=F32)
        hbuf[t] = (abuf[t] * u).astype(BF16)
        return carry

    with scope('up_half'):
        lax.fori_loop(0, 2, up_half, 0)
    for part in (0, 1):
        with scope('last_d'):
            for color in (0, 1):
                for q in (0, 1):
                    far_piece(q, part, color).wait_recv()
                hand_piece(part, color).start()
            d_loads = []
            for color in (0, 1):
                hand_piece(part, color).wait_recv()
                d_loads.append(pltpu.make_async_copy(hd.at[last, :, piece(color, part)], bd.at[:, piece(color, part)], wsem.at[color]))
                d_loads[-1].start()
            for cp in d_loads:
                cp.wait()
        down(last, [piece(0, part), piece(1, part)])
        send(last, part)
    with scope('relay'):
        relay_rows(last, 0)
    with scope('combine'):
        combine(last - 1)
    with scope('relay'):
        relay_rows(last, 1)

    for part in (0, 1):
        def then(j, color):
            @pl.when(j == 0)
            def _():
                far_sum(color, 0, part).start()
                far_sum(color, 1, part).start()

            for h in (0, 1):
                @pl.when(j == 1 + h)
                def _():
                    near_sum(color, h, 0, part).start()

        with scope('combine'):
            combine(last, part, then)
    for part in (0, 1):
        for color, h in both:
            with scope('farsum_wait'):
                far_sum(color, h, part).wait_recv()
            r, w = pl.ds(h * half, half), within(part)
            acc[color, 1 + 2 * h, r, w] = acc[color, 1 + 2 * h, r, w] + rf2[color, h, :, w]
            near_sum(color, h, 1, part).start()
    for part in (0, 1):
        w = within(part)
        for color in (0, 1):
            with scope('nearsum_wait'):
                for h in (0, 1):
                    for waits in (0, 1):
                        near_sum(color, h, waits, part).wait_recv()
            out[:, piece(color, part)] = (acc[color, 0, :, w] + rn2[color, 0, :, w] + rn2[color, 1, :, w]).astype(out.dtype)

    for part in (0, 1):
        for color, h in both:
            far_sum(color, h, part).wait_send()
            near_sum(color, h, 0, part).wait_send()
            near_sum(color, h, 1, part).wait_send()
            near_rows(last, color, h, part).wait_send()
            far_rows(last, color, h, part).wait_send()
            pass_rows(last, color, h, part).wait_send()
            far_piece(h, part, color).wait_send()
        for color in (0, 1):
            hand_piece(part, color).wait_send()

    def drain(i, carry):
        for color, h in both:
            near_rows(i, color, h).wait_send()
            far_rows(i, color, h).wait_send()
            pass_rows(i, color, h).wait_send()
        return carry

    lax.fori_loop(0, EXPERTS - 1, drain, 0)
    for dz, dy in peers:
        for cp in route_copies(dz, dy):
            cp.wait_send()
    for m in range(3):
        for n in (0, 1):
            hand_own(m, n).wait_send()
            for k in (0, 1):
                if (k, m) != (1, 2):
                    far_copy(k, m, n).wait_send()
                for way in (0, 1):
                    line_copy(way, k, m, n, held[m].at[k]).wait_send()
        for slot in range(2, 8 if m < 2 else 7):
            hand_on(slot, m).wait_send()


def run_moe(hidden, ids, gates, w_gate, w_up, w_down):
    tokens, d = hidden.shape
    f = w_gate.shape[1]
    half, cols = tokens // 2, d // 2
    hbm = pl.BlockSpec(memory_space=pl.ANY)
    dma = pltpu.SemaphoreType.DMA
    flops = 2 * EXPERTS * BLOCKS * ROW_CAP * d * (3 * f + 4 * tokens)

    def both_ways(*shape):
        return [dma(shape), dma(shape)]

    return pl.pallas_call(
        moe_kernel,
        in_specs=[hbm] * 6,
        out_specs=[pl.BlockSpec(memory_space=pltpu.VMEM)] + [hbm] * 7,
        out_shape=[
            jax.ShapeDtypeStruct((tokens, d), BF16),
            jax.ShapeDtypeStruct((EXPERTS, 4, 4, ROW_CAP, d), BF16),
            jax.ShapeDtypeStruct((EXPERTS, BLOCKS, ROW_CAP, d), BF16),
            jax.ShapeDtypeStruct((EXPERTS, 2, 3, 4, ROW_CAP, cols), BF16),
            jax.ShapeDtypeStruct((EXPERTS, 2, 2, 2, ROW_CAP, cols), BF16),
            jax.ShapeDtypeStruct((8, d, f), BF16),
            jax.ShapeDtypeStruct((8, d, f), BF16),
            jax.ShapeDtypeStruct((8, f, d), BF16),
        ],
        scratch_shapes=[
            pltpu.VMEM((BLOCKS, tokens, d), BF16),
            pltpu.VMEM((BLOCKS,) + ids.shape, jnp.int32),
            pltpu.VMEM((BLOCKS,) + gates.shape, F32),
            pltpu.VMEM((BLOCKS, EXPERTS, tokens), F32),
            pltpu.VMEM((2, 4, 4, 4, EXPERTS, tokens), F32),
            pltpu.VMEM((2, 4, tokens, cols), F32),
            pltpu.VMEM((2, 2, half, cols), F32),
            pltpu.VMEM((2, 2, tokens, cols), F32),
            pltpu.VMEM((2, 2, 4, ROW_CAP, d), BF16),
            pltpu.VMEM((2, TILE, ROW_CAP, d), BF16),
            pltpu.VMEM((2, TILE * ROW_CAP, f), F32),
            pltpu.VMEM((2, TILE * ROW_CAP, f), BF16),
            pltpu.VMEM((d, f), BF16),
            pltpu.VMEM((d, f), BF16),
            pltpu.VMEM((f, d), BF16),
            *both_ways(2, 5, 4), *both_ways(2, BLOCKS), *both_ways(2, 2, 3, 2), *both_ways(2, 3, 2), *both_ways(3, 2), *both_ways(6, 3),
            *both_ways(EXPERTS + 1, 2, 2), *both_ways(EXPERTS + 1, 2, 2), *both_ways(EXPERTS + 1, 2, 2), *both_ways(2, 2, 2), *both_ways(2, 2, 2, 2),
            *both_ways(2, 2, 2), *both_ways(2, 2), dma((3,)), dma((2,)), dma((2, 2)), dma((3,)), dma((2,)), dma((2, 4)),
        ],
        compiler_params=pltpu.CompilerParams(collective_id=0, has_side_effects=True, vmem_limit_bytes=63 * MIB),
        cost_estimate=pl.CostEstimate(flops=flops, bytes_accessed=400 * MIB, transcendentals=0),
        name='run_moe',
    )(hidden, ids, gates, w_gate, w_up, w_down)[0]


def solution(mesh):
    grid = Mesh(mesh.devices.reshape((mesh.shape['dp'],) + SIZES), ('dp',) + GRID)

    def body(hidden, route_idx, gate_weights, w_gate, w_up, w_down):
        return run_moe(hidden, route_idx.T, gate_weights.T, w_gate[0], w_up[0], w_down[0])

    r = P(('dp',) + GRID, None)
    e = P(GRID, None, None)
    return jax.shard_map(body, mesh=grid, in_specs=(r, r, r, e, e, e), out_specs=r, check_vma=False)
```

time: 400 us -> 381 us (0.953)
  Pallas kernels: 393 us -> 376 us
    pallas_call x1, Pallas kernels: 393 us -> 376 us  [run_moe(): pl.pallas_call(moe_kernel, in_specs=[hbm] * 6, out_specs=[pl.BlockSpec(me...]
where the time goes in v4:
time: 381 us; the launch traced here: 379 us
  Pallas kernels  376 us (99%)
    pallas_call x1, Pallas kernels, run_moe(): pl.pallas_call(moe_kernel, in_specs=[hbm] * 6, out_specs=[pl.BlockSpec(me...  376 us

profile of v4, /device:TPU:1, one launch (start us, length us, event | category | flops | bytes accessed | tf_op | source)
XLA Modules:
  0.0 378.5 jit_solution(9866711104072011274)
XLA Ops:
  0.0 376.2 %run_moe.1 = (bf16[256,2048]{1,0:T(8,128)(2,1)}, bf16[8,4,4,64,2048]{4,3,2,1,0:T(8,128)(2,1)}, bf16[8,16,64,2048]{3,2,1,0:T(8,128)(2,1)}, bf16[8,2,3,4,64,1024]{...) custom-call(bf16[256,2048]{1,0:T(8,128)(2,1)} %hid.1, ...), custom_call_target="tpu_custom_call" | custom-call | flops 111669149696 | bytes 419430400 | tf_op jit(solution)/shard_map/run_moe/pallas_call | solution.py:632
  376.2 2.3 copy.8

commit v5 on v4

--- a/solution.py
+++ b/solution.py
@@ -14,6 +14,9 @@
 EXPERTS = 8
 BLOCKS = 16
 TILE = 8
+PARTS = 4
+SUMS = 2
+UPS = 2
 MIB = 1024 * 1024
 scope = jax.named_scope
 
@@ -30,7 +33,7 @@
                tok, all_ids, all_gates, slots, tabs, acc, rf2, rn2, stage, xt, abuf, hbuf, bg, bu, bd,
                tsend, trecv, msend, mrecv, isend, irecv, fsend, frecv, dsend, drecv, psend, precv,
                nrsend, nrrecv, frsend, frrecv, fwsend, fwrecv, f2send, f2recv, n2send, n2recv,
-               gsend, grecv, qsend, qrecv, lsem, ssem, osem, wsem, xsem, csem):
+               gsend, grecv, qsend, qrecv, usend, urecv, vsend, vrecv, lsem, ssem, osem, wsem, xsem, csem):
     z, y, x, c = (lax.axis_index(a) for a in GRID)
     right, left = lax.rem(x + 1, 4), lax.rem(x + 3, 4)
     tokens, d = hid.shape
@@ -72,7 +75,7 @@
             line_copy(1, k, m, 1 - n, srcs[m]).start()
 
     def piece(color, part):
-        return pl.ds(color * cols + part * (cols // 2), cols // 2)
+        return pl.ds(color * cols + part * (cols // PARTS), cols // PARTS)
 
     def piece_of(ref, lane, q, count, color, part):
         n = ref.shape[0] // 4
@@ -85,6 +88,21 @@
     def hand_piece(part, color):
         ref = piece_of(hd.at[7], c, 0, 2, color, part)
         return remote(ref, ref, qsend.at[part, color], qrecv.at[part, color], partner)
+
+    def strip(part):
+        n = wu.shape[1] // UPS
+        return pl.ds(part * n, n)
+
+    def strip_of(ref, lane, q, count, part):
+        n = ref.shape[0] // 4
+        return ref.at[pl.ds(pl.multiple_of((2 * lane + q) * n, n), count * n), strip(part)]
+
+    def far_strip(q, part):
+        return remote(strip_of(hu.at[4 + q], c, q, 1, part), strip_of(hu.at[7], c, q, 1, part), usend.at[q, part], urecv.at[q, part], {'x': right if q == 0 else left})
+
+    def hand_strip(part):
+        ref = strip_of(hu.at[7], c, 0, 2, part)
+        return remote(ref, ref, vsend.at[part], vrecv.at[part], partner)
 
     def place(k, a, b):
         return a * 4 + b if k == 0 else b * 4 + a
@@ -118,8 +136,8 @@
             return o_hbm.at[i, pl.ds(m, n), ring, :, w]
         return o_hbm.at[i, ring, pl.ds(m, n), :, w]
 
-    def within(part):
-        return pl.ds(0, cols) if part is None else pl.ds(part * (cols // 2), cols // 2)
+    def within(part, parts=PARTS):
+        return pl.ds(0, cols) if part is None else pl.ds(part * (cols // parts), cols // parts)
 
     def row_sems(send, recv, i, part, color, h):
         n = i if part is None else i + part
@@ -135,11 +153,11 @@
         return remote(relay.at[i, color, h, :, :, within(part)], rows_in.at[i, color, 1, pl.ds(2 * h, 2), :, within(part)], *row_sems(fwsend, fwrecv, i, part, color, h))
 
     def far_sum(color, h, part):
-        r, w = pl.ds(h * half, half), within(part)
+        r, w = pl.ds(h * half, half), within(part, SUMS)
         return remote(acc.at[color, 2, r, w], rf2.at[color, h, :, w], f2send.at[color, h, part], f2recv.at[color, h, part], along(color, 1 + 2 * h))
 
     def near_sum(color, h, waits, part):
-        r, w = pl.ds((h if waits else 1 - h) * half, half), within(part)
+        r, w = pl.ds((h if waits else 1 - h) * half, half), within(part, SUMS)
         return remote(acc.at[color, 1 + 2 * h, r, w], rn2.at[color, h, r, w], n2send.at[color, h, waits, part], n2recv.at[color, h, waits, part], along(color, 1 + 2 * h))
 
     both = [(color, h) for color in (0, 1) for h in (0, 1)]
@@ -308,8 +326,11 @@
             for way in (0, 1):
                 for q in (way, 1 - way):
                     line_copy(way, k, m, q, held[m].at[k]).wait_recv()
-                if (k, m) == (1, 2):
-                    for part in (0, 1):
+                if (k, m) == (1, 1):
+                    for part in range(UPS):
+                        far_strip(way, part).start()
+                elif (k, m) == (1, 2):
+                    for part in range(PARTS):
                         for color in (0, 1):
                             far_piece(way, part, color).start()
                 else:
@@ -351,40 +372,50 @@
             far_rows(i, color, h, part).wait_recv()
             pass_rows(i, color, h, part).start()
 
-    def row_loads(i, color, part):
+    def row_loads(i, color, w):
         at = pl.ds(8 * lax.rem(i, 2) + 4 * color, 4)
-        srcs = [spread(color, i, 0, 0, 4, part)] + [rows_in.at[i, color, s, :, :, within(part)] for s in range(3)]
-        return [pltpu.make_async_copy(src, tok.at[at, pl.ds(s * ROW_CAP, ROW_CAP), within(part)], csem.at[color, s]) for s, src in enumerate(srcs)]
-
-    def combine(i, part=None, then=None):
+        here = pl.ds(color * cols + w.start, w.size)
+        srcs = [o_hbm.at[i, :, 0, :, here] if color == 0 else o_hbm.at[i, 0, :, :, here]] + [rows_in.at[i, color, s, :, :, w] for s in range(3)]
+        return [pltpu.make_async_copy(src, tok.at[at, pl.ds(s * ROW_CAP, ROW_CAP), w], csem.at[color, s]) for s, src in enumerate(srcs)]
+
+    def fetch_rows(i, w, parts=(None,)):
         for color in (0, 1):
             with scope('rows_wait'):
-                for h in (0, 1):
-                    near_rows(i, color, h, part).wait_recv()
-                    pass_rows(i, color, h, part).wait_recv()
-            for cp in row_loads(i, color, part):
+                for part in parts:
+                    for h in (0, 1):
+                        near_rows(i, color, h, part).wait_recv()
+                        pass_rows(i, color, h, part).wait_recv()
+            for cp in row_loads(i, color, w):
                 cp.start()
+
+    def await_rows(i, w):
         with scope('rowload_wait'):
             for color in (0, 1):
-                for cp in row_loads(i, color, part):
+                for cp in row_loads(i, color, w):
                     cp.wait()
 
+    def add_rows(i, w, start=0, stop=8, then=None):
         def one(n, carry):
             j, color = n // 2, lax.rem(n, 2)
             m = lax.rem(2 + 3 * j + 3 * (j * (j - 1) // 2), 4)
-            got = tok[8 * lax.rem(i, 2) + 4 * color + m, :, within(part)]
-            total = acc[color, m, :, within(part)]
+            got = tok[8 * lax.rem(i, 2) + 4 * color + m, :, w]
+            total = acc[color, m, :, w]
             for p in range(1, 4):
                 g = jnp.concatenate([
                     jnp.where(tabs[color, m, s, 0, pl.ds(i, 1), :] == lanes, tabs[color, m, s, p, pl.ds(i, 1), :], 0.0).astype(BF16)
                     for s in range(4)], axis=0)
                 total += lax.dot_general(g, got, (((0,), (0,)), ((), ())), preferred_element_type=F32)
-            acc[color, m, :, within(part)] = total
+            acc[color, m, :, w] = total
             if then is not None:
                 then(j, color)
             return carry
 
-        lax.fori_loop(0, 8, one, 0)
+        lax.fori_loop(start, stop, one, 0)
+
+    def combine(i, w, parts=(None,), then=None):
+        fetch_rows(i, w, parts)
+        await_rows(i, w)
+        add_rows(i, w, then=then)
 
     def load_up(i):
         handed(i, (0, 1))
@@ -467,7 +498,7 @@
         @pl.when(i >= 2)
         def _():
             with scope('combine'):
-                combine(i - 2)
+                combine(i - 2, within(None))
 
         @pl.when(i == 3)
         def _():
@@ -498,13 +529,20 @@
     last = EXPERTS - 1
     for t in (0, 1):
         x_load(last, t).start()
-    with scope('combine'):
-        combine(last - 2)
+    def strip_arrived(part):
+        far_strip(0, part).wait_recv()
+        far_strip(1, part).wait_recv()
+        hand_strip(part).start()
+
     with scope('last_g'):
         far_arrived(1, (0,))
+    with scope('combine'):
+        combine(last - 2, within(None))
+    with scope('last_g'):
         hand_on(last, 0).wait_recv()
         g_load = pltpu.make_async_copy(hg.at[last], bg, wsem.at[0])
         g_load.start()
+        strip_arrived(0)
         g_load.wait()
 
     def gate_half(t, carry):
@@ -517,26 +555,55 @@
         lax.fori_loop(0, 2, gate_half, 0)
     with scope('relay'):
         relay_rows(last - 1)
-    with scope('last_u'):
-        far_arrived(1, (1,))
-        hand_on(last, 1).wait_recv()
-        u_load = pltpu.make_async_copy(hu.at[last], bu, wsem.at[1])
-        u_load.start()
-        u_load.wait()
-
-    def up_half(t, carry):
-        u = jnp.dot(xt[t].reshape(rows, d), bu[...], preferred_element_type=F32)
-        hbuf[t] = (abuf[t] * u).astype(BF16)
-        return carry
-
-    with scope('up_half'):
-        lax.fori_loop(0, 2, up_half, 0)
-    for part in (0, 1):
+    def piece_arrived(part):
+        for color in (0, 1):
+            for q in (0, 1):
+                far_piece(q, part, color).wait_recv()
+            hand_piece(part, color).start()
+
+    for part in range(UPS):
+        with scope('last_u'):
+            hand_strip(part).wait_recv()
+            u_load = pltpu.make_async_copy(hu.at[last, :, strip(part)], bu.at[:, strip(part)], wsem.at[1])
+            u_load.start()
+            u_load.wait()
+        if part + 1 == UPS:
+            with scope('piece'):
+                piece_arrived(0)
+
+        def up_half(t, carry):
+            u = jnp.dot(xt[t].reshape(rows, d), bu[:, strip(part)], preferred_element_type=F32)
+            hbuf[t, :, strip(part)] = (abuf[t, :, strip(part)] * u).astype(BF16)
+            return carry
+
+        with scope('up_half'):
+            lax.fori_loop(0, 2, up_half, 0)
+        if part + 1 < UPS:
+            with scope('strip'):
+                strip_arrived(part + 1)
+
+    every = within(None)
+    first, second = within(0, SUMS), within(1, SUMS)
+
+    def then_first(j, color):
+        spread_sums(j, color, 0)
+
+    def then_second(j, color):
+        spread_sums(j, color, 1)
+
+    def spread_sums(j, color, part):
+        @pl.when(j == 0)
+        def _():
+            far_sum(color, 0, part).start()
+            far_sum(color, 1, part).start()
+
+        for h in (0, 1):
+            @pl.when(j == 1 + h)
+            def _():
+                near_sum(color, h, 0, part).start()
+
+    for part in range(PARTS):
         with scope('last_d'):
-            for color in (0, 1):
-                for q in (0, 1):
-                    far_piece(q, part, color).wait_recv()
-                hand_piece(part, color).start()
             d_loads = []
             for color in (0, 1):
                 hand_piece(part, color).wait_recv()
@@ -544,56 +611,68 @@
                 d_loads[-1].start()
             for cp in d_loads:
                 cp.wait()
+        if part + 1 < PARTS:
+            with scope('piece'):
+                piece_arrived(part + 1)
         down(last, [piece(0, part), piece(1, part)])
+        if part:
+            with scope('relay'):
+                relay_rows(last, part - 1)
         send(last, part)
+        with scope('between'):
+            if part == 0:
+                fetch_rows(last - 1, every)
+            if part == 1:
+                await_rows(last - 1, every)
+                add_rows(last - 1, every, 0, 3)
+            if part == 2:
+                add_rows(last - 1, every, 3, 6)
+            if part == 3:
+                fetch_rows(last, first, range(PARTS // SUMS))
+                add_rows(last - 1, every, 6, 8)
+    with scope('first_sums'):
+        await_rows(last, first)
+        add_rows(last, first, 0, 2, then_first)
     with scope('relay'):
-        relay_rows(last, 0)
-    with scope('combine'):
-        combine(last - 1)
-    with scope('relay'):
-        relay_rows(last, 1)
-
-    for part in (0, 1):
-        def then(j, color):
-            @pl.when(j == 0)
-            def _():
-                far_sum(color, 0, part).start()
-                far_sum(color, 1, part).start()
-
-            for h in (0, 1):
-                @pl.when(j == 1 + h)
-                def _():
-                    near_sum(color, h, 0, part).start()
-
-        with scope('combine'):
-            combine(last, part, then)
-    for part in (0, 1):
+        relay_rows(last, PARTS - 1)
+    with scope('first_sums'):
+        add_rows(last, first, 2, 8, then_first)
+    with scope('second_sums'):
+        combine(last, second, range(PARTS // SUMS, PARTS), then_second)
+    for part in range(SUMS):
         for color, h in both:
             with scope('farsum_wait'):
                 far_sum(color, h, part).wait_recv()
-            r, w = pl.ds(h * half, half), within(part)
+            r, w = pl.ds(h * half, half), within(part, SUMS)
             acc[color, 1 + 2 * h, r, w] = acc[color, 1 + 2 * h, r, w] + rf2[color, h, :, w]
             near_sum(color, h, 1, part).start()
-    for part in (0, 1):
-        w = within(part)
+    for part in range(SUMS):
+        w = within(part, SUMS)
         for color in (0, 1):
             with scope('nearsum_wait'):
                 for h in (0, 1):
                     for waits in (0, 1):
                         near_sum(color, h, waits, part).wait_recv()
-            out[:, piece(color, part)] = (acc[color, 0, :, w] + rn2[color, 0, :, w] + rn2[color, 1, :, w]).astype(out.dtype)
-
-    for part in (0, 1):
-        for color, h in both:
+            here = pl.ds(color * cols + w.start, w.size)
+            out[:, here] = (acc[color, 0, :, w] + rn2[color, 0, :, w] + rn2[color, 1, :, w]).astype(out.dtype)
+
+    for color, h in both:
+        for part in range(SUMS):
             far_sum(color, h, part).wait_send()
             near_sum(color, h, 0, part).wait_send()
             near_sum(color, h, 1, part).wait_send()
+        for part in range(PARTS):
             near_rows(last, color, h, part).wait_send()
             far_rows(last, color, h, part).wait_send()
             pass_rows(last, color, h, part).wait_send()
             far_piece(h, part, color).wait_send()
-        for color in (0, 1):
+    for color in (0, 1):
+        for part in range(PARTS):
             hand_piece(part, color).wait_send()
+    for part in range(UPS):
+        far_strip(0, part).wait_send()
+        far_strip(1, part).wait_send()
+        hand_strip(part).wait_send()
 
     def drain(i, carry):
         for color, h in both:
@@ -610,11 +689,11 @@
         for n in (0, 1):
             hand_own(m, n).wait_send()
             for k in (0, 1):
-                if (k, m) != (1, 2):
+                if k == 0 or m == 0:
                     far_copy(k, m, n).wait_send()
                 for way in (0, 1):
                     line_copy(way, k, m, n, held[m].at[k]).wait_send()
-        for slot in range(2, 8 if m < 2 else 7):
+        for slot in range(2, 8 if m == 0 else 7):
             hand_on(slot, m).wait_send()
 
 
@@ -660,8 +739,8 @@
             pltpu.VMEM((d, f), BF16),
             pltpu.VMEM((f, d), BF16),
             *both_ways(2, 5, 4), *both_ways(2, BLOCKS), *both_ways(2, 2, 3, 2), *both_ways(2, 3, 2), *both_ways(3, 2), *both_ways(6, 3),
-            *both_ways(EXPERTS + 1, 2, 2), *both_ways(EXPERTS + 1, 2, 2), *both_ways(EXPERTS + 1, 2, 2), *both_ways(2, 2, 2), *both_ways(2, 2, 2, 2),
-            *both_ways(2, 2, 2), *both_ways(2, 2), dma((3,)), dma((2,)), dma((2, 2)), dma((3,)), dma((2,)), dma((2, 4)),
+            *[sem for _ in range(3) for sem in both_ways(EXPERTS - 1 + PARTS, 2, 2)], *both_ways(2, 2, SUMS), *both_ways(2, 2, 2, SUMS),
+            *both_ways(2, PARTS, 2), *both_ways(PARTS, 2), *both_ways(2, UPS), *both_ways(UPS), dma((3,)), dma((2,)), dma((2, 2)), dma((3,)), dma((2,)), dma((2, 4)),
         ],
         compiler_params=pltpu.CompilerParams(collective_id=0, has_side_effects=True, vmem_limit_bytes=63 * MIB),
         cost_estimate=pl.CostEstimate(flops=flops, bytes_accessed=400 * MIB, transcendentals=0),

time: 381 us -> 375 us (0.984)
  Pallas kernels: 376 us -> 372 us
    pallas_call x1, Pallas kernels: 376 us -> 372 us  [run_moe(): pl.pallas_call(moe_kernel, in_specs=[hbm] * 6, out_specs=[pl.BlockSpec(me...]
where the time goes in v5:
time: 375 us
  Pallas kernels  372 us (99%)
    pallas_call x1, Pallas kernels, run_moe(): pl.pallas_call(moe_kernel, in_specs=[hbm] * 6, out_specs=[pl.BlockSpec(me...  372 us

profile of v5, /device:TPU:1, one launch (start us, length us, event | category | flops | bytes accessed | tf_op | source)
XLA Modules:
  0.0 374.6 jit_solution(11553448051138313005)
XLA Ops:
  0.0 372.3 %run_moe.1 = (bf16[256,2048]{1,0:T(8,128)(2,1)}, bf16[8,4,4,64,2048]{4,3,2,1,0:T(8,128)(2,1)}, bf16[8,16,64,2048]{3,2,1,0:T(8,128)(2,1)}, bf16[8,2,3,4,64,1024]{...) custom-call(bf16[256,2048]{1,0:T(8,128)(2,1)} %hid.1, ...), custom_call_target="tpu_custom_call" | custom-call | flops 111669149696 | bytes 419430400 | tf_op jit(solution)/shard_map/run_moe/pallas_call | solution.py:711
  372.3 2.3 copy.8

commit v6 on v5

--- a/solution.py
+++ b/solution.py
@@ -14,9 +14,12 @@
 EXPERTS = 8
 BLOCKS = 16
 TILE = 8
-PARTS = 4
+EDGES = (0, 256, 512, 768, 1024)
+PARTS = len(EDGES) - 1
 SUMS = 2
-UPS = 2
+FIRST = 2
+OPENING = 128
+UPS = 3
 MIB = 1024 * 1024
 scope = jax.named_scope
 
@@ -53,9 +56,15 @@
         n = own[m].shape[0] // 4
         return ref.at[pl.ds(pl.multiple_of((2 * lane + q) * n, n), count * n), :]
 
-    def line_copy(way, k, m, q, src):
-        dst = held[m].at[2 + 2 * k + way]
-        return remote(quarter(src, m, c, q), quarter(dst, m, c, q), isend.at[way, k, m, q], irecv.at[way, k, m, q], {'x': right if way == 0 else left})
+    def line_copies(way, k, m, src):
+        n = own[m].shape[0] // 2
+        cuts = (0, OPENING, n) if (k, m) == (1, 0) else (0, n)
+        dst, where = held[m].at[2 + 2 * k + way], {'x': right if way == 0 else left}
+        copies = []
+        for j, (a, b) in enumerate(zip(cuts, cuts[1:])):
+            at = pl.ds(pl.multiple_of(c * n + a, 64), b - a)
+            copies.append(remote(src.at[at, :], dst.at[at, :], isend.at[way, k, m, j], irecv.at[way, k, m, j], where))
+        return copies
 
     def far_copy(k, m, q):
         src, dst = held[m].at[2 + 2 * k + q], held[m].at[6 + k]
@@ -69,25 +78,23 @@
         ref = quarter(held[m].at[slot], m, c, 0, 2)
         return remote(ref, ref, psend.at[slot - 2, m], precv.at[slot - 2, m], partner)
 
-    def start_line(k, srcs, skip=0):
-        for n, m in [(n, m) for n in (0, 1) for m in range(3)][skip:]:
-            line_copy(0, k, m, n, srcs[m]).start()
-            line_copy(1, k, m, 1 - n, srcs[m]).start()
+    def start_line(k, m, src, which=(0, 1)):
+        for way in (0, 1):
+            for j, cp in enumerate(line_copies(way, k, m, src)):
+                if j in which:
+                    cp.start()
 
     def piece(color, part):
-        return pl.ds(color * cols + part * (cols // PARTS), cols // PARTS)
-
-    def piece_of(ref, lane, q, count, color, part):
-        n = ref.shape[0] // 4
-        return ref.at[pl.ds(pl.multiple_of((2 * lane + q) * n, n), count * n), piece(color, part)]
-
-    def far_piece(q, part, color):
-        src, dst = hd.at[4 + q], hd.at[7]
-        return remote(piece_of(src, c, q, 1, color, part), piece_of(dst, c, q, 1, color, part), gsend.at[q, part, color], grecv.at[q, part, color], {'x': right if q == 0 else left})
-
-    def hand_piece(part, color):
-        ref = piece_of(hd.at[7], c, 0, 2, color, part)
-        return remote(ref, ref, qsend.at[part, color], qrecv.at[part, color], partner)
+        return pl.ds(pl.multiple_of(color * cols + EDGES[part], 128), EDGES[part + 1] - EDGES[part])
+
+    def far_piece(q, part):
+        n = wd.shape[0] // 2
+        at = pl.ds(q * n, n), piece(c, part)
+        return remote(hd.at[4 + q, *at], hd.at[7, *at], gsend.at[q, part], grecv.at[q, part], {'x': right if q == 0 else left})
+
+    def hand_piece(part):
+        ref = hd.at[7, :, piece(c, part)]
+        return remote(ref, ref, qsend.at[part], qrecv.at[part], partner)
 
     def strip(part):
         n = wu.shape[1] // UPS
@@ -136,8 +143,11 @@
             return o_hbm.at[i, pl.ds(m, n), ring, :, w]
         return o_hbm.at[i, ring, pl.ds(m, n), :, w]
 
-    def within(part, parts=PARTS):
-        return pl.ds(0, cols) if part is None else pl.ds(part * (cols // parts), cols // parts)
+    def within(part):
+        return pl.ds(0, cols) if part is None else pl.ds(EDGES[part], EDGES[part + 1] - EDGES[part])
+
+    def sums(part):
+        return pl.ds(part * (cols // SUMS), cols // SUMS)
 
     def row_sems(send, recv, i, part, color, h):
         n = i if part is None else i + part
@@ -153,11 +163,11 @@
         return remote(relay.at[i, color, h, :, :, within(part)], rows_in.at[i, color, 1, pl.ds(2 * h, 2), :, within(part)], *row_sems(fwsend, fwrecv, i, part, color, h))
 
     def far_sum(color, h, part):
-        r, w = pl.ds(h * half, half), within(part, SUMS)
+        r, w = pl.ds(h * half, half), sums(part)
         return remote(acc.at[color, 2, r, w], rf2.at[color, h, :, w], f2send.at[color, h, part], f2recv.at[color, h, part], along(color, 1 + 2 * h))
 
     def near_sum(color, h, waits, part):
-        r, w = pl.ds((h if waits else 1 - h) * half, half), within(part, SUMS)
+        r, w = pl.ds((h if waits else 1 - h) * half, half), sums(part)
         return remote(acc.at[color, 1 + 2 * h, r, w], rn2.at[color, h, r, w], n2send.at[color, h, waits, part], n2recv.at[color, h, waits, part], along(color, 1 + 2 * h))
 
     both = [(color, h) for color in (0, 1) for h in (0, 1)]
@@ -179,12 +189,12 @@
 
     @pl.when(c == 0)
     def _():
-        start_line(0, own)
+        for m in range(3):
+            start_line(0, m, own[m])
 
     @pl.when(c == 1)
     def _():
-        line_copy(0, 1, 0, 0, own[0]).start()
-        line_copy(1, 1, 0, 1, own[0]).start()
+        start_line(1, 0, own[0], (0,))
 
     own_tok.wait()
     for k in (0, 1):
@@ -199,14 +209,18 @@
     for m in range(3):
         hand_own(m, 0).wait_recv()
 
-    @pl.when(c == 0)
-    def _():
-        start_line(1, [ref.at[1] for ref in held])
-
-    @pl.when(c == 1)
-    def _():
-        start_line(0, [ref.at[0] for ref in held])
-        start_line(1, own, 1)
+        @pl.when(c == 1)
+        def _():
+            start_line(0, m, held[m].at[0])
+
+    for m in range(3):
+        @pl.when(c == 0)
+        def _():
+            start_line(1, m, held[m].at[1])
+
+        @pl.when(c == 1)
+        def _():
+            start_line(1, m, own[m], (1,) if m == 0 else (0,))
 
     for k in (0, 1):
         first_copy(k, 0).wait_recv()
@@ -324,16 +338,12 @@
     def line_arrived(k, ms):
         for m in ms:
             for way in (0, 1):
-                for q in (way, 1 - way):
-                    line_copy(way, k, m, q, held[m].at[k]).wait_recv()
+                for cp in line_copies(way, k, m, held[m].at[k]):
+                    cp.wait_recv()
                 if (k, m) == (1, 1):
                     for part in range(UPS):
                         far_strip(way, part).start()
-                elif (k, m) == (1, 2):
-                    for part in range(PARTS):
-                        for color in (0, 1):
-                            far_piece(way, part, color).start()
-                else:
+                elif (k, m) != (1, 2):
                     far_copy(k, m, way).start()
                 hand_on(2 + 2 * k + way, m).start()
 
@@ -357,8 +367,7 @@
     def x_load(i, t):
         return pltpu.make_async_copy(x_hbm.at[i, pl.ds(t * TILE, TILE)], xt.at[t], xsem.at[t])
 
-    def o_store(i, t, w):
-        n = 0 if w.size == d else w.start // cols
+    def o_store(i, t, w, n):
         return pltpu.make_async_copy(stage.at[t, :, :, :, w], o_hbm.at[i, pl.ds(2 * t, 2), :, :, w], osem.at[t, n])
 
     def begin(cp):
@@ -428,23 +437,25 @@
 
     def down(i, ws):
         def one(t, carry):
-            for w in ws:
+            for n, w in enumerate(ws):
                 o = jnp.dot(hbuf[t], bd[:, w], preferred_element_type=F32).astype(BF16)
                 stage[t, :, :, :, w] = o.reshape(2, 4, ROW_CAP, o.shape[-1])
-                o_store(i, t, w).start()
+                o_store(i, t, w, n).start()
             return carry
 
         with scope('down'):
             lax.fori_loop(0, 2, one, 0)
             for t in (0, 1):
-                for w in ws:
-                    o_store(i, t, w).wait()
-
-    def send(i, part=None):
-        for color, h in both:
-            far_rows(i, color, h, part).start()
-        for color, h in both:
-            near_rows(i, color, h, part).start()
+                for n, w in enumerate(ws):
+                    o_store(i, t, w, n).wait()
+
+    def send(i, part=None, colors=(0, 1)):
+        for color in colors:
+            for h in (0, 1):
+                far_rows(i, color, h, part).start()
+        for color in colors:
+            for h in (0, 1):
+                near_rows(i, color, h, part).start()
 
     def expert(i, carry):
         late = (i == 4) | (i == 6)
@@ -454,6 +465,12 @@
         @pl.when(jnp.logical_not(late))
         def _():
             load_down(i)
+
+        @pl.when(i == 5)
+        def _():
+            for part in range(PARTS):
+                for q in (0, 1):
+                    far_piece(q, part).start()
 
         @pl.when(late)
         def _():
@@ -475,7 +492,12 @@
         with scope('up'):
             lax.fori_loop(0, 2, up, 0)
 
-        @pl.when((i < 3) | (i == 4))
+        @pl.when(i == 1)
+        def _():
+            with scope('line0'):
+                line_arrived(0, (0, 1, 2))
+
+        @pl.when((i == 0) | (i == 2) | (i == 4))
         def _():
             with scope('next_gu'):
                 load_up(i + 1)
@@ -499,6 +521,11 @@
         def _():
             with scope('combine'):
                 combine(i - 2, within(None))
+
+        @pl.when(i == 1)
+        def _():
+            with scope('next_gu'):
+                load_up(i + 1)
 
         @pl.when(i == 3)
         def _():
@@ -521,8 +548,6 @@
         send(i)
         return carry
 
-    with scope('line0'):
-        line_arrived(0, (0, 1, 2))
     load_up(0)
     lax.fori_loop(0, EXPERTS - 1, expert, 0)
 
@@ -533,6 +558,18 @@
         far_strip(0, part).wait_recv()
         far_strip(1, part).wait_recv()
         hand_strip(part).start()
+
+    def strip_arrived(part):
+        with scope('strip'):
+            far_strip(0, part).wait_recv()
+            far_strip(1, part).wait_recv()
+            hand_strip(part).start()
+
+    def gate_half(t, carry):
+        x_load(last, t).wait()
+        a = jnp.dot(xt[t].reshape(rows, d), bg[...], preferred_element_type=F32)
+        abuf[t] = jax.nn.silu(a)
+        return carry
 
     with scope('last_g'):
         far_arrived(1, (0,))
@@ -542,24 +579,24 @@
         hand_on(last, 0).wait_recv()
         g_load = pltpu.make_async_copy(hg.at[last], bg, wsem.at[0])
         g_load.start()
-        strip_arrived(0)
+    strip_arrived(0)
+    with scope('last_g'):
         g_load.wait()
-
-    def gate_half(t, carry):
-        x_load(last, t).wait()
-        a = jnp.dot(xt[t].reshape(rows, d), bg[...], preferred_element_type=F32)
-        abuf[t] = jax.nn.silu(a)
-        return carry
-
     with scope('gate_half'):
         lax.fori_loop(0, 2, gate_half, 0)
+    strip_arrived(1)
     with scope('relay'):
         relay_rows(last - 1)
+
     def piece_arrived(part):
-        for color in (0, 1):
+        with scope('piece'):
             for q in (0, 1):
-                far_piece(q, part, color).wait_recv()
-            hand_piece(part, color).start()
+                far_piece(q, part).wait_recv()
+            hand_piece(part).start()
+
+    def piece_load(color, part):
+        at = piece(color, part)
+        return pltpu.make_async_copy(hd.at[last, :, at], bd.at[:, at], wsem.at[color])
 
     for part in range(UPS):
         with scope('last_u'):
@@ -567,9 +604,6 @@
             u_load = pltpu.make_async_copy(hu.at[last, :, strip(part)], bu.at[:, strip(part)], wsem.at[1])
             u_load.start()
             u_load.wait()
-        if part + 1 == UPS:
-            with scope('piece'):
-                piece_arrived(0)
 
         def up_half(t, carry):
             u = jnp.dot(xt[t].reshape(rows, d), bu[:, strip(part)], preferred_element_type=F32)
@@ -578,12 +612,12 @@
 
         with scope('up_half'):
             lax.fori_loop(0, 2, up_half, 0)
-        if part + 1 < UPS:
-            with scope('strip'):
-                strip_arrived(part + 1)
+        if part + 2 < UPS:
+            strip_arrived(part + 2)
+    piece_arrived(0)
 
     every = within(None)
-    first, second = within(0, SUMS), within(1, SUMS)
+    first, second = sums(0), sums(1)
 
     def then_first(j, color):
         spread_sums(j, color, 0)
@@ -602,34 +636,43 @@
             def _():
                 near_sum(color, h, 0, part).start()
 
-    for part in range(PARTS):
+    for step in (0, 1):
         with scope('last_d'):
-            d_loads = []
+            if step:
+                hand_piece(0).wait_recv()
+            color = c if step == 0 else 1 - c
+            piece_load(color, 0).start()
+            piece_load(color, 0).wait()
+        if step:
+            piece_arrived(1)
+        down(last, [piece(color, 0)])
+        for k in (0, 1):
+            @pl.when(color == k)
+            def _():
+                send(last, 0, (k,))
+
+    for part in range(1, PARTS):
+        with scope('last_d'):
+            hand_piece(part).wait_recv()
             for color in (0, 1):
-                hand_piece(part, color).wait_recv()
-                d_loads.append(pltpu.make_async_copy(hd.at[last, :, piece(color, part)], bd.at[:, piece(color, part)], wsem.at[color]))
-                d_loads[-1].start()
-            for cp in d_loads:
-                cp.wait()
+                piece_load(color, part).start()
+            for color in (0, 1):
+                piece_load(color, part).wait()
         if part + 1 < PARTS:
-            with scope('piece'):
-                piece_arrived(part + 1)
+            piece_arrived(part + 1)
         down(last, [piece(0, part), piece(1, part)])
-        if part:
-            with scope('relay'):
-                relay_rows(last, part - 1)
+        with scope('relay'):
+            relay_rows(last, part - 1)
         send(last, part)
         with scope('between'):
-            if part == 0:
+            if part == 1:
                 fetch_rows(last - 1, every)
-            if part == 1:
+            if part == 2:
                 await_rows(last - 1, every)
-                add_rows(last - 1, every, 0, 3)
-            if part == 2:
-                add_rows(last - 1, every, 3, 6)
+                add_rows(last - 1, every, 0, 4)
             if part == 3:
-                fetch_rows(last, first, range(PARTS // SUMS))
-                add_rows(last - 1, every, 6, 8)
+                fetch_rows(last, first, range(FIRST))
+                add_rows(last - 1, every, 4, 8)
     with scope('first_sums'):
         await_rows(last, first)
         add_rows(last, first, 0, 2, then_first)
@@ -638,16 +681,16 @@
     with scope('first_sums'):
         add_rows(last, first, 2, 8, then_first)
     with scope('second_sums'):
-        combine(last, second, range(PARTS // SUMS, PARTS), then_second)
+        combine(last, second, range(FIRST, PARTS), then_second)
     for part in range(SUMS):
         for color, h in both:
             with scope('farsum_wait'):
                 far_sum(color, h, part).wait_recv()
-            r, w = pl.ds(h * half, half), within(part, SUMS)
+            r, w = pl.ds(h * half, half), sums(part)
             acc[color, 1 + 2 * h, r, w] = acc[color, 1 + 2 * h, r, w] + rf2[color, h, :, w]
             near_sum(color, h, 1, part).start()
     for part in range(SUMS):
-        w = within(part, SUMS)
+        w = sums(part)
         for color in (0, 1):
             with scope('nearsum_wait'):
                 for h in (0, 1):
@@ -665,10 +708,10 @@
             near_rows(last, color, h, part).wait_send()
             far_rows(last, color, h, part).wait_send()
             pass_rows(last, color, h, part).wait_send()
-            far_piece(h, part, color).wait_send()
-    for color in (0, 1):
-        for part in range(PARTS):
-            hand_piece(part, color).wait_send()
+    for part in range(PARTS):
+        far_piece(0, part).wait_send()
+        far_piece(1, part).wait_send()
+        hand_piece(part).wait_send()
     for part in range(UPS):
         far_strip(0, part).wait_send()
         far_strip(1, part).wait_send()
@@ -691,8 +734,8 @@
             for k in (0, 1):
                 if k == 0 or m == 0:
                     far_copy(k, m, n).wait_send()
-                for way in (0, 1):
-                    line_copy(way, k, m, n, held[m].at[k]).wait_send()
+                for cp in line_copies(n, k, m, held[m].at[k]):
+                    cp.wait_send()
         for slot in range(2, 8 if m == 0 else 7):
             hand_on(slot, m).wait_send()
 
@@ -713,7 +756,7 @@
         in_specs=[hbm] * 6,
         out_specs=[pl.BlockSpec(memory_space=pltpu.VMEM)] + [hbm] * 7,
         out_shape=[
-            jax.ShapeDtypeStruct((tokens, d), BF16),
+            pltpu.VMEM((tokens, d), BF16),
             jax.ShapeDtypeStruct((EXPERTS, 4, 4, ROW_CAP, d), BF16),
             jax.ShapeDtypeStruct((EXPERTS, BLOCKS, ROW_CAP, d), BF16),
             jax.ShapeDtypeStruct((EXPERTS, 2, 3, 4, ROW_CAP, cols), BF16),
@@ -740,9 +783,9 @@
             pltpu.VMEM((f, d), BF16),
             *both_ways(2, 5, 4), *both_ways(2, BLOCKS), *both_ways(2, 2, 3, 2), *both_ways(2, 3, 2), *both_ways(3, 2), *both_ways(6, 3),
             *[sem for _ in range(3) for sem in both_ways(EXPERTS - 1 + PARTS, 2, 2)], *both_ways(2, 2, SUMS), *both_ways(2, 2, 2, SUMS),
-            *both_ways(2, PARTS, 2), *both_ways(PARTS, 2), *both_ways(2, UPS), *both_ways(UPS), dma((3,)), dma((2,)), dma((2, 2)), dma((3,)), dma((2,)), dma((2, 4)),
+            *both_ways(2, PARTS), *both_ways(PARTS), *both_ways(2, UPS), *both_ways(UPS), dma((3,)), dma((2,)), dma((2, 2)), dma((3,)), dma((2,)), dma((2, 4)),
         ],
-        compiler_params=pltpu.CompilerParams(collective_id=0, has_side_effects=True, vmem_limit_bytes=63 * MIB),
+        compiler_params=pltpu.CompilerParams(collective_id=0, has_side_effects=True, vmem_limit_bytes=60 * MIB),
         cost_estimate=pl.CostEstimate(flops=flops, bytes_accessed=400 * MIB, transcendentals=0),
         name='run_moe',
     )(hidden, ids, gates, w_gate, w_up, w_down)[0]

time: 375 us -> 373 us (level)
  no operation moved by 1% of the time
where the time goes in v6:
time: 373 us; the launch traced here: 372 us
  Pallas kernels  371 us (99%)
    pallas_call x1, Pallas kernels, run_moe(): pl.pallas_call(moe_kernel, in_specs=[hbm] * 6, out_specs=[pl.BlockSpec(me...  371 us

profile of v6, /device:TPU:1, one launch (start us, length us, event | category | flops | bytes accessed | tf_op | source)
XLA Modules:
  0.0 371.7 jit_solution(2387953020158209751)
XLA Ops:
  0.0 370.7 %run_moe.1 = (bf16[256,2048]{1,0:T(8,128)(2,1)S(1)}, bf16[8,4,4,64,2048]{4,3,2,1,0:T(8,128)(2,1)}, bf16[8,16,64,2048]{3,2,1,0:T(8,128)(2,1)}, bf16[8,2,3,4,64,10...) custom-call(bf16[256,2048]{1,0:T(8,128)(2,1)} %hid.1, ...), custom_call_target="tpu_custom_call" | custom-call | flops 111669149696 | bytes 419430400 | tf_op jit(solution)/shard_map/run_moe/pallas_call | solution.py:754
  370.7 1.0 copy.8

commit v7 on v6

--- a/solution.py
+++ b/solution.py
@@ -33,10 +33,9 @@
 
 
 def moe_kernel(hid, ids, gates, wg, wu, wd, out, o_hbm, x_hbm, rows_in, relay, hg, hu, hd,
-               tok, all_ids, all_gates, slots, tabs, acc, rf2, rn2, stage, xt, abuf, hbuf, bg, bu, bd,
-               tsend, trecv, msend, mrecv, isend, irecv, fsend, frecv, dsend, drecv, psend, precv,
-               nrsend, nrrecv, frsend, frrecv, fwsend, fwrecv, f2send, f2recv, n2send, n2recv,
-               gsend, grecv, qsend, qrecv, usend, urecv, vsend, vrecv, lsem, ssem, osem, wsem, xsem, csem):
+               tok, all_ids, all_gates, slots, tabs, acc, rf2, rn2, last_relay, last_in, stage, xt, abuf, hbuf, bg, bu, bd,
+               tsend, trecv, msend, mrecv, wsend, irecv, frecv, drecv, precv, grecv, qrecv, urecv, vrecv,
+               rsend, rrecv, hrecv, ssend, f2recv, n2recv, lsem, ssem, wsem, xsem, csem):
     z, y, x, c = (lax.axis_index(a) for a in GRID)
     right, left = lax.rem(x + 1, 4), lax.rem(x + 3, 4)
     tokens, d = hid.shape
@@ -49,6 +48,12 @@
     def remote(src, dst, send, recv, where):
         return pltpu.make_async_remote_copy(src_ref=src, dst_ref=dst, send_sem=send, recv_sem=recv, device_id=where, device_id_type=MESH)
 
+    def received(ref, sem):
+        remote(ref, ref, sem, sem, partner).wait_recv()
+
+    def sent(ref, sem):
+        remote(ref, ref, sem, sem, partner).wait_send()
+
     def along(dim, step):
         return {'z': lax.rem(z + (1 - dim) * step, 4), 'y': lax.rem(y + dim * step, 4)}
 
@@ -56,33 +61,33 @@
         n = own[m].shape[0] // 4
         return ref.at[pl.ds(pl.multiple_of((2 * lane + q) * n, n), count * n), :]
 
-    def line_copies(way, k, m, src):
+    def line_copies(way, k, m, src, which=(0, 1)):
         n = own[m].shape[0] // 2
         cuts = (0, OPENING, n) if (k, m) == (1, 0) else (0, n)
         dst, where = held[m].at[2 + 2 * k + way], {'x': right if way == 0 else left}
         copies = []
-        for j, (a, b) in enumerate(zip(cuts, cuts[1:])):
+        for j in which[:len(cuts) - 1]:
+            a, b = cuts[j:j + 2]
             at = pl.ds(pl.multiple_of(c * n + a, 64), b - a)
-            copies.append(remote(src.at[at, :], dst.at[at, :], isend.at[way, k, m, j], irecv.at[way, k, m, j], where))
+            copies.append(remote(src.at[at, :], dst.at[at, :], wsend.at[m], irecv.at[way, k, m], where))
         return copies
 
     def far_copy(k, m, q):
         src, dst = held[m].at[2 + 2 * k + q], held[m].at[6 + k]
-        return remote(quarter(src, m, c, q), quarter(dst, m, c, q), fsend.at[k, m, q], frecv.at[k, m, q], {'x': right if q == 0 else left})
+        return remote(quarter(src, m, c, q), quarter(dst, m, c, q), wsend.at[m], frecv.at[3 * k + m], {'x': right if q == 0 else left})
 
     def hand_own(m, n):
         lane = 1 - c if n == 0 else c
-        return remote(quarter(own[m], m, lane, 0, 2), quarter(held[m].at[c], m, lane, 0, 2), dsend.at[m, n], drecv.at[m, n], partner)
+        return remote(quarter(own[m], m, lane, 0, 2), quarter(held[m].at[c], m, lane, 0, 2), wsend.at[m], drecv.at[m, n], partner)
 
     def hand_on(slot, m):
         ref = quarter(held[m].at[slot], m, c, 0, 2)
-        return remote(ref, ref, psend.at[slot - 2, m], precv.at[slot - 2, m], partner)
+        return remote(ref, ref, wsend.at[m], precv.at[3 * (slot - 2) + m], partner)
 
     def start_line(k, m, src, which=(0, 1)):
         for way in (0, 1):
-            for j, cp in enumerate(line_copies(way, k, m, src)):
-                if j in which:
-                    cp.start()
+            for cp in line_copies(way, k, m, src, which):
+                cp.start()
 
     def piece(color, part):
         return pl.ds(pl.multiple_of(color * cols + EDGES[part], 128), EDGES[part + 1] - EDGES[part])
@@ -90,11 +95,11 @@
     def far_piece(q, part):
         n = wd.shape[0] // 2
         at = pl.ds(q * n, n), piece(c, part)
-        return remote(hd.at[4 + q, *at], hd.at[7, *at], gsend.at[q, part], grecv.at[q, part], {'x': right if q == 0 else left})
+        return remote(hd.at[4 + q, *at], hd.at[7, *at], wsend.at[2], grecv.at[part], {'x': right if q == 0 else left})
 
     def hand_piece(part):
         ref = hd.at[7, :, piece(c, part)]
-        return remote(ref, ref, qsend.at[part], qrecv.at[part], partner)
+        return remote(ref, ref, wsend.at[2], qrecv.at[part], partner)
 
     def strip(part):
         n = wu.shape[1] // UPS
@@ -105,11 +110,11 @@
         return ref.at[pl.ds(pl.multiple_of((2 * lane + q) * n, n), count * n), strip(part)]
 
     def far_strip(q, part):
-        return remote(strip_of(hu.at[4 + q], c, q, 1, part), strip_of(hu.at[7], c, q, 1, part), usend.at[q, part], urecv.at[q, part], {'x': right if q == 0 else left})
+        return remote(strip_of(hu.at[4 + q], c, q, 1, part), strip_of(hu.at[7], c, q, 1, part), wsend.at[1], urecv.at[part], {'x': right if q == 0 else left})
 
     def hand_strip(part):
         ref = strip_of(hu.at[7], c, 0, 2, part)
-        return remote(ref, ref, vsend.at[part], vrecv.at[part], partner)
+        return remote(ref, ref, wsend.at[1], vrecv.at[part], partner)
 
     def place(k, a, b):
         return a * 4 + b if k == 0 else b * 4 + a
@@ -119,13 +124,13 @@
         return tok.at[place(k, a, b), r, pl.ds(k * cols, cols)]
 
     def first_copy(k, way):
-        sems = tsend.at[k, 4, way], trecv.at[k, 4, way], along(k, 1 + 2 * (way % 2))
+        sems = tsend, trecv.at[k, 4, min(way, 2)], along(k, 1 + 2 * (way % 2))
         if way < 2:
             return remote(part(k, 0, 0), part(k, 3 - 2 * way, 0), *sems)
         return remote(part(k, 7 - 2 * way, 0, way - 2), part(k, 2, 0, way - 2), *sems)
 
     def second_copy(k, a, way):
-        sems = tsend.at[k, a, way], trecv.at[k, a, way], along(1 - k, 1 + 2 * (way % 2))
+        sems = tsend, trecv.at[k, a, min(way, 2)], along(1 - k, 1 + 2 * (way % 2))
         if way < 2:
             return remote(part(k, a, 0), part(k, a, 3 - 2 * way), *sems)
         return remote(part(k, a, 7 - 2 * way, way - 2), part(k, a, 2, way - 2), *sems)
@@ -133,15 +138,23 @@
     def route_copies(dz, dy):
         s = ((4 - dz) % 4) * 4 + (4 - dy) % 4
         where = {'z': lax.rem(z + dz, 4), 'y': lax.rem(y + dy, 4)}
-        return [remote(ref.at[0], ref.at[s], msend.at[n, s], mrecv.at[n, s], where) for n, ref in enumerate((all_ids, all_gates))]
+        return [remote(ref.at[0], ref.at[s], msend.at[n], mrecv.at[n], where) for n, ref in enumerate((all_ids, all_gates))]
 
     peers = [(dz, dy) for dz in range(4) for dy in range(4) if dz or dy]
 
     def spread(color, i, ring, m, n, part=None):
-        w = pl.ds(color * cols, cols) if part is None else piece(color, part)
+        ref, w = (o_hbm.at[i], pl.ds(color * cols, cols)) if part is None else (stage, piece(color, part))
         if color == 0:
-            return o_hbm.at[i, pl.ds(m, n), ring, :, w]
-        return o_hbm.at[i, ring, pl.ds(m, n), :, w]
+            return ref.at[pl.ds(m, n), ring, :, w]
+        return ref.at[ring, pl.ds(m, n), :, w]
+
+    def landing(i, color, s, m, n, part):
+        if part is None:
+            return rows_in.at[i, color, s - 1, pl.ds(m, n)]
+        return last_in.at[color, s - 1, pl.ds(m, n), :, within(part)]
+
+    def halfway(i, color, h, part):
+        return relay.at[i, color, h] if part is None else last_relay.at[color, h, :, :, within(part)]
 
     def within(part):
         return pl.ds(0, cols) if part is None else pl.ds(EDGES[part], EDGES[part + 1] - EDGES[part])
@@ -150,25 +163,24 @@
         return pl.ds(part * (cols // SUMS), cols // SUMS)
 
     def row_sems(send, recv, i, part, color, h):
-        n = i if part is None else i + part
-        return send.at[n, color, h], recv.at[n, color, h], along(1 - color, 1 + 2 * h)
+        return send.at[i], recv.at[i if part is None else i + part], along(1 - color, 1 + 2 * h)
 
     def near_rows(i, color, h, part=None):
-        return remote(spread(color, i, 1 + 2 * h, 0, 4, part), rows_in.at[i, color, 2 - 2 * h, :, :, within(part)], *row_sems(nrsend, nrrecv, i, part, color, h))
+        return remote(spread(color, i, 1 + 2 * h, 0, 4, part), landing(i, color, 3 - 2 * h, 0, 4, part), *row_sems(rsend, rrecv, i, part, color, h))
 
     def far_rows(i, color, h, part=None):
-        return remote(spread(color, i, 2, 2 * h, 2, part), relay.at[i, color, h, :, :, within(part)], *row_sems(frsend, frrecv, i, part, color, h))
+        return remote(spread(color, i, 2, 2 * h, 2, part), halfway(i, color, h, part), *row_sems(rsend, hrecv, i, part, color, h))
 
     def pass_rows(i, color, h, part=None):
-        return remote(relay.at[i, color, h, :, :, within(part)], rows_in.at[i, color, 1, pl.ds(2 * h, 2), :, within(part)], *row_sems(fwsend, fwrecv, i, part, color, h))
+        return remote(halfway(i, color, h, part), landing(i, color, 2, 2 * h, 2, part), *row_sems(rsend, rrecv, i, part, color, h))
 
     def far_sum(color, h, part):
         r, w = pl.ds(h * half, half), sums(part)
-        return remote(acc.at[color, 2, r, w], rf2.at[color, h, :, w], f2send.at[color, h, part], f2recv.at[color, h, part], along(color, 1 + 2 * h))
+        return remote(acc.at[color, 2, r, w], rf2.at[color, h, :, w], ssend, f2recv.at[color, h, part], along(color, 1 + 2 * h))
 
     def near_sum(color, h, waits, part):
         r, w = pl.ds((h if waits else 1 - h) * half, half), sums(part)
-        return remote(acc.at[color, 1 + 2 * h, r, w], rn2.at[color, h, r, w], n2send.at[color, h, waits, part], n2recv.at[color, h, waits, part], along(color, 1 + 2 * h))
+        return remote(acc.at[color, 1 + 2 * h, r, w], rn2.at[color, h, r, w], ssend, n2recv.at[color, part], along(color, 1 + 2 * h))
 
     both = [(color, h) for color in (0, 1) for h in (0, 1)]
 
@@ -236,14 +248,12 @@
             second_copy(k, 0, way).wait_recv()
             second_copy(k, 0, 2 + way).start()
     for k in (0, 1):
-        first_copy(k, 2).wait_recv()
-        first_copy(k, 3).wait_recv()
+        received(part(k, 2, 0), trecv.at[k, 4, 2])
         second_copy(k, 2, 0).start()
         second_copy(k, 2, 1).start()
 
-    for dz, dy in peers:
-        for cp in route_copies(dz, dy):
-            cp.wait_recv()
+    for n, ref in enumerate((all_ids, all_gates)):
+        received(ref.at[pl.ds(1, BLOCKS - 1)], mrecv.at[n])
     order = lax.broadcasted_iota(jnp.int32, (EXPERTS, tokens), 0)
     earlier = lax.broadcasted_iota(jnp.int32, (tokens, tokens), 0) < lax.broadcasted_iota(jnp.int32, (tokens, tokens), 1)
     earlier = jnp.where(earlier, 1.0, 0.0).astype(BF16)
@@ -289,11 +299,10 @@
     lax.fori_loop(0, 32, ring_table, 0)
     for a in range(4):
         for k in (0, 1):
-            for way in (2, 3):
-                second_copy(k, a, way).wait_recv()
+            received(part(k, a, 2), trecv.at[k, a, 2])
 
     def x_store(s, b):
-        return pltpu.make_async_copy(stage.at[b].reshape(EXPERTS, ROW_CAP, d), x_hbm.at[:, s], ssem.at[b])
+        return pltpu.make_async_copy(stage.at[pl.ds(2 * b, 2)].reshape(EXPERTS, ROW_CAP, d), x_hbm.at[:, s], ssem.at[b])
 
     lanes = lax.broadcasted_iota(jnp.int32, (ROW_CAP, tokens), 0).astype(F32)
 
@@ -306,7 +315,7 @@
         def _():
             x_store(s, b).wait()
 
-        stage[b] = got.reshape(2, 4, ROW_CAP, d)
+        stage[pl.ds(2 * b, 2)] = got.reshape(2, 4, ROW_CAP, d)
         x_store(s, b).start()
         return carry
 
@@ -314,11 +323,7 @@
     acc[...] = jnp.zeros(acc.shape, F32)
     x_store(0, 0).wait()
     x_store(0, 1).wait()
-    for k in (0, 1):
-        for way in range(4):
-            first_copy(k, way).wait_send()
-            for a in range(4):
-                second_copy(k, a, way).wait_send()
+    sent(tok.at[pl.ds(1, BLOCKS - 1)], tsend)
 
     def load(i, m, go):
         dst = (bg, bu, bd)[m]
@@ -338,8 +343,7 @@
     def line_arrived(k, ms):
         for m in ms:
             for way in (0, 1):
-                for cp in line_copies(way, k, m, held[m].at[k]):
-                    cp.wait_recv()
+                received(quarter(held[m].at[2 + 2 * k + way], m, c, 0, 2), irecv.at[way, k, m])
                 if (k, m) == (1, 1):
                     for part in range(UPS):
                         far_strip(way, part).start()
@@ -349,8 +353,7 @@
 
     def far_arrived(k, ms):
         for m in ms:
-            far_copy(k, m, 0).wait_recv()
-            far_copy(k, m, 1).wait_recv()
+            received(quarter(held[m].at[6 + k], m, c, 0, 2), frecv.at[3 * k + m])
             hand_on(6 + k, m).start()
 
     def handed(i, ms):
@@ -367,8 +370,8 @@
     def x_load(i, t):
         return pltpu.make_async_copy(x_hbm.at[i, pl.ds(t * TILE, TILE)], xt.at[t], xsem.at[t])
 
-    def o_store(i, t, w, n):
-        return pltpu.make_async_copy(stage.at[t, :, :, :, w], o_hbm.at[i, pl.ds(2 * t, 2), :, :, w], osem.at[t, n])
+    def o_store(i, t):
+        return pltpu.make_async_copy(stage.at[pl.ds(2 * t, 2)], o_hbm.at[i, pl.ds(2 * t, 2)], ssem.at[t])
 
     def begin(cp):
         cp.start()
@@ -377,37 +380,43 @@
         cp.wait()
 
     def relay_rows(i, part=None):
+        if part is None:
+            received(relay.at[i], hrecv.at[i])
+        else:
+            received(last_relay.at[:, :, :, :, within(part)], hrecv.at[i + part])
         for color, h in both:
-            far_rows(i, color, h, part).wait_recv()
             pass_rows(i, color, h, part).start()
 
-    def row_loads(i, color, w):
+    def row_loads(i, color):
         at = pl.ds(8 * lax.rem(i, 2) + 4 * color, 4)
-        here = pl.ds(color * cols + w.start, w.size)
-        srcs = [o_hbm.at[i, :, 0, :, here] if color == 0 else o_hbm.at[i, 0, :, :, here]] + [rows_in.at[i, color, s, :, :, w] for s in range(3)]
-        return [pltpu.make_async_copy(src, tok.at[at, pl.ds(s * ROW_CAP, ROW_CAP), w], csem.at[color, s]) for s, src in enumerate(srcs)]
-
-    def fetch_rows(i, w, parts=(None,)):
+        srcs = [spread(color, i, 0, 0, 4)] + [rows_in.at[i, color, s] for s in range(3)]
+        return [pltpu.make_async_copy(src, tok.at[at, pl.ds(s * ROW_CAP, ROW_CAP), pl.ds(0, cols)], csem.at[color]) for s, src in enumerate(srcs)]
+
+    def rows_arrived(i, parts=(None,)):
+        with scope('rows_wait'):
+            for part in parts:
+                if part is None:
+                    received(rows_in.at[i], rrecv.at[i])
+                else:
+                    received(last_in.at[:, :, :, :, within(part)], rrecv.at[i + part])
+
+    def fetch_rows(i):
+        rows_arrived(i)
         for color in (0, 1):
-            with scope('rows_wait'):
-                for part in parts:
-                    for h in (0, 1):
-                        near_rows(i, color, h, part).wait_recv()
-                        pass_rows(i, color, h, part).wait_recv()
-            for cp in row_loads(i, color, w):
+            for cp in row_loads(i, color):
                 cp.start()
 
-    def await_rows(i, w):
+    def await_rows(i):
         with scope('rowload_wait'):
             for color in (0, 1):
-                for cp in row_loads(i, color, w):
-                    cp.wait()
-
-    def add_rows(i, w, start=0, stop=8, then=None):
+                ref = tok.at[pl.ds(8 * lax.rem(i, 2) + 4 * color, 4), :, pl.ds(0, cols)]
+                pltpu.make_async_copy(ref, ref, csem.at[color]).wait()
+
+    def add_rows(i, w, take, start=0, stop=8, then=None):
         def one(n, carry):
             j, color = n // 2, lax.rem(n, 2)
             m = lax.rem(2 + 3 * j + 3 * (j * (j - 1) // 2), 4)
-            got = tok[8 * lax.rem(i, 2) + 4 * color + m, :, w]
+            got = take(color, m)
             total = acc[color, m, :, w]
             for p in range(1, 4):
                 g = jnp.concatenate([
@@ -421,10 +430,20 @@
 
         lax.fori_loop(start, stop, one, 0)
 
-    def combine(i, w, parts=(None,), then=None):
-        fetch_rows(i, w, parts)
-        await_rows(i, w)
-        add_rows(i, w, then=then)
+    def add_fetched(i, start=0, stop=8):
+        add_rows(i, pl.ds(0, cols), lambda color, m: tok[8 * lax.rem(i, 2) + 4 * color + m, :, pl.ds(0, cols)], start, stop)
+
+    def add_last(w, start, stop, then):
+        def take(color, m):
+            here = pl.ds(pl.multiple_of(color * cols + w.start, 128), w.size)
+            return jnp.concatenate([stage[(1 - color) * m, color * m, :, here]] + [last_in[color, s, m, :, w] for s in range(3)], axis=0)
+
+        add_rows(EXPERTS - 1, w, take, start, stop, then)
+
+    def combine(i):
+        fetch_rows(i)
+        await_rows(i)
+        add_fetched(i)
 
     def load_up(i):
         handed(i, (0, 1))
@@ -435,19 +454,15 @@
         handed(i, (2,))
         load(i, 2, begin)
 
-    def down(i, ws):
+    def down(ws):
         def one(t, carry):
-            for n, w in enumerate(ws):
+            for w in ws:
                 o = jnp.dot(hbuf[t], bd[:, w], preferred_element_type=F32).astype(BF16)
-                stage[t, :, :, :, w] = o.reshape(2, 4, ROW_CAP, o.shape[-1])
-                o_store(i, t, w, n).start()
+                stage[pl.ds(2 * t, 2), :, :, w] = o.reshape(2, 4, ROW_CAP, o.shape[-1])
             return carry
 
         with scope('down'):
             lax.fori_loop(0, 2, one, 0)
-            for t in (0, 1):
-                for n, w in enumerate(ws):
-                    o_store(i, t, w, n).wait()
 
     def send(i, part=None, colors=(0, 1)):
         for color in colors:
@@ -520,7 +535,7 @@
         @pl.when(i >= 2)
         def _():
             with scope('combine'):
-                combine(i - 2, within(None))
+                combine(i - 2)
 
         @pl.when(i == 1)
         def _():
@@ -544,7 +559,12 @@
 
         with scope('load_d'):
             load(i, 2, finish)
-        down(i, [pl.ds(0, d)])
+        down([pl.ds(0, d)])
+        with scope('store'):
+            for t in (0, 1):
+                o_store(i, t).start()
+            for t in (0, 1):
+                o_store(i, t).wait()
         send(i)
         return carry
 
@@ -561,8 +581,7 @@
 
     def strip_arrived(part):
         with scope('strip'):
-            far_strip(0, part).wait_recv()
-            far_strip(1, part).wait_recv()
+            received(strip_of(hu.at[7], c, 0, 2, part), urecv.at[part])
             hand_strip(part).start()
 
     def gate_half(t, carry):
@@ -574,7 +593,7 @@
     with scope('last_g'):
         far_arrived(1, (0,))
     with scope('combine'):
-        combine(last - 2, within(None))
+        combine(last - 2)
     with scope('last_g'):
         hand_on(last, 0).wait_recv()
         g_load = pltpu.make_async_copy(hg.at[last], bg, wsem.at[0])
@@ -590,8 +609,7 @@
 
     def piece_arrived(part):
         with scope('piece'):
-            for q in (0, 1):
-                far_piece(q, part).wait_recv()
+            received(hd.at[7, :, piece(c, part)], grecv.at[part])
             hand_piece(part).start()
 
     def piece_load(color, part):
@@ -616,7 +634,6 @@
             strip_arrived(part + 2)
     piece_arrived(0)
 
-    every = within(None)
     first, second = sums(0), sums(1)
 
     def then_first(j, color):
@@ -645,7 +662,7 @@
             piece_load(color, 0).wait()
         if step:
             piece_arrived(1)
-        down(last, [piece(color, 0)])
+        down([piece(color, 0)])
         for k in (0, 1):
             @pl.when(color == k)
             def _():
@@ -658,30 +675,30 @@
                 piece_load(color, part).start()
             for color in (0, 1):
                 piece_load(color, part).wait()
+        down([piece(0, part), piece(1, part)])
+        send(last, part)
         if part + 1 < PARTS:
             piece_arrived(part + 1)
-        down(last, [piece(0, part), piece(1, part)])
         with scope('relay'):
             relay_rows(last, part - 1)
-        send(last, part)
         with scope('between'):
             if part == 1:
-                fetch_rows(last - 1, every)
+                fetch_rows(last - 1)
             if part == 2:
-                await_rows(last - 1, every)
-                add_rows(last - 1, every, 0, 4)
+                await_rows(last - 1)
+                add_fetched(last - 1, 0, 4)
             if part == 3:
-                fetch_rows(last, first, range(FIRST))
-                add_rows(last - 1, every, 4, 8)
+                add_fetched(last - 1, 4, 8)
+    rows_arrived(last, range(FIRST))
     with scope('first_sums'):
-        await_rows(last, first)
-        add_rows(last, first, 0, 2, then_first)
+        add_last(first, 0, 2, then_first)
     with scope('relay'):
         relay_rows(last, PARTS - 1)
     with scope('first_sums'):
-        add_rows(last, first, 2, 8, then_first)
+        add_last(first, 2, 8, then_first)
+    rows_arrived(last, range(FIRST, PARTS))
     with scope('second_sums'):
-        combine(last, second, range(FIRST, PARTS), then_second)
+        add_last(second, 0, 8, then_second)
     for part in range(SUMS):
         for color, h in both:
             with scope('farsum_wait'):
@@ -693,51 +710,18 @@
         w = sums(part)
         for color in (0, 1):
             with scope('nearsum_wait'):
-                for h in (0, 1):
-                    for waits in (0, 1):
-                        near_sum(color, h, waits, part).wait_recv()
+                received(rn2.at[color, :, :, w], n2recv.at[color, part])
             here = pl.ds(color * cols + w.start, w.size)
             out[:, here] = (acc[color, 0, :, w] + rn2[color, 0, :, w] + rn2[color, 1, :, w]).astype(out.dtype)
 
-    for color, h in both:
-        for part in range(SUMS):
-            far_sum(color, h, part).wait_send()
-            near_sum(color, h, 0, part).wait_send()
-            near_sum(color, h, 1, part).wait_send()
-        for part in range(PARTS):
-            near_rows(last, color, h, part).wait_send()
-            far_rows(last, color, h, part).wait_send()
-            pass_rows(last, color, h, part).wait_send()
-    for part in range(PARTS):
-        far_piece(0, part).wait_send()
-        far_piece(1, part).wait_send()
-        hand_piece(part).wait_send()
-    for part in range(UPS):
-        far_strip(0, part).wait_send()
-        far_strip(1, part).wait_send()
-        hand_strip(part).wait_send()
-
-    def drain(i, carry):
-        for color, h in both:
-            near_rows(i, color, h).wait_send()
-            far_rows(i, color, h).wait_send()
-            pass_rows(i, color, h).wait_send()
-        return carry
-
-    lax.fori_loop(0, EXPERTS - 1, drain, 0)
-    for dz, dy in peers:
-        for cp in route_copies(dz, dy):
-            cp.wait_send()
+    sent(acc.at[:, pl.ds(1, 3)], ssend)
+    for i in range(EXPERTS - 1):
+        sent(o_hbm.at[i], rsend.at[i])
+    sent(stage, rsend.at[last])
+    for n, ref in enumerate((all_ids, all_gates)):
+        sent(ref.at[pl.ds(1, BLOCKS - 1)], msend.at[n])
     for m in range(3):
-        for n in (0, 1):
-            hand_own(m, n).wait_send()
-            for k in (0, 1):
-                if k == 0 or m == 0:
-                    far_copy(k, m, n).wait_send()
-                for cp in line_copies(n, k, m, held[m].at[k]):
-                    cp.wait_send()
-        for slot in range(2, 8 if m == 0 else 7):
-            hand_on(slot, m).wait_send()
+        sent(held[m].at[pl.ds(0, EXPERTS - 1)], wsend.at[m])
 
 
 def run_moe(hidden, ids, gates, w_gate, w_up, w_down):
@@ -747,9 +731,6 @@
     hbm = pl.BlockSpec(memory_space=pl.ANY)
     dma = pltpu.SemaphoreType.DMA
     flops = 2 * EXPERTS * BLOCKS * ROW_CAP * d * (3 * f + 4 * tokens)
-
-    def both_ways(*shape):
-        return [dma(shape), dma(shape)]
 
     return pl.pallas_call(
         moe_kernel,
@@ -774,18 +755,19 @@
             pltpu.VMEM((2, 4, tokens, cols), F32),
             pltpu.VMEM((2, 2, half, cols), F32),
             pltpu.VMEM((2, 2, tokens, cols), F32),
-            pltpu.VMEM((2, 2, 4, ROW_CAP, d), BF16),
+            pltpu.VMEM((2, 2, 2, ROW_CAP, cols), BF16),
+            pltpu.VMEM((2, 3, 4, ROW_CAP, cols), BF16),
+            pltpu.VMEM((4, 4, ROW_CAP, d), BF16),
             pltpu.VMEM((2, TILE, ROW_CAP, d), BF16),
             pltpu.VMEM((2, TILE * ROW_CAP, f), F32),
             pltpu.VMEM((2, TILE * ROW_CAP, f), BF16),
             pltpu.VMEM((d, f), BF16),
             pltpu.VMEM((d, f), BF16),
             pltpu.VMEM((f, d), BF16),
-            *both_ways(2, 5, 4), *both_ways(2, BLOCKS), *both_ways(2, 2, 3, 2), *both_ways(2, 3, 2), *both_ways(3, 2), *both_ways(6, 3),
-            *[sem for _ in range(3) for sem in both_ways(EXPERTS - 1 + PARTS, 2, 2)], *both_ways(2, 2, SUMS), *both_ways(2, 2, 2, SUMS),
-            *both_ways(2, PARTS), *both_ways(PARTS), *both_ways(2, UPS), *both_ways(UPS), dma((3,)), dma((2,)), dma((2, 2)), dma((3,)), dma((2,)), dma((2, 4)),
+            dma(()), dma((2, 5, 3)), dma((2,)), dma((2,)), dma((3,)), dma((2, 2, 3)), dma((4,)), dma((3, 2)), dma((16,)), dma((PARTS,)), dma((PARTS,)), dma((UPS,)), dma((UPS,)),
+            dma((EXPERTS,)), dma((EXPERTS - 1 + PARTS,)), dma((EXPERTS - 1 + PARTS,)), dma(()), dma((2, 2, SUMS)), dma((2, SUMS)), dma((3,)), dma((2,)), dma((3,)), dma((2,)), dma((2,)),
         ],
-        compiler_params=pltpu.CompilerParams(collective_id=0, has_side_effects=True, vmem_limit_bytes=60 * MIB),
+        compiler_params=pltpu.CompilerParams(collective_id=0, has_side_effects=True, vmem_limit_bytes=62 * MIB),
         cost_estimate=pl.CostEstimate(flops=flops, bytes_accessed=400 * MIB, transcendentals=0),
         name='run_moe',
     )(hidden, ids, gates, w_gate, w_up, w_down)[0]

time: 373 us -> 367 us (0.984)
  Pallas kernels: 371 us -> 365 us
    pallas_call x1, Pallas kernels: 371 us -> 365 us  [run_moe(): pl.pallas_call(moe_kernel, in_specs=[hbm] * 6, out_specs=[pl.BlockSpec(me...]
where the time goes in v7:
time: 367 us; the launch traced here: 366 us
  Pallas kernels  365 us (99%)
    pallas_call x1, Pallas kernels, run_moe(): pl.pallas_call(moe_kernel, in_specs=[hbm] * 6, out_specs=[pl.BlockSpec(me...  365 us

profile of v7, /device:TPU:1, one launch (start us, length us, event | category | flops | bytes accessed | tf_op | source)
XLA Modules:
  0.0 366.2 jit_solution(2079940460960826859)
XLA Ops:
  0.0 365.2 %run_moe.1 = (bf16[256,2048]{1,0:T(8,128)(2,1)S(1)}, bf16[8,4,4,64,2048]{4,3,2,1,0:T(8,128)(2,1)}, bf16[8,16,64,2048]{3,2,1,0:T(8,128)(2,1)}, bf16[8,2,3,4,64,10...) custom-call(bf16[256,2048]{1,0:T(8,128)(2,1)} %hid.1, ...), custom_call_target="tpu_custom_call" | custom-call | flops 111669149696 | bytes 419430400 | tf_op jit(solution)/shard_map/run_moe/pallas_call | solution.py:735
  365.2 1.0 copy.8

commit v8 on v7

--- a/solution.py
+++ b/solution.py
@@ -282,7 +282,7 @@
         slot, gate = table((4 - 3 * color) * m, line)
         tabs[color, m, s, 0] = slot
         for p in range(1, 4):
-            term = gate.astype(BF16).astype(F32)
+            term = (gate * (1 - 2.0 ** -8) if p == 1 else gate).astype(BF16).astype(F32)
             tabs[color, m, s, p] = term
             gate = gate - term
         return carry

time: 367 us -> 367 us (level)
  no operation moved by 1% of the time
where the time goes in v8:
time: 367 us; the launch traced here: 366 us
  Pallas kernels  365 us (99%)
    pallas_call x1, Pallas kernels, run_moe(): pl.pallas_call(moe_kernel, in_specs=[hbm] * 6, out_specs=[pl.BlockSpec(me...  365 us

profile of v8, /device:TPU:1, one launch (start us, length us, event | category | flops | bytes accessed | tf_op | source)
XLA Modules:
  0.0 366.2 jit_solution(5763043786522886540)
XLA Ops:
  0.0 365.2 %run_moe.1 = (bf16[256,2048]{1,0:T(8,128)(2,1)S(1)}, bf16[8,4,4,64,2048]{4,3,2,1,0:T(8,128)(2,1)}, bf16[8,16,64,2048]{3,2,1,0:T(8,128)(2,1)}, bf16[8,2,3,4,64,10...) custom-call(bf16[256,2048]{1,0:T(8,128)(2,1)} %hid.1, ...), custom_call_target="tpu_custom_call" | custom-call | flops 111669149696 | bytes 419430400 | tf_op jit(solution)/shard_map/run_moe/pallas_call | solution.py:735
  365.2 1.0 copy.8

commit v9 on v8

--- a/solution.py
+++ b/solution.py
@@ -35,7 +35,7 @@
 def moe_kernel(hid, ids, gates, wg, wu, wd, out, o_hbm, x_hbm, rows_in, relay, hg, hu, hd,
                tok, all_ids, all_gates, slots, tabs, acc, rf2, rn2, last_relay, last_in, stage, xt, abuf, hbuf, bg, bu, bd,
                tsend, trecv, msend, mrecv, wsend, irecv, frecv, drecv, precv, grecv, qrecv, urecv, vrecv,
-               rsend, rrecv, hrecv, ssend, f2recv, n2recv, lsem, ssem, wsem, xsem, csem):
+               rsend, rrecv, hrecv, ssend, f2recv, n2recv, lsem, ssem, wsem, xsem, csem, free):
     z, y, x, c = (lax.axis_index(a) for a in GRID)
     right, left = lax.rem(x + 1, 4), lax.rem(x + 3, 4)
     tokens, d = hid.shape
@@ -95,10 +95,10 @@
     def far_piece(q, part):
         n = wd.shape[0] // 2
         at = pl.ds(q * n, n), piece(c, part)
-        return remote(hd.at[4 + q, *at], hd.at[7, *at], wsend.at[2], grecv.at[part], {'x': right if q == 0 else left})
+        return remote(hd.at[4 + q, *at], bd.at[*at], wsend.at[2], grecv.at[part], {'x': right if q == 0 else left})
 
     def hand_piece(part):
-        ref = hd.at[7, :, piece(c, part)]
+        ref = bd.at[:, piece(c, part)]
         return remote(ref, ref, wsend.at[2], qrecv.at[part], partner)
 
     def strip(part):
@@ -481,11 +481,6 @@
         def _():
             load_down(i)
 
-        @pl.when(i == 5)
-        def _():
-            for part in range(PARTS):
-                for q in (0, 1):
-                    far_piece(q, part).start()
 
         @pl.when(late)
         def _():
@@ -574,6 +569,13 @@
     last = EXPERTS - 1
     for t in (0, 1):
         x_load(last, t).start()
+    for where in (partner, {'x': right}, {'x': left}):
+        pl.semaphore_signal(free, inc=1, device_id=where, device_id_type=MESH)
+    with scope('free'):
+        pl.semaphore_wait(free, 3)
+    for part in range(PARTS):
+        for q in (0, 1):
+            far_piece(q, part).start()
     def strip_arrived(part):
         far_strip(0, part).wait_recv()
         far_strip(1, part).wait_recv()
@@ -609,12 +611,8 @@
 
     def piece_arrived(part):
         with scope('piece'):
-            received(hd.at[7, :, piece(c, part)], grecv.at[part])
+            received(bd.at[:, piece(c, part)], grecv.at[part])
             hand_piece(part).start()
-
-    def piece_load(color, part):
-        at = piece(color, part)
-        return pltpu.make_async_copy(hd.at[last, :, at], bd.at[:, at], wsem.at[color])
 
     for part in range(UPS):
         with scope('last_u'):
@@ -630,8 +628,8 @@
 
         with scope('up_half'):
             lax.fori_loop(0, 2, up_half, 0)
-        if part + 2 < UPS:
-            strip_arrived(part + 2)
+        if 1 <= part < UPS - 1:
+            strip_arrived(part + 1)
     piece_arrived(0)
 
     first, second = sums(0), sums(1)
@@ -654,27 +652,20 @@
                 near_sum(color, h, 0, part).start()
 
     for step in (0, 1):
-        with scope('last_d'):
-            if step:
+        color = c if step == 0 else 1 - c
+        if step:
+            with scope('last_d'):
                 hand_piece(0).wait_recv()
-            color = c if step == 0 else 1 - c
-            piece_load(color, 0).start()
-            piece_load(color, 0).wait()
-        if step:
-            piece_arrived(1)
         down([piece(color, 0)])
         for k in (0, 1):
             @pl.when(color == k)
             def _():
                 send(last, 0, (k,))
+    piece_arrived(1)
 
     for part in range(1, PARTS):
         with scope('last_d'):
             hand_piece(part).wait_recv()
-            for color in (0, 1):
-                piece_load(color, part).start()
-            for color in (0, 1):
-                piece_load(color, part).wait()
         down([piece(0, part), piece(1, part)])
         send(last, part)
         if part + 1 < PARTS:
@@ -765,7 +756,7 @@
             pltpu.VMEM((d, f), BF16),
             pltpu.VMEM((f, d), BF16),
             dma(()), dma((2, 5, 3)), dma((2,)), dma((2,)), dma((3,)), dma((2, 2, 3)), dma((4,)), dma((3, 2)), dma((16,)), dma((PARTS,)), dma((PARTS,)), dma((UPS,)), dma((UPS,)),
-            dma((EXPERTS,)), dma((EXPERTS - 1 + PARTS,)), dma((EXPERTS - 1 + PARTS,)), dma(()), dma((2, 2, SUMS)), dma((2, SUMS)), dma((3,)), dma((2,)), dma((3,)), dma((2,)), dma((2,)),
+            dma((EXPERTS,)), dma((EXPERTS - 1 + PARTS,)), dma((EXPERTS - 1 + PARTS,)), dma(()), dma((2, 2, SUMS)), dma((2, SUMS)), dma((3,)), dma((2,)), dma((3,)), dma((2,)), dma((2,)), pltpu.SemaphoreType.REGULAR,
         ],
         compiler_params=pltpu.CompilerParams(collective_id=0, has_side_effects=True, vmem_limit_bytes=62 * MIB),
         cost_estimate=pl.CostEstimate(flops=flops, bytes_accessed=400 * MIB, transcendentals=0),

time: 367 us -> 365 us (level)
  no operation moved by 1% of the time
where the time goes in v9:
time: 365 us
  Pallas kernels  364 us (100%)
    pallas_call x1, Pallas kernels, run_moe(): pl.pallas_call(moe_kernel, in_specs=[hbm] * 6, out_specs=[pl.BlockSpec(me...  364 us

profile of v9, /device:TPU:1, one launch (start us, length us, event | category | flops | bytes accessed | tf_op | source)
XLA Modules:
  0.0 364.6 jit_solution(7635868091798612616)
XLA Ops:
  0.0 363.6 %run_moe.1 = (bf16[256,2048]{1,0:T(8,128)(2,1)S(1)}, bf16[8,4,4,64,2048]{4,3,2,1,0:T(8,128)(2,1)}, bf16[8,16,64,2048]{3,2,1,0:T(8,128)(2,1)}, bf16[8,2,3,4,64,10...) custom-call(bf16[256,2048]{1,0:T(8,128)(2,1)} %hid.1, ...), custom_call_target="tpu_custom_call" | custom-call | flops 111669149696 | bytes 419430400 | tf_op jit(solution)/shard_map/run_moe/pallas_call | solution.py:726
  363.6 1.0 copy.8

commit v10 on v9

--- a/solution.py
+++ b/solution.py
@@ -14,10 +14,10 @@
 EXPERTS = 8
 BLOCKS = 16
 TILE = 8
-EDGES = (0, 256, 512, 768, 1024)
+EDGES = (0, 128, 256, 512, 768, 1024)
 PARTS = len(EDGES) - 1
 SUMS = 2
-FIRST = 2
+FIRST = 3
 OPENING = 128
 UPS = 3
 MIB = 1024 * 1024
@@ -35,7 +35,7 @@
 def moe_kernel(hid, ids, gates, wg, wu, wd, out, o_hbm, x_hbm, rows_in, relay, hg, hu, hd,
                tok, all_ids, all_gates, slots, tabs, acc, rf2, rn2, last_relay, last_in, stage, xt, abuf, hbuf, bg, bu, bd,
                tsend, trecv, msend, mrecv, wsend, irecv, frecv, drecv, precv, grecv, qrecv, urecv, vrecv,
-               rsend, rrecv, hrecv, ssend, f2recv, n2recv, lsem, ssem, wsem, xsem, csem, free):
+               rsend, rrecv, hrecv, ssend, f2recv, n2recv, lsem, ssem, wsem, xsem, csem, up_free, down_free):
     z, y, x, c = (lax.axis_index(a) for a in GRID)
     right, left = lax.rem(x + 1, 4), lax.rem(x + 3, 4)
     tokens, d = hid.shape
@@ -69,7 +69,7 @@
         for j in which[:len(cuts) - 1]:
             a, b = cuts[j:j + 2]
             at = pl.ds(pl.multiple_of(c * n + a, 64), b - a)
-            copies.append(remote(src.at[at, :], dst.at[at, :], wsend.at[m], irecv.at[way, k, m], where))
+            copies.append(remote(src.at[at, :], dst.at[at, :], wsend.at[m], irecv.at[k, m], where))
         return copies
 
     def far_copy(k, m, q):
@@ -82,7 +82,7 @@
 
     def hand_on(slot, m):
         ref = quarter(held[m].at[slot], m, c, 0, 2)
-        return remote(ref, ref, wsend.at[m], precv.at[3 * (slot - 2) + m], partner)
+        return remote(ref, ref, wsend.at[m], precv.at[2 * (slot - 2) + m // 2], partner)
 
     def start_line(k, m, src, which=(0, 1)):
         for way in (0, 1):
@@ -110,10 +110,10 @@
         return ref.at[pl.ds(pl.multiple_of((2 * lane + q) * n, n), count * n), strip(part)]
 
     def far_strip(q, part):
-        return remote(strip_of(hu.at[4 + q], c, q, 1, part), strip_of(hu.at[7], c, q, 1, part), wsend.at[1], urecv.at[part], {'x': right if q == 0 else left})
+        return remote(strip_of(hu.at[4 + q], c, q, 1, part), strip_of(bu, c, q, 1, part), wsend.at[1], urecv.at[part], {'x': right if q == 0 else left})
 
     def hand_strip(part):
-        ref = strip_of(hu.at[7], c, 0, 2, part)
+        ref = strip_of(bu, c, 0, 2, part)
         return remote(ref, ref, wsend.at[1], vrecv.at[part], partner)
 
     def place(k, a, b):
@@ -124,13 +124,13 @@
         return tok.at[place(k, a, b), r, pl.ds(k * cols, cols)]
 
     def first_copy(k, way):
-        sems = tsend, trecv.at[k, 4, min(way, 2)], along(k, 1 + 2 * (way % 2))
+        sems = tsend, trecv.at[4, way // 2], along(k, 1 + 2 * (way % 2))
         if way < 2:
             return remote(part(k, 0, 0), part(k, 3 - 2 * way, 0), *sems)
         return remote(part(k, 7 - 2 * way, 0, way - 2), part(k, 2, 0, way - 2), *sems)
 
     def second_copy(k, a, way):
-        sems = tsend, trecv.at[k, a, min(way, 2)], along(1 - k, 1 + 2 * (way % 2))
+        sems = tsend, trecv.at[a, way // 2], along(1 - k, 1 + 2 * (way % 2))
         if way < 2:
             return remote(part(k, a, 0), part(k, a, 3 - 2 * way), *sems)
         return remote(part(k, a, 7 - 2 * way, way - 2), part(k, a, 2, way - 2), *sems)
@@ -163,7 +163,7 @@
         return pl.ds(part * (cols // SUMS), cols // SUMS)
 
     def row_sems(send, recv, i, part, color, h):
-        return send.at[i], recv.at[i if part is None else i + part], along(1 - color, 1 + 2 * h)
+        return send, recv.at[i if part is None else i + part], along(1 - color, 1 + 2 * h)
 
     def near_rows(i, color, h, part=None):
         return remote(spread(color, i, 1 + 2 * h, 0, 4, part), landing(i, color, 3 - 2 * h, 0, 4, part), *row_sems(rsend, rrecv, i, part, color, h))
@@ -176,7 +176,7 @@
 
     def far_sum(color, h, part):
         r, w = pl.ds(h * half, half), sums(part)
-        return remote(acc.at[color, 2, r, w], rf2.at[color, h, :, w], ssend, f2recv.at[color, h, part], along(color, 1 + 2 * h))
+        return remote(acc.at[color, 2, r, w], rf2.at[color, h, :, w], ssend, f2recv.at[color, part], along(color, 1 + 2 * h))
 
     def near_sum(color, h, waits, part):
         r, w = pl.ds((h if waits else 1 - h) * half, half), sums(part)
@@ -234,23 +234,23 @@
         def _():
             start_line(1, m, own[m], (1,) if m == 0 else (0,))
 
-    for k in (0, 1):
-        first_copy(k, 0).wait_recv()
-        first_copy(k, 2).start()
-        second_copy(k, 3, 0).start()
-        second_copy(k, 3, 1).start()
-        first_copy(k, 1).wait_recv()
-        first_copy(k, 3).start()
-        second_copy(k, 1, 0).start()
-        second_copy(k, 1, 1).start()
+    def tokens_arrived(a, late):
+        received(tok.at[pl.ds(0, 1 if late else 2)], trecv.at[a, late])
+
+    tokens_arrived(4, 0)
     for k in (0, 1):
         for way in (0, 1):
-            second_copy(k, 0, way).wait_recv()
+            first_copy(k, 2 + way).start()
+            second_copy(k, 3, way).start()
+            second_copy(k, 1, way).start()
+    tokens_arrived(0, 0)
+    for k in (0, 1):
+        for way in (0, 1):
             second_copy(k, 0, 2 + way).start()
+    tokens_arrived(4, 1)
     for k in (0, 1):
-        received(part(k, 2, 0), trecv.at[k, 4, 2])
-        second_copy(k, 2, 0).start()
-        second_copy(k, 2, 1).start()
+        for way in (0, 1):
+            second_copy(k, 2, way).start()
 
     for n, ref in enumerate((all_ids, all_gates)):
         received(ref.at[pl.ds(1, BLOCKS - 1)], mrecv.at[n])
@@ -288,9 +288,9 @@
         return carry
 
     def turn(a):
+        tokens_arrived(a, 0)
         for k in (0, 1):
             for way in (0, 1):
-                second_copy(k, a, way).wait_recv()
                 second_copy(k, a, 2 + way).start()
 
     turn(3)
@@ -298,8 +298,7 @@
     turn(2)
     lax.fori_loop(0, 32, ring_table, 0)
     for a in range(4):
-        for k in (0, 1):
-            received(part(k, a, 2), trecv.at[k, a, 2])
+        tokens_arrived(a, 1)
 
     def x_store(s, b):
         return pltpu.make_async_copy(stage.at[pl.ds(2 * b, 2)].reshape(EXPERTS, ROW_CAP, d), x_hbm.at[:, s], ssem.at[b])
@@ -342,12 +341,9 @@
 
     def line_arrived(k, ms):
         for m in ms:
+            received(held[m].at[0], irecv.at[k, m])
             for way in (0, 1):
-                received(quarter(held[m].at[2 + 2 * k + way], m, c, 0, 2), irecv.at[way, k, m])
-                if (k, m) == (1, 1):
-                    for part in range(UPS):
-                        far_strip(way, part).start()
-                elif (k, m) != (1, 2):
+                if k == 0 or m == 0:
                     far_copy(k, m, way).start()
                 hand_on(2 + 2 * k + way, m).start()
 
@@ -364,8 +360,10 @@
 
         @pl.when(i >= 2)
         def _():
-            for m in ms:
-                hand_on(i, m).wait_recv()
+            if ms == (2,):
+                hand_on(i, 2).wait_recv()
+            else:
+                received(held[0].at[0], precv.at[2 * (i - 2)])
 
     def x_load(i, t):
         return pltpu.make_async_copy(x_hbm.at[i, pl.ds(t * TILE, TILE)], xt.at[t], xsem.at[t])
@@ -472,6 +470,10 @@
             for h in (0, 1):
                 near_rows(i, color, h, part).start()
 
+    def release(sem):
+        for where in (partner, {'x': right}, {'x': left}):
+            pl.semaphore_signal(sem, inc=1, device_id=where, device_id_type=MESH)
+
     def expert(i, carry):
         late = (i == 4) | (i == 6)
         for t in (0, 1):
@@ -507,6 +509,10 @@
             with scope('line0'):
                 line_arrived(0, (0, 1, 2))
 
+        @pl.when(i == 6)
+        def _():
+            release(up_free)
+
         @pl.when((i == 0) | (i == 2) | (i == 4))
         def _():
             with scope('next_gu'):
@@ -546,6 +552,13 @@
         def _():
             with scope('far0_gu'):
                 far_arrived(0, (0, 1))
+
+        @pl.when(i == 6)
+        def _():
+            pl.semaphore_wait(up_free, 3)
+            for part in range(UPS):
+                for q in (0, 1):
+                    far_strip(q, part).start()
 
         @pl.when(late)
         def _():
@@ -569,10 +582,8 @@
     last = EXPERTS - 1
     for t in (0, 1):
         x_load(last, t).start()
-    for where in (partner, {'x': right}, {'x': left}):
-        pl.semaphore_signal(free, inc=1, device_id=where, device_id_type=MESH)
-    with scope('free'):
-        pl.semaphore_wait(free, 3)
+    release(down_free)
+    pl.semaphore_wait(down_free, 3)
     for part in range(PARTS):
         for q in (0, 1):
             far_piece(q, part).start()
@@ -583,7 +594,7 @@
 
     def strip_arrived(part):
         with scope('strip'):
-            received(strip_of(hu.at[7], c, 0, 2, part), urecv.at[part])
+            received(strip_of(bu, c, 0, 2, part), urecv.at[part])
             hand_strip(part).start()
 
     def gate_half(t, carry):
@@ -617,19 +628,16 @@
     for part in range(UPS):
         with scope('last_u'):
             hand_strip(part).wait_recv()
-            u_load = pltpu.make_async_copy(hu.at[last, :, strip(part)], bu.at[:, strip(part)], wsem.at[1])
-            u_load.start()
-            u_load.wait()
 
         def up_half(t, carry):
             u = jnp.dot(xt[t].reshape(rows, d), bu[:, strip(part)], preferred_element_type=F32)
             hbuf[t, :, strip(part)] = (abuf[t, :, strip(part)] * u).astype(BF16)
             return carry
 
+        if 1 <= part < UPS - 1:
+            strip_arrived(part + 1)
         with scope('up_half'):
             lax.fori_loop(0, 2, up_half, 0)
-        if 1 <= part < UPS - 1:
-            strip_arrived(part + 1)
     piece_arrived(0)
 
     first, second = sums(0), sums(1)
@@ -651,35 +659,41 @@
             def _():
                 near_sum(color, h, 0, part).start()
 
-    for step in (0, 1):
-        color = c if step == 0 else 1 - c
-        if step:
-            with scope('last_d'):
-                hand_piece(0).wait_recv()
-        down([piece(color, 0)])
+    def result(part, color):
+        down([piece(color, part)])
         for k in (0, 1):
             @pl.when(color == k)
             def _():
-                send(last, 0, (k,))
+                send(last, part, (k,))
+
+    result(0, c)
     piece_arrived(1)
-
-    for part in range(1, PARTS):
+    with scope('last_d'):
+        hand_piece(0).wait_recv()
+    result(0, 1 - c)
+    result(1, c)
+    with scope('last_d'):
+        hand_piece(1).wait_recv()
+    result(1, 1 - c)
+    with scope('relay'):
+        relay_rows(last, 0)
+    for part in range(2, PARTS):
+        piece_arrived(part)
+        result(part, c)
+        if part == 2:
+            with scope('relay'):
+                relay_rows(last, 1)
+            fetch_rows(last - 1)
         with scope('last_d'):
             hand_piece(part).wait_recv()
-        down([piece(0, part), piece(1, part)])
-        send(last, part)
-        if part + 1 < PARTS:
-            piece_arrived(part + 1)
-        with scope('relay'):
-            relay_rows(last, part - 1)
+        result(part, 1 - c)
+        if part > 2:
+            with scope('relay'):
+                relay_rows(last, part - 1)
         with scope('between'):
-            if part == 1:
-                fetch_rows(last - 1)
             if part == 2:
                 await_rows(last - 1)
-                add_fetched(last - 1, 0, 4)
-            if part == 3:
-                add_fetched(last - 1, 4, 8)
+            add_fetched(last - 1, 2 * part - 4, 2 * part - 2 if part < PARTS - 1 else 8)
     rows_arrived(last, range(FIRST))
     with scope('first_sums'):
         add_last(first, 0, 2, then_first)
@@ -691,12 +705,14 @@
     with scope('second_sums'):
         add_last(second, 0, 8, then_second)
     for part in range(SUMS):
-        for color, h in both:
+        w = sums(part)
+        for color in (0, 1):
             with scope('farsum_wait'):
-                far_sum(color, h, part).wait_recv()
-            r, w = pl.ds(h * half, half), sums(part)
-            acc[color, 1 + 2 * h, r, w] = acc[color, 1 + 2 * h, r, w] + rf2[color, h, :, w]
-            near_sum(color, h, 1, part).start()
+                received(rf2.at[color, :, :, w], f2recv.at[color, part])
+            for h in (0, 1):
+                r = pl.ds(h * half, half)
+                acc[color, 1 + 2 * h, r, w] = acc[color, 1 + 2 * h, r, w] + rf2[color, h, :, w]
+                near_sum(color, h, 1, part).start()
     for part in range(SUMS):
         w = sums(part)
         for color in (0, 1):
@@ -706,9 +722,7 @@
             out[:, here] = (acc[color, 0, :, w] + rn2[color, 0, :, w] + rn2[color, 1, :, w]).astype(out.dtype)
 
     sent(acc.at[:, pl.ds(1, 3)], ssend)
-    for i in range(EXPERTS - 1):
-        sent(o_hbm.at[i], rsend.at[i])
-    sent(stage, rsend.at[last])
+    sent(o_hbm, rsend)
     for n, ref in enumerate((all_ids, all_gates)):
         sent(ref.at[pl.ds(1, BLOCKS - 1)], msend.at[n])
     for m in range(3):
@@ -755,8 +769,8 @@
             pltpu.VMEM((d, f), BF16),
             pltpu.VMEM((d, f), BF16),
             pltpu.VMEM((f, d), BF16),
-            dma(()), dma((2, 5, 3)), dma((2,)), dma((2,)), dma((3,)), dma((2, 2, 3)), dma((4,)), dma((3, 2)), dma((16,)), dma((PARTS,)), dma((PARTS,)), dma((UPS,)), dma((UPS,)),
-            dma((EXPERTS,)), dma((EXPERTS - 1 + PARTS,)), dma((EXPERTS - 1 + PARTS,)), dma(()), dma((2, 2, SUMS)), dma((2, SUMS)), dma((3,)), dma((2,)), dma((3,)), dma((2,)), dma((2,)), pltpu.SemaphoreType.REGULAR,
+            dma(()), dma((5, 2)), dma((2,)), dma((2,)), dma((3,)), dma((2, 3)), dma((4,)), dma((3, 2)), dma((11,)), dma((PARTS,)), dma((PARTS,)), dma((UPS,)), dma((UPS,)),
+            dma(()), dma((EXPERTS - 1 + PARTS,)), dma((EXPERTS - 1 + PARTS,)), dma(()), dma((2, SUMS)), dma((2, SUMS)), dma((3,)), dma((2,)), dma((3,)), dma((2,)), dma((2,)), pltpu.SemaphoreType.REGULAR, pltpu.SemaphoreType.REGULAR,
         ],
         compiler_params=pltpu.CompilerParams(collective_id=0, has_side_effects=True, vmem_limit_bytes=62 * MIB),
         cost_estimate=pl.CostEstimate(flops=flops, bytes_accessed=400 * MIB, transcendentals=0),

time: 365 us -> 363 us (level)
  no operation moved by 1% of the time
where the time goes in v10:
time: 363 us
  Pallas kernels  362 us (100%)
    pallas_call x1, Pallas kernels, run_moe(): pl.pallas_call(moe_kernel, in_specs=[hbm] * 6, out_specs=[pl.BlockSpec(me...  362 us

profile of v10, /device:TPU:1, one launch (start us, length us, event | category | flops | bytes accessed | tf_op | source)
XLA Modules:
  0.0 363.1 jit_solution(12489561501185607168)
XLA Ops:
  0.0 362.1 %run_moe.1 = (bf16[256,2048]{1,0:T(8,128)(2,1)S(1)}, bf16[8,4,4,64,2048]{4,3,2,1,0:T(8,128)(2,1)}, bf16[8,16,64,2048]{3,2,1,0:T(8,128)(2,1)}, bf16[8,2,3,4,64,10...) custom-call(bf16[256,2048]{1,0:T(8,128)(2,1)} %hid.1, ...), custom_call_target="tpu_custom_call" | custom-call | flops 111669149696 | bytes 419430400 | tf_op jit(solution)/shard_map/run_moe/pallas_call | solution.py:740
  362.1 1.0 copy.8

commit v11 on v10

--- a/solution.py
+++ b/solution.py
@@ -21,7 +21,24 @@
 OPENING = 128
 UPS = 3
 MIB = 1024 * 1024
+BOTH = (0, 1)
+RING = 4
+PAIR = 2
+WHOLE = None
+OTHERS = pl.ds(1, BLOCKS - 1)
 scope = jax.named_scope
+
+
+def repeat(count, step):
+    lax.fori_loop(0, count, step, 0)
+
+
+def wrap(n):
+    return lax.rem(n, RING)
+
+
+def toward(h):
+    return 1 + 2 * h
 
 
 def expert_ids(place, x, c, line):
@@ -29,17 +46,18 @@
     dx += jnp.where(place >= 6, 2, 0)
     core = jnp.where(place == 0, c, 0) + jnp.where(place == 1, 1 - c, 0)
     core += jnp.where((place == 4) | (place == 5) | (place == 7), 1, 0)
-    return line * EXPERTS + lax.rem(x + dx, 4) * 2 + core
+    return line * EXPERTS + wrap(x + dx) * 2 + core
 
 
 def moe_kernel(hid, ids, gates, wg, wu, wd, out, o_hbm, x_hbm, rows_in, relay, hg, hu, hd,
-               tok, all_ids, all_gates, slots, tabs, acc, rf2, rn2, last_relay, last_in, stage, xt, abuf, hbuf, bg, bu, bd,
+               tok, all_ids, all_gates, slots, tabs, acc, rf2, rn2, last_relay, last_in, stage, xt, abuf, ubuf, hbuf, bg, bu, bd,
                tsend, trecv, msend, mrecv, wsend, irecv, frecv, drecv, precv, grecv, qrecv, urecv, vrecv,
                rsend, rrecv, hrecv, ssend, f2recv, n2recv, lsem, ssem, wsem, xsem, csem, up_free, down_free):
     z, y, x, c = (lax.axis_index(a) for a in GRID)
-    right, left = lax.rem(x + 1, 4), lax.rem(x + 3, 4)
+    right, left = wrap(x + 1), wrap(x + 3)
     tokens, d = hid.shape
     half, cols = tokens // 2, d // 2
+    every = pl.ds(0, cols)
     rows = TILE * ROW_CAP
     own = (wg, wu, wd)
     held = (hg, hu, hd)
@@ -55,13 +73,16 @@
         remote(ref, ref, sem, sem, partner).wait_send()
 
     def along(dim, step):
-        return {'z': lax.rem(z + (1 - dim) * step, 4), 'y': lax.rem(y + dim * step, 4)}
+        return {'z': wrap(z + (1 - dim) * step), 'y': wrap(y + dim * step)}
 
     def quarter(ref, m, lane, q, count=1):
         n = own[m].shape[0] // 4
         return ref.at[pl.ds(pl.multiple_of((2 * lane + q) * n, n), count * n), :]
 
-    def line_copies(way, k, m, src, which=(0, 1)):
+    def lane_of(ref, m, lane):
+        return quarter(ref, m, lane, 0, 2)
+
+    def line_copies(way, k, m, src, which=BOTH):
         n = own[m].shape[0] // 2
         cuts = (0, OPENING, n) if (k, m) == (1, 0) else (0, n)
         dst, where = held[m].at[2 + 2 * k + way], {'x': right if way == 0 else left}
@@ -78,14 +99,14 @@
 
     def hand_own(m, n):
         lane = 1 - c if n == 0 else c
-        return remote(quarter(own[m], m, lane, 0, 2), quarter(held[m].at[c], m, lane, 0, 2), wsend.at[m], drecv.at[m, n], partner)
+        return remote(lane_of(own[m], m, lane), lane_of(held[m].at[c], m, lane), wsend.at[m], drecv.at[m, n], partner)
 
     def hand_on(slot, m):
-        ref = quarter(held[m].at[slot], m, c, 0, 2)
+        ref = lane_of(held[m].at[slot], m, c)
         return remote(ref, ref, wsend.at[m], precv.at[2 * (slot - 2) + m // 2], partner)
 
-    def start_line(k, m, src, which=(0, 1)):
-        for way in (0, 1):
+    def start_line(k, m, src, which=BOTH):
+        for way in BOTH:
             for cp in line_copies(way, k, m, src, which):
                 cp.start()
 
@@ -119,70 +140,70 @@
     def place(k, a, b):
         return a * 4 + b if k == 0 else b * 4 + a
 
-    def part(k, a, b, h=None):
-        r = pl.ds(0, tokens) if h is None else pl.ds(h * half, half)
+    def part(k, a, b, h=WHOLE):
+        r = pl.ds(0, tokens) if h is WHOLE else pl.ds(h * half, half)
         return tok.at[place(k, a, b), r, pl.ds(k * cols, cols)]
 
     def first_copy(k, way):
-        sems = tsend, trecv.at[4, way // 2], along(k, 1 + 2 * (way % 2))
+        sems = tsend, trecv.at[4, way // 2], along(k, toward(way % 2))
         if way < 2:
             return remote(part(k, 0, 0), part(k, 3 - 2 * way, 0), *sems)
         return remote(part(k, 7 - 2 * way, 0, way - 2), part(k, 2, 0, way - 2), *sems)
 
     def second_copy(k, a, way):
-        sems = tsend, trecv.at[a, way // 2], along(1 - k, 1 + 2 * (way % 2))
+        sems = tsend, trecv.at[a, way // 2], along(1 - k, toward(way % 2))
         if way < 2:
             return remote(part(k, a, 0), part(k, a, 3 - 2 * way), *sems)
         return remote(part(k, a, 7 - 2 * way, way - 2), part(k, a, 2, way - 2), *sems)
 
     def route_copies(dz, dy):
         s = ((4 - dz) % 4) * 4 + (4 - dy) % 4
-        where = {'z': lax.rem(z + dz, 4), 'y': lax.rem(y + dy, 4)}
+        where = {'z': wrap(z + dz), 'y': wrap(y + dy)}
         return [remote(ref.at[0], ref.at[s], msend.at[n], mrecv.at[n], where) for n, ref in enumerate((all_ids, all_gates))]
 
     peers = [(dz, dy) for dz in range(4) for dy in range(4) if dz or dy]
 
-    def spread(color, i, ring, m, n, part=None):
-        ref, w = (o_hbm.at[i], pl.ds(color * cols, cols)) if part is None else (stage, piece(color, part))
+    def spread(color, i, ring, m, n, part=WHOLE):
+        ref, w = (o_hbm.at[i], pl.ds(color * cols, cols)) if part is WHOLE else (stage, piece(color, part))
         if color == 0:
             return ref.at[pl.ds(m, n), ring, :, w]
         return ref.at[ring, pl.ds(m, n), :, w]
 
     def landing(i, color, s, m, n, part):
-        if part is None:
+        if part is WHOLE:
             return rows_in.at[i, color, s - 1, pl.ds(m, n)]
         return last_in.at[color, s - 1, pl.ds(m, n), :, within(part)]
 
     def halfway(i, color, h, part):
-        return relay.at[i, color, h] if part is None else last_relay.at[color, h, :, :, within(part)]
+        return relay.at[i, color, h] if part is WHOLE else last_relay.at[color, h, :, :, within(part)]
 
     def within(part):
-        return pl.ds(0, cols) if part is None else pl.ds(EDGES[part], EDGES[part + 1] - EDGES[part])
+        return every if part is WHOLE else pl.ds(EDGES[part], EDGES[part + 1] - EDGES[part])
 
     def sums(part):
         return pl.ds(part * (cols // SUMS), cols // SUMS)
 
     def row_sems(send, recv, i, part, color, h):
-        return send, recv.at[i if part is None else i + part], along(1 - color, 1 + 2 * h)
-
-    def near_rows(i, color, h, part=None):
-        return remote(spread(color, i, 1 + 2 * h, 0, 4, part), landing(i, color, 3 - 2 * h, 0, 4, part), *row_sems(rsend, rrecv, i, part, color, h))
-
-    def far_rows(i, color, h, part=None):
+        return send, recv.at[i if part is WHOLE else i + part], along(1 - color, toward(h))
+
+    def near_rows(i, color, h, part=WHOLE):
+        return remote(spread(color, i, toward(h), 0, 4, part), landing(i, color, 3 - 2 * h, 0, 4, part), *row_sems(rsend, rrecv, i, part, color, h))
+
+    def far_rows(i, color, h, part=WHOLE):
         return remote(spread(color, i, 2, 2 * h, 2, part), halfway(i, color, h, part), *row_sems(rsend, hrecv, i, part, color, h))
 
-    def pass_rows(i, color, h, part=None):
+    def pass_rows(i, color, h, part=WHOLE):
         return remote(halfway(i, color, h, part), landing(i, color, 2, 2 * h, 2, part), *row_sems(rsend, rrecv, i, part, color, h))
 
     def far_sum(color, h, part):
         r, w = pl.ds(h * half, half), sums(part)
-        return remote(acc.at[color, 2, r, w], rf2.at[color, h, :, w], ssend, f2recv.at[color, part], along(color, 1 + 2 * h))
+        return remote(acc.at[color, 2, r, w], rf2.at[color, h, :, w], ssend, f2recv.at[color, part], along(color, toward(h)))
 
     def near_sum(color, h, waits, part):
         r, w = pl.ds((h if waits else 1 - h) * half, half), sums(part)
-        return remote(acc.at[color, 1 + 2 * h, r, w], rn2.at[color, h, r, w], ssend, n2recv.at[color, part], along(color, 1 + 2 * h))
-
-    both = [(color, h) for color in (0, 1) for h in (0, 1)]
+        return remote(acc.at[color, toward(h), r, w], rn2.at[color, h, r, w], ssend, n2recv.at[color, part], along(color, toward(h)))
+
+    both = [(color, h) for color in BOTH for h in BOTH]
 
     own_tok = pltpu.make_async_copy(hid, tok.at[0], lsem.at[0])
     own_tok.start()
@@ -191,11 +212,11 @@
         cp.start()
 
     barrier = pltpu.get_barrier_semaphore()
-    for where in [partner, {'x': right}, {'x': left}] + [{'z': lax.rem(z + dz, 4), 'y': lax.rem(y + dy, 4)} for dz, dy in peers]:
+    for where in [partner, {'x': right}, {'x': left}] + [{'z': wrap(z + dz), 'y': wrap(y + dy)} for dz, dy in peers]:
         pl.semaphore_signal(barrier, inc=1, device_id=where, device_id_type=MESH)
     pl.semaphore_wait(barrier, 3 + len(peers))
 
-    for n in (0, 1):
+    for n in BOTH:
         for m in range(3):
             hand_own(m, n).start()
 
@@ -209,8 +230,8 @@
         start_line(1, 0, own[0], (0,))
 
     own_tok.wait()
-    for k in (0, 1):
-        for way in (0, 1):
+    for k in BOTH:
+        for way in BOTH:
             first_copy(k, way).start()
             second_copy(k, 0, way).start()
     for cp in own_routes:
@@ -238,22 +259,22 @@
         received(tok.at[pl.ds(0, 1 if late else 2)], trecv.at[a, late])
 
     tokens_arrived(4, 0)
-    for k in (0, 1):
-        for way in (0, 1):
+    for k in BOTH:
+        for way in BOTH:
             first_copy(k, 2 + way).start()
             second_copy(k, 3, way).start()
             second_copy(k, 1, way).start()
     tokens_arrived(0, 0)
-    for k in (0, 1):
-        for way in (0, 1):
+    for k in BOTH:
+        for way in BOTH:
             second_copy(k, 0, 2 + way).start()
     tokens_arrived(4, 1)
-    for k in (0, 1):
-        for way in (0, 1):
+    for k in BOTH:
+        for way in BOTH:
             second_copy(k, 2, way).start()
 
     for n, ref in enumerate((all_ids, all_gates)):
-        received(ref.at[pl.ds(1, BLOCKS - 1)], mrecv.at[n])
+        received(ref.at[OTHERS], mrecv.at[n])
     order = lax.broadcasted_iota(jnp.int32, (EXPERTS, tokens), 0)
     earlier = lax.broadcasted_iota(jnp.int32, (tokens, tokens), 0) < lax.broadcasted_iota(jnp.int32, (tokens, tokens), 1)
     earlier = jnp.where(earlier, 1.0, 0.0).astype(BF16)
@@ -274,11 +295,11 @@
         slots[s] = table(s, z * 4 + y)[0]
         return carry
 
-    lax.fori_loop(0, BLOCKS, own_table, 0)
+    repeat(BLOCKS, own_table)
 
     def ring_table(n, carry):
-        color, m, s = n // 16, lax.rem(n // 4, 4), lax.rem(n, 4)
-        line = lax.rem(z + color * s, 4) * 4 + lax.rem(y + (1 - color) * s, 4)
+        color, m, s = n // 16, wrap(n // 4), wrap(n)
+        line = wrap(z + color * s) * 4 + wrap(y + (1 - color) * s)
         slot, gate = table((4 - 3 * color) * m, line)
         tabs[color, m, s, 0] = slot
         for p in range(1, 4):
@@ -289,14 +310,14 @@
 
     def turn(a):
         tokens_arrived(a, 0)
-        for k in (0, 1):
-            for way in (0, 1):
+        for k in BOTH:
+            for way in BOTH:
                 second_copy(k, a, 2 + way).start()
 
     turn(3)
     turn(1)
     turn(2)
-    lax.fori_loop(0, 32, ring_table, 0)
+    repeat(32, ring_table)
     for a in range(4):
         tokens_arrived(a, 1)
 
@@ -318,11 +339,11 @@
         x_store(s, b).start()
         return carry
 
-    lax.fori_loop(0, BLOCKS, gather, 0)
+    repeat(BLOCKS, gather)
     acc[...] = jnp.zeros(acc.shape, F32)
     x_store(0, 0).wait()
     x_store(0, 1).wait()
-    sent(tok.at[pl.ds(1, BLOCKS - 1)], tsend)
+    sent(tok.at[OTHERS], tsend)
 
     def load(i, m, go):
         dst = (bg, bu, bd)[m]
@@ -342,14 +363,14 @@
     def line_arrived(k, ms):
         for m in ms:
             received(held[m].at[0], irecv.at[k, m])
-            for way in (0, 1):
+            for way in BOTH:
                 if k == 0 or m == 0:
                     far_copy(k, m, way).start()
                 hand_on(2 + 2 * k + way, m).start()
 
     def far_arrived(k, ms):
         for m in ms:
-            received(quarter(held[m].at[6 + k], m, c, 0, 2), frecv.at[3 * k + m])
+            received(lane_of(held[m].at[6 + k], m, c), frecv.at[3 * k + m])
             hand_on(6 + k, m).start()
 
     def handed(i, ms):
@@ -377,8 +398,8 @@
     def finish(cp):
         cp.wait()
 
-    def relay_rows(i, part=None):
-        if part is None:
+    def relay_rows(i, part=WHOLE):
+        if part is WHOLE:
             received(relay.at[i], hrecv.at[i])
         else:
             received(last_relay.at[:, :, :, :, within(part)], hrecv.at[i + part])
@@ -388,32 +409,32 @@
     def row_loads(i, color):
         at = pl.ds(8 * lax.rem(i, 2) + 4 * color, 4)
         srcs = [spread(color, i, 0, 0, 4)] + [rows_in.at[i, color, s] for s in range(3)]
-        return [pltpu.make_async_copy(src, tok.at[at, pl.ds(s * ROW_CAP, ROW_CAP), pl.ds(0, cols)], csem.at[color]) for s, src in enumerate(srcs)]
-
-    def rows_arrived(i, parts=(None,)):
+        return [pltpu.make_async_copy(src, tok.at[at, pl.ds(s * ROW_CAP, ROW_CAP), every], csem.at[color]) for s, src in enumerate(srcs)]
+
+    def rows_arrived(i, parts=(WHOLE,)):
         with scope('rows_wait'):
             for part in parts:
-                if part is None:
+                if part is WHOLE:
                     received(rows_in.at[i], rrecv.at[i])
                 else:
                     received(last_in.at[:, :, :, :, within(part)], rrecv.at[i + part])
 
     def fetch_rows(i):
         rows_arrived(i)
-        for color in (0, 1):
+        for color in BOTH:
             for cp in row_loads(i, color):
                 cp.start()
 
     def await_rows(i):
         with scope('rowload_wait'):
-            for color in (0, 1):
-                ref = tok.at[pl.ds(8 * lax.rem(i, 2) + 4 * color, 4), :, pl.ds(0, cols)]
+            for color in BOTH:
+                ref = tok.at[pl.ds(8 * lax.rem(i, 2) + 4 * color, 4), :, every]
                 pltpu.make_async_copy(ref, ref, csem.at[color]).wait()
 
-    def add_rows(i, w, take, start=0, stop=8, then=None):
+    def add_rows(i, w, take, start=0, stop=8, then=WHOLE):
         def one(n, carry):
             j, color = n // 2, lax.rem(n, 2)
-            m = lax.rem(2 + 3 * j + 3 * (j * (j - 1) // 2), 4)
+            m = wrap(2 + 3 * j + 3 * (j * (j - 1) // 2))
             got = take(color, m)
             total = acc[color, m, :, w]
             for p in range(1, 4):
@@ -422,14 +443,14 @@
                     for s in range(4)], axis=0)
                 total += lax.dot_general(g, got, (((0,), (0,)), ((), ())), preferred_element_type=F32)
             acc[color, m, :, w] = total
-            if then is not None:
+            if then is not WHOLE:
                 then(j, color)
             return carry
 
         lax.fori_loop(start, stop, one, 0)
 
     def add_fetched(i, start=0, stop=8):
-        add_rows(i, pl.ds(0, cols), lambda color, m: tok[8 * lax.rem(i, 2) + 4 * color + m, :, pl.ds(0, cols)], start, stop)
+        add_rows(i, every, lambda color, m: tok[8 * lax.rem(i, 2) + 4 * color + m, :, every], start, stop)
 
     def add_last(w, start, stop, then):
         def take(color, m):
@@ -444,7 +465,7 @@
         add_fetched(i)
 
     def load_up(i):
-        handed(i, (0, 1))
+        handed(i, BOTH)
         load(i, 0, begin)
         load(i, 1, begin)
 
@@ -460,14 +481,14 @@
             return carry
 
         with scope('down'):
-            lax.fori_loop(0, 2, one, 0)
-
-    def send(i, part=None, colors=(0, 1)):
+            repeat(2, one)
+
+    def send(i, part=WHOLE, colors=BOTH):
         for color in colors:
-            for h in (0, 1):
+            for h in BOTH:
                 far_rows(i, color, h, part).start()
         for color in colors:
-            for h in (0, 1):
+            for h in BOTH:
                 near_rows(i, color, h, part).start()
 
     def release(sem):
@@ -476,7 +497,7 @@
 
     def expert(i, carry):
         late = (i == 4) | (i == 6)
-        for t in (0, 1):
+        for t in BOTH:
             x_load(i, t).start()
 
         @pl.when(jnp.logical_not(late))
@@ -502,7 +523,7 @@
             return carry
 
         with scope('up'):
-            lax.fori_loop(0, 2, up, 0)
+            repeat(2, up)
 
         @pl.when(i == 1)
         def _():
@@ -546,18 +567,18 @@
         @pl.when(i == 3)
         def _():
             with scope('line1_gu'):
-                line_arrived(1, (0, 1))
+                line_arrived(1, BOTH)
 
         @pl.when(i == 5)
         def _():
             with scope('far0_gu'):
-                far_arrived(0, (0, 1))
+                far_arrived(0, BOTH)
 
         @pl.when(i == 6)
         def _():
             pl.semaphore_wait(up_free, 3)
             for part in range(UPS):
-                for q in (0, 1):
+                for q in BOTH:
                     far_strip(q, part).start()
 
         @pl.when(late)
@@ -569,23 +590,23 @@
             load(i, 2, finish)
         down([pl.ds(0, d)])
         with scope('store'):
-            for t in (0, 1):
+            for t in BOTH:
                 o_store(i, t).start()
-            for t in (0, 1):
+            for t in BOTH:
                 o_store(i, t).wait()
         send(i)
         return carry
 
     load_up(0)
-    lax.fori_loop(0, EXPERTS - 1, expert, 0)
+    repeat(EXPERTS - 1, expert)
 
     last = EXPERTS - 1
-    for t in (0, 1):
+    for t in BOTH:
         x_load(last, t).start()
     release(down_free)
     pl.semaphore_wait(down_free, 3)
     for part in range(PARTS):
-        for q in (0, 1):
+        for q in BOTH:
             far_piece(q, part).start()
     def strip_arrived(part):
         far_strip(0, part).wait_recv()
@@ -615,7 +636,7 @@
     with scope('last_g'):
         g_load.wait()
     with scope('gate_half'):
-        lax.fori_loop(0, 2, gate_half, 0)
+        repeat(2, gate_half)
     strip_arrived(1)
     with scope('relay'):
         relay_rows(last - 1)
@@ -625,19 +646,41 @@
             received(bd.at[:, piece(c, part)], grecv.at[part])
             hand_piece(part).start()
 
-    for part in range(UPS):
-        with scope('last_u'):
-            hand_strip(part).wait_recv()
-
-        def up_half(t, carry):
+    def up_half(part):
+        def one(t, carry):
             u = jnp.dot(xt[t].reshape(rows, d), bu[:, strip(part)], preferred_element_type=F32)
             hbuf[t, :, strip(part)] = (abuf[t, :, strip(part)] * u).astype(BF16)
             return carry
 
-        if 1 <= part < UPS - 1:
-            strip_arrived(part + 1)
+        with scope('last_u'):
+            hand_strip(part).wait_recv()
         with scope('up_half'):
-            lax.fori_loop(0, 2, up_half, 0)
+            repeat(PAIR, one)
+
+    for part in range(UPS - 1):
+        up_half(part)
+    end = UPS - 1
+    strip_arrived(end)
+
+    def by_lane(t, lane):
+        at = pl.ds(pl.multiple_of(lane * (d // PAIR), 128), d // PAIR)
+        return jnp.dot(xt[t, :, :, at].reshape(rows, d // PAIR), bu[at, strip(end)], preferred_element_type=F32)
+
+    def own_lane(t, carry):
+        ubuf[t] = by_lane(t, c)
+        return carry
+
+    def other_lane(t, carry):
+        u = ubuf[t] + by_lane(t, 1 - c)
+        hbuf[t, :, strip(end)] = (abuf[t, :, strip(end)] * u).astype(BF16)
+        return carry
+
+    with scope('own_lane'):
+        repeat(PAIR, own_lane)
+    with scope('last_u'):
+        hand_strip(end).wait_recv()
+    with scope('other_lane'):
+        repeat(PAIR, other_lane)
     piece_arrived(0)
 
     first, second = sums(0), sums(1)
@@ -654,23 +697,23 @@
             far_sum(color, 0, part).start()
             far_sum(color, 1, part).start()
 
-        for h in (0, 1):
+        for h in BOTH:
             @pl.when(j == 1 + h)
             def _():
                 near_sum(color, h, 0, part).start()
 
     def result(part, color):
         down([piece(color, part)])
-        for k in (0, 1):
+        for k in BOTH:
             @pl.when(color == k)
             def _():
                 send(last, part, (k,))
 
     result(0, c)
-    piece_arrived(1)
     with scope('last_d'):
         hand_piece(0).wait_recv()
     result(0, 1 - c)
+    piece_arrived(1)
     result(1, c)
     with scope('last_d'):
         hand_piece(1).wait_recv()
@@ -706,16 +749,16 @@
         add_last(second, 0, 8, then_second)
     for part in range(SUMS):
         w = sums(part)
-        for color in (0, 1):
+        for color in BOTH:
             with scope('farsum_wait'):
                 received(rf2.at[color, :, :, w], f2recv.at[color, part])
-            for h in (0, 1):
+            for h in BOTH:
                 r = pl.ds(h * half, half)
-                acc[color, 1 + 2 * h, r, w] = acc[color, 1 + 2 * h, r, w] + rf2[color, h, :, w]
+                acc[color, toward(h), r, w] = acc[color, toward(h), r, w] + rf2[color, h, :, w]
                 near_sum(color, h, 1, part).start()
     for part in range(SUMS):
         w = sums(part)
-        for color in (0, 1):
+        for color in BOTH:
             with scope('nearsum_wait'):
                 received(rn2.at[color, :, :, w], n2recv.at[color, part])
             here = pl.ds(color * cols + w.start, w.size)
@@ -724,7 +767,7 @@
     sent(acc.at[:, pl.ds(1, 3)], ssend)
     sent(o_hbm, rsend)
     for n, ref in enumerate((all_ids, all_gates)):
-        sent(ref.at[pl.ds(1, BLOCKS - 1)], msend.at[n])
+        sent(ref.at[OTHERS], msend.at[n])
     for m in range(3):
         sent(held[m].at[pl.ds(0, EXPERTS - 1)], wsend.at[m])
 
@@ -743,34 +786,35 @@
         out_specs=[pl.BlockSpec(memory_space=pltpu.VMEM)] + [hbm] * 7,
         out_shape=[
             pltpu.VMEM((tokens, d), BF16),
-            jax.ShapeDtypeStruct((EXPERTS, 4, 4, ROW_CAP, d), BF16),
+            jax.ShapeDtypeStruct((EXPERTS, RING, RING, ROW_CAP, d), BF16),
             jax.ShapeDtypeStruct((EXPERTS, BLOCKS, ROW_CAP, d), BF16),
-            jax.ShapeDtypeStruct((EXPERTS, 2, 3, 4, ROW_CAP, cols), BF16),
-            jax.ShapeDtypeStruct((EXPERTS, 2, 2, 2, ROW_CAP, cols), BF16),
-            jax.ShapeDtypeStruct((8, d, f), BF16),
-            jax.ShapeDtypeStruct((8, d, f), BF16),
-            jax.ShapeDtypeStruct((8, f, d), BF16),
+            jax.ShapeDtypeStruct((EXPERTS, PAIR, 3, RING, ROW_CAP, cols), BF16),
+            jax.ShapeDtypeStruct((EXPERTS, PAIR, PAIR, PAIR, ROW_CAP, cols), BF16),
+            jax.ShapeDtypeStruct((EXPERTS, d, f), BF16),
+            jax.ShapeDtypeStruct((EXPERTS, d, f), BF16),
+            jax.ShapeDtypeStruct((EXPERTS, f, d), BF16),
         ],
         scratch_shapes=[
             pltpu.VMEM((BLOCKS, tokens, d), BF16),
             pltpu.VMEM((BLOCKS,) + ids.shape, jnp.int32),
             pltpu.VMEM((BLOCKS,) + gates.shape, F32),
             pltpu.VMEM((BLOCKS, EXPERTS, tokens), F32),
-            pltpu.VMEM((2, 4, 4, 4, EXPERTS, tokens), F32),
-            pltpu.VMEM((2, 4, tokens, cols), F32),
-            pltpu.VMEM((2, 2, half, cols), F32),
-            pltpu.VMEM((2, 2, tokens, cols), F32),
-            pltpu.VMEM((2, 2, 2, ROW_CAP, cols), BF16),
-            pltpu.VMEM((2, 3, 4, ROW_CAP, cols), BF16),
-            pltpu.VMEM((4, 4, ROW_CAP, d), BF16),
-            pltpu.VMEM((2, TILE, ROW_CAP, d), BF16),
-            pltpu.VMEM((2, TILE * ROW_CAP, f), F32),
-            pltpu.VMEM((2, TILE * ROW_CAP, f), BF16),
+            pltpu.VMEM((PAIR, RING, RING, 4, EXPERTS, tokens), F32),
+            pltpu.VMEM((PAIR, RING, tokens, cols), F32),
+            pltpu.VMEM((PAIR, PAIR, half, cols), F32),
+            pltpu.VMEM((PAIR, PAIR, tokens, cols), F32),
+            pltpu.VMEM((PAIR, PAIR, PAIR, ROW_CAP, cols), BF16),
+            pltpu.VMEM((PAIR, 3, RING, ROW_CAP, cols), BF16),
+            pltpu.VMEM((RING, RING, ROW_CAP, d), BF16),
+            pltpu.VMEM((PAIR, TILE, ROW_CAP, d), BF16),
+            pltpu.VMEM((PAIR, TILE * ROW_CAP, f), F32),
+            pltpu.VMEM((PAIR, TILE * ROW_CAP, f // UPS), F32),
+            pltpu.VMEM((PAIR, TILE * ROW_CAP, f), BF16),
             pltpu.VMEM((d, f), BF16),
             pltpu.VMEM((d, f), BF16),
             pltpu.VMEM((f, d), BF16),
-            dma(()), dma((5, 2)), dma((2,)), dma((2,)), dma((3,)), dma((2, 3)), dma((4,)), dma((3, 2)), dma((11,)), dma((PARTS,)), dma((PARTS,)), dma((UPS,)), dma((UPS,)),
-            dma(()), dma((EXPERTS - 1 + PARTS,)), dma((EXPERTS - 1 + PARTS,)), dma(()), dma((2, SUMS)), dma((2, SUMS)), dma((3,)), dma((2,)), dma((3,)), dma((2,)), dma((2,)), pltpu.SemaphoreType.REGULAR, pltpu.SemaphoreType.REGULAR,
+            dma(()), dma((5, 2)), dma((PAIR,)), dma((PAIR,)), dma((3,)), dma((2, 3)), dma((4,)), dma((3, 2)), dma((11,)), dma((PARTS,)), dma((PARTS,)), dma((UPS,)), dma((UPS,)),
+            dma(()), dma((EXPERTS - 1 + PARTS,)), dma((EXPERTS - 1 + PARTS,)), dma(()), dma((PAIR, SUMS)), dma((PAIR, SUMS)), dma((3,)), dma((PAIR,)), dma((3,)), dma((PAIR,)), dma((PAIR,)), pltpu.SemaphoreType.REGULAR, pltpu.SemaphoreType.REGULAR,
         ],
         compiler_params=pltpu.CompilerParams(collective_id=0, has_side_effects=True, vmem_limit_bytes=62 * MIB),
         cost_estimate=pl.CostEstimate(flops=flops, bytes_accessed=400 * MIB, transcendentals=0),

time: 363 us -> 363 us (level)
  no operation moved by 1% of the time
where the time goes in v11:
time: 363 us
  Pallas kernels  362 us (100%)
    pallas_call x1, Pallas kernels, run_moe(): pl.pallas_call(moe_kernel, in_specs=[hbm] * 6, out_specs=[pl.BlockSpec(me...  362 us

profile of v11, /device:TPU:1, one launch (start us, length us, event | category | flops | bytes accessed | tf_op | source)
XLA Modules:
  0.0 363.0 jit_solution(7152290779733426982)
XLA Ops:
  0.0 362.0 %run_moe.1 = (bf16[256,2048]{1,0:T(8,128)(2,1)S(1)}, bf16[8,4,4,64,2048]{4,3,2,1,0:T(8,128)(2,1)}, bf16[8,16,64,2048]{3,2,1,0:T(8,128)(2,1)}, bf16[8,2,3,4,64,10...) custom-call(bf16[256,2048]{1,0:T(8,128)(2,1)} %hid.1, ...), custom_call_target="tpu_custom_call" | custom-call | flops 111669149696 | bytes 419430400 | tf_op jit(solution)/shard_map/run_moe/pallas_call | solution.py:783
  362.0 1.0 copy.8

commit v12 on v11

--- a/solution.py
+++ b/solution.py
@@ -52,7 +52,7 @@
 def moe_kernel(hid, ids, gates, wg, wu, wd, out, o_hbm, x_hbm, rows_in, relay, hg, hu, hd,
                tok, all_ids, all_gates, slots, tabs, acc, rf2, rn2, last_relay, last_in, stage, xt, abuf, ubuf, hbuf, bg, bu, bd,
                tsend, trecv, msend, mrecv, wsend, irecv, frecv, drecv, precv, grecv, qrecv, urecv, vrecv,
-               rsend, rrecv, hrecv, ssend, f2recv, n2recv, lsem, ssem, wsem, xsem, csem, up_free, down_free):
+               rsend, rrecv, hrecv, ssend, f2recv, n2recv, ssem, wsem, xsem, csem, up_free, down_free):
     z, y, x, c = (lax.axis_index(a) for a in GRID)
     right, left = wrap(x + 1), wrap(x + 3)
     tokens, d = hid.shape
@@ -90,7 +90,7 @@
         for j in which[:len(cuts) - 1]:
             a, b = cuts[j:j + 2]
             at = pl.ds(pl.multiple_of(c * n + a, 64), b - a)
-            copies.append(remote(src.at[at, :], dst.at[at, :], wsend.at[m], irecv.at[k, m], where))
+            copies.append(remote(src.at[at, :], dst.at[at, :], wsend.at[m], irecv.at[k * (1 + m // 2)], where))
         return copies
 
     def far_copy(k, m, q):
@@ -151,7 +151,7 @@
         return remote(part(k, 7 - 2 * way, 0, way - 2), part(k, 2, 0, way - 2), *sems)
 
     def second_copy(k, a, way):
-        sems = tsend, trecv.at[a, way // 2], along(1 - k, toward(way % 2))
+        sems = tsend, trecv.at[0 if way >= PAIR else a, way // 2], along(1 - k, toward(way % 2))
         if way < 2:
             return remote(part(k, a, 0), part(k, a, 3 - 2 * way), *sems)
         return remote(part(k, a, 7 - 2 * way, way - 2), part(k, a, 2, way - 2), *sems)
@@ -205,9 +205,9 @@
 
     both = [(color, h) for color in BOTH for h in BOTH]
 
-    own_tok = pltpu.make_async_copy(hid, tok.at[0], lsem.at[0])
+    own_tok = pltpu.make_async_copy(hid, tok.at[0], wsem.at[0])
     own_tok.start()
-    own_routes = [pltpu.make_async_copy(ids, all_ids.at[0], lsem.at[1]), pltpu.make_async_copy(gates, all_gates.at[0], lsem.at[2])]
+    own_routes = [pltpu.make_async_copy(ids, all_ids.at[0], wsem.at[1]), pltpu.make_async_copy(gates, all_gates.at[0], wsem.at[2])]
     for cp in own_routes:
         cp.start()
 
@@ -318,8 +318,7 @@
     turn(1)
     turn(2)
     repeat(32, ring_table)
-    for a in range(4):
-        tokens_arrived(a, 1)
+    received(tok.at[pl.ds(0, RING)], trecv.at[0, 1])
 
     def x_store(s, b):
         return pltpu.make_async_copy(stage.at[pl.ds(2 * b, 2)].reshape(EXPERTS, ROW_CAP, d), x_hbm.at[:, s], ssem.at[b])
@@ -361,8 +360,8 @@
             go(pltpu.make_async_copy(held[m].at[i], dst, wsem.at[m]))
 
     def line_arrived(k, ms):
+        received(hg.at[pl.ds(0, len(ms))], irecv.at[k * (1 + ms[0] // 2)])
         for m in ms:
-            received(held[m].at[0], irecv.at[k, m])
             for way in BOTH:
                 if k == 0 or m == 0:
                     far_copy(k, m, way).start()
@@ -813,8 +812,8 @@
             pltpu.VMEM((d, f), BF16),
             pltpu.VMEM((d, f), BF16),
             pltpu.VMEM((f, d), BF16),
-            dma(()), dma((5, 2)), dma((PAIR,)), dma((PAIR,)), dma((3,)), dma((2, 3)), dma((4,)), dma((3, 2)), dma((11,)), dma((PARTS,)), dma((PARTS,)), dma((UPS,)), dma((UPS,)),
-            dma(()), dma((EXPERTS - 1 + PARTS,)), dma((EXPERTS - 1 + PARTS,)), dma(()), dma((PAIR, SUMS)), dma((PAIR, SUMS)), dma((3,)), dma((PAIR,)), dma((3,)), dma((PAIR,)), dma((PAIR,)), pltpu.SemaphoreType.REGULAR, pltpu.SemaphoreType.REGULAR,
+            dma(()), dma((5, 2)), dma((PAIR,)), dma((PAIR,)), dma((3,)), dma((3,)), dma((4,)), dma((3, 2)), dma((11,)), dma((PARTS,)), dma((PARTS,)), dma((UPS,)), dma((UPS,)),
+            dma(()), dma((EXPERTS - 1 + PARTS,)), dma((EXPERTS - 1 + PARTS,)), dma(()), dma((PAIR, SUMS)), dma((PAIR, SUMS)), dma((PAIR,)), dma((3,)), dma((PAIR,)), dma((PAIR,)), pltpu.SemaphoreType.REGULAR, pltpu.SemaphoreType.REGULAR,
         ],
         compiler_params=pltpu.CompilerParams(collective_id=0, has_side_effects=True, vmem_limit_bytes=62 * MIB),
         cost_estimate=pl.CostEstimate(flops=flops, bytes_accessed=400 * MIB, transcendentals=0),

time: 363 us -> 363 us (level)
  no operation moved by 1% of the time
where the time goes in v12:
time: 363 us
  Pallas kernels  362 us (100%)
    pallas_call x1, Pallas kernels, run_moe(): pl.pallas_call(moe_kernel, in_specs=[hbm] * 6, out_specs=[pl.BlockSpec(me...  362 us

profile of v12, /device:TPU:1, one launch (start us, length us, event | category | flops | bytes accessed | tf_op | source)
XLA Modules:
  0.0 362.9 jit_solution(15793167171965530557)
XLA Ops:
  0.0 361.9 %run_moe.1 = (bf16[256,2048]{1,0:T(8,128)(2,1)S(1)}, bf16[8,4,4,64,2048]{4,3,2,1,0:T(8,128)(2,1)}, bf16[8,16,64,2048]{3,2,1,0:T(8,128)(2,1)}, bf16[8,2,3,4,64,10...) custom-call(bf16[256,2048]{1,0:T(8,128)(2,1)} %hid.1, ...), custom_call_target="tpu_custom_call" | custom-call | flops 111669149696 | bytes 419430400 | tf_op jit(solution)/shard_map/run_moe/pallas_call | solution.py:782
  361.9 1.0 copy.8

commit v13 on v12

--- a/solution.py
+++ b/solution.py
@@ -183,17 +183,25 @@
     def sums(part):
         return pl.ds(part * (cols // SUMS), cols // SUMS)
 
-    def row_sems(send, recv, i, part, color, h):
-        return send, recv.at[i if part is WHOLE else i + part], along(1 - color, toward(h))
+    def row_sems(recv, n, color, h):
+        return rsend, recv.at[n], along(1 - color, toward(h))
+
+    def side(i, part):
+        return i if part is WHOLE else i + (part >= FIRST)
 
     def near_rows(i, color, h, part=WHOLE):
-        return remote(spread(color, i, toward(h), 0, 4, part), landing(i, color, 3 - 2 * h, 0, 4, part), *row_sems(rsend, rrecv, i, part, color, h))
+        return remote(spread(color, i, toward(h), 0, 4, part), landing(i, color, 3 - 2 * h, 0, 4, part), *row_sems(rrecv, side(i, part), color, h))
 
     def far_rows(i, color, h, part=WHOLE):
-        return remote(spread(color, i, 2, 2 * h, 2, part), halfway(i, color, h, part), *row_sems(rsend, hrecv, i, part, color, h))
-
-    def pass_rows(i, color, h, part=WHOLE):
-        return remote(halfway(i, color, h, part), landing(i, color, 2, 2 * h, 2, part), *row_sems(rsend, rrecv, i, part, color, h))
+        return remote(spread(color, i, 2, 2 * h, 2, part), halfway(i, color, h, part), *row_sems(hrecv, i if part is WHOLE else i + part, color, h))
+
+    def pass_rows(i, color, h):
+        return remote(halfway(i, color, h, WHOLE), landing(i, color, 2, 2 * h, 2, WHOLE), *row_sems(rrecv, i, color, h))
+
+    def pass_last(color, h, start, stop):
+        w = pl.ds(EDGES[start], EDGES[stop] - EDGES[start])
+        dst = last_in.at[color, 1, pl.ds(2 * h, 2), :, w]
+        return remote(last_relay.at[color, h, :, :, w], dst, *row_sems(rrecv, side(EXPERTS - 1, start), color, h))
 
     def far_sum(color, h, part):
         r, w = pl.ds(h * half, half), sums(part)
@@ -397,29 +405,29 @@
     def finish(cp):
         cp.wait()
 
-    def relay_rows(i, part=WHOLE):
-        if part is WHOLE:
-            received(relay.at[i], hrecv.at[i])
-        else:
-            received(last_relay.at[:, :, :, :, within(part)], hrecv.at[i + part])
+    def relay_rows(i):
+        received(relay.at[i], hrecv.at[i])
         for color, h in both:
-            pass_rows(i, color, h, part).start()
+            pass_rows(i, color, h).start()
+
+    def relay_last(start, stop):
+        with scope('relay'):
+            for part in range(start, stop):
+                received(last_relay.at[:, :, :, :, within(part)], hrecv.at[EXPERTS - 1 + part])
+            for color, h in both:
+                pass_last(color, h, start, stop).start()
 
     def row_loads(i, color):
         at = pl.ds(8 * lax.rem(i, 2) + 4 * color, 4)
         srcs = [spread(color, i, 0, 0, 4)] + [rows_in.at[i, color, s] for s in range(3)]
         return [pltpu.make_async_copy(src, tok.at[at, pl.ds(s * ROW_CAP, ROW_CAP), every], csem.at[color]) for s, src in enumerate(srcs)]
 
-    def rows_arrived(i, parts=(WHOLE,)):
+    def last_arrived(part):
         with scope('rows_wait'):
-            for part in parts:
-                if part is WHOLE:
-                    received(rows_in.at[i], rrecv.at[i])
-                else:
-                    received(last_in.at[:, :, :, :, within(part)], rrecv.at[i + part])
+            received(last_in.at[:, :, :, :, sums(part)], rrecv.at[EXPERTS - 1 + part])
 
     def fetch_rows(i):
-        rows_arrived(i)
+        received(rows_in.at[i], rrecv.at[i])
         for color in BOTH:
             for cp in row_loads(i, color):
                 cp.start()
@@ -717,33 +725,29 @@
     with scope('last_d'):
         hand_piece(1).wait_recv()
     result(1, 1 - c)
-    with scope('relay'):
-        relay_rows(last, 0)
+    relay_last(0, 1)
     for part in range(2, PARTS):
         piece_arrived(part)
         result(part, c)
         if part == 2:
-            with scope('relay'):
-                relay_rows(last, 1)
+            relay_last(1, 2)
             fetch_rows(last - 1)
         with scope('last_d'):
             hand_piece(part).wait_recv()
         result(part, 1 - c)
         if part > 2:
-            with scope('relay'):
-                relay_rows(last, part - 1)
+            relay_last(part - 1, part)
         with scope('between'):
             if part == 2:
                 await_rows(last - 1)
             add_fetched(last - 1, 2 * part - 4, 2 * part - 2 if part < PARTS - 1 else 8)
-    rows_arrived(last, range(FIRST))
+    last_arrived(0)
     with scope('first_sums'):
         add_last(first, 0, 2, then_first)
-    with scope('relay'):
-        relay_rows(last, PARTS - 1)
+    relay_last(PARTS - 1, PARTS)
     with scope('first_sums'):
         add_last(first, 2, 8, then_first)
-    rows_arrived(last, range(FIRST, PARTS))
+    last_arrived(1)
     with scope('second_sums'):
         add_last(second, 0, 8, then_second)
     for part in range(SUMS):
@@ -813,7 +817,7 @@
             pltpu.VMEM((d, f), BF16),
             pltpu.VMEM((f, d), BF16),
             dma(()), dma((5, 2)), dma((PAIR,)), dma((PAIR,)), dma((3,)), dma((3,)), dma((4,)), dma((3, 2)), dma((11,)), dma((PARTS,)), dma((PARTS,)), dma((UPS,)), dma((UPS,)),
-            dma(()), dma((EXPERTS - 1 + PARTS,)), dma((EXPERTS - 1 + PARTS,)), dma(()), dma((PAIR, SUMS)), dma((PAIR, SUMS)), dma((PAIR,)), dma((3,)), dma((PAIR,)), dma((PAIR,)), pltpu.SemaphoreType.REGULAR, pltpu.SemaphoreType.REGULAR,
+            dma(()), dma((EXPERTS + 1,)), dma((EXPERTS - 1 + PARTS,)), dma(()), dma((PAIR, SUMS)), dma((PAIR, SUMS)), dma((PAIR,)), dma((3,)), dma((PAIR,)), dma((PAIR,)), pltpu.SemaphoreType.REGULAR, pltpu.SemaphoreType.REGULAR,
         ],
         compiler_params=pltpu.CompilerParams(collective_id=0, has_side_effects=True, vmem_limit_bytes=62 * MIB),
         cost_estimate=pl.CostEstimate(flops=flops, bytes_accessed=400 * MIB, transcendentals=0),

time: 363 us -> 363 us (level)
  no operation moved by 1% of the time
where the time goes in v13:
time: 363 us
  Pallas kernels  362 us (100%)
    pallas_call x1, Pallas kernels, run_moe(): pl.pallas_call(moe_kernel, in_specs=[hbm] * 6, out_specs=[pl.BlockSpec(me...  362 us

profile of v13, /device:TPU:1, one launch (start us, length us, event | category | flops | bytes accessed | tf_op | source)
XLA Modules:
  0.0 362.9 jit_solution(17697621539294706741)
XLA Ops:
  0.0 361.9 %run_moe.1 = (bf16[256,2048]{1,0:T(8,128)(2,1)S(1)}, bf16[8,4,4,64,2048]{4,3,2,1,0:T(8,128)(2,1)}, bf16[8,16,64,2048]{3,2,1,0:T(8,128)(2,1)}, bf16[8,2,3,4,64,10...) custom-call(bf16[256,2048]{1,0:T(8,128)(2,1)} %hid.1, ...), custom_call_target="tpu_custom_call" | custom-call | flops 111669149696 | bytes 419430400 | tf_op jit(solution)/shard_map/run_moe/pallas_call | solution.py:786
  361.9 1.0 copy.8
